TPU v7x, 256 devices: a whole 4x4x8 slice. The times are simulated.
256 devices in a mesh: gx: 8 (over z), gy: 8 (over y, core), gz: 4 (over x).
Axes of the slice: x: 4, y: 4, z: 8, core: 2. Of those that a mesh axis runs over, the one named last changes fastest.
Arguments:
- density: float32 [64, 64, 512], P('gx', 'gy', 'gz'), may hold values from 0.5 to 2
- base_velocity: float32 [3, 64, 64, 512], P(None, 'gx', 'gy', 'gz'), may hold values from -0.4 to 0.4
- cells: int32 [3, 65536], P(None, ('gx', 'gy', 'gz')), may hold values from 0 to 511, as said below
- offsets: float32 [3, 65536], P(None, ('gx', 'gy', 'gz')), may hold values from 0 to 1
- target: float32 [3, 65536], P(None, ('gx', 'gy', 'gz')), may hold values from -0.4 to 0.4
- stiffness: float32 [65536], P(('gx', 'gy', 'gz')), may hold values from 0.01 to 0.1
- counts: int32 [256], P(('gx', 'gy', 'gz')), may hold values from 1 to 256, as said below
Outputs:
- forces: float32 [3, 65536], P(None, ('gx', 'gy', 'gz'))
Inputs may be any that keep to these rules, and one draw needn't show every extreme that they name: `cells`: each marker's cell lies inside the lattice block of the device that holds its slot. `counts`: some device holds exactly 256 live markers in every draw.
All inputs are finite; a program needn't handle non-finite values.
Results may differ from a plain program's by a relative error of at most 0.0001.
Values sent between devices are 32-bit elements; how exact they have to be, the bound alone decides.
No kernel may reach another device: no remote copies, remote signals or barrier semaphores. Data moves between devices by JAX's collectives and lax.ppermute only.
A program may use at most 64 MiB of HBM per device.

v0:
```python
import jax
import jax.numpy as jnp
from jax import lax
from jax.sharding import Mesh
from jax.sharding import PartitionSpec as P

ITERS = 3
GY = ("gy_0", "gy_1")
GX_GY_GZ = ("gx", "gy_0", "gy_1", "gz")


def shifted(shard, axis, by):
    length = lax.axis_size(axis)
    return lax.ppermute(shard, axis, [(i, (i + by) % length) for i in range(length)])


def extended(cells, sides, width):
    for axis, dim in sides:
        count = lax.axis_size(axis)
        head = lax.slice_in_dim(cells, 0, width, axis=dim)
        tail = lax.slice_in_dim(cells, cells.shape[dim] - width, cells.shape[dim], axis=dim)
        cells = jnp.concatenate(
            [
                lax.ppermute(tail, axis, [(i, (i + 1) % count) for i in range(count)]),
                cells,
                lax.ppermute(head, axis, [((i + 1) % count, i) for i in range(count)]),
            ],
            axis=dim,
        )
    return cells


def one_axis_at_a_time(shard, axes):
    for axis in axes:
        shard = lax.psum(shard, axis)
    return shard


def moving_directions():
    listing = []
    for along_x in (-1, 0, 1):
        for along_y in (-1, 0, 1):
            for along_z in (-1, 0, 1):
                order = abs(along_x) + abs(along_y) + abs(along_z)
                if order == 1:
                    listing.append((along_x, along_y, along_z, 1.0 / 18.0))
                elif order == 2:
                    listing.append((along_x, along_y, along_z, 1.0 / 36.0))
    return listing


def delta_weights(fraction):

    def inner(radius):
        return (3.0 - 2.0 * radius + jnp.sqrt(1.0 + 4.0 * radius - 4.0 * radius * radius)) / 8.0

    def outer(radius):
        return (5.0 - 2.0 * radius - jnp.sqrt(-7.0 + 12.0 * radius - 4.0 * radius * radius)) / 8.0

    return jnp.stack(
        [outer(1.0 + fraction), inner(fraction), inner(1.0 - fraction), outer(2.0 - fraction)]
    )


def axis_rows(local, fraction, offset, extent):
    places = local[None, :] + jnp.arange(4, dtype=jnp.int32)[:, None] + offset
    hits = (places[:, :, None] == jnp.arange(extent, dtype=jnp.int32)[None, None, :]).astype(
        jnp.float32
    )
    return jnp.sum(delta_weights(fraction)[:, :, None] * hits, axis=0)


def make_tables(local, fractions, offset, extents):
    table_x = axis_rows(local[0], fractions[0], offset, extents[0]).T
    table_y = axis_rows(local[1], fractions[1], offset, extents[1]).T
    table_z = axis_rows(local[2], fractions[2], offset, extents[2])
    return (table_x, table_y, table_z)


def spread_dense(vector, tables):
    table_x, table_y, table_z = tables
    weighted = vector[:, None, None, :] * table_x[None, :, None, :] * table_y[None, None, :, :]
    return jnp.einsum("cxym,mz->cxyz", weighted, table_z, precision=lax.Precision.HIGHEST)


def interpolate_dense(field, tables):
    table_x, table_y, table_z = tables
    partial_rows = jnp.einsum("cxyz,mz->cxym", field, table_z, precision=lax.Precision.HIGHEST)
    return jnp.sum(partial_rows * (table_x[:, None, :] * table_y[None, :, :])[None], axis=(1, 2))


def surround(payload):
    stack = payload[None]
    tags = [(0, 0, 0)]
    pieces = [stack]
    grown = list(tags)
    for by in (-1, 1):
        pieces.append(shifted(stack, "gx", by))
        grown = grown + [(by, tag[1], tag[2]) for tag in tags]
    stack = jnp.concatenate(pieces, axis=0)
    tags = grown
    pieces = [stack]
    for by in (-1, 1):
        pieces.append(shifted(stack, GY, by))
        grown = grown + [(tag[0], by, tag[2]) for tag in tags]
    stack = jnp.concatenate(pieces, axis=0)
    tags = grown
    pieces = [stack]
    for by in (-1, 1):
        pieces.append(shifted(stack, "gz", by))
        grown = grown + [(tag[0], tag[1], by) for tag in tags]
    stack = jnp.concatenate(pieces, axis=0)
    return (stack, jnp.array(grown, dtype=jnp.int32))


def body(density, base_velocity, cells, offsets, target, stiffness, counts):
    size_x, size_y, size_z = density.shape
    capacity = cells.shape[1]
    anchor = jnp.stack(
        [lax.axis_index("gx") * size_x, lax.axis_index(GY) * size_y, lax.axis_index("gz") * size_z]
    )
    own_tables = make_tables(
        cells - anchor[:, None], offsets, 1, (size_x + 4, size_y + 4, size_z + 4)
    )
    live = (jnp.arange(capacity, dtype=jnp.int32) < counts[0]).astype(jnp.float32)
    scale = lax.rsqrt(density)
    stacked = jnp.concatenate([base_velocity, scale[None]], axis=0)
    fields = extended(stacked, (("gx", 1), (GY, 2), ("gz", 3)), 3)
    base_wide = fields[:3, 1 : size_x + 5, 1 : size_y + 5, 1 : size_z + 5]
    scale_wide = fields[3, 1 : size_x + 5, 1 : size_y + 5, 1 : size_z + 5]
    scale_full = fields[3]
    directions = moving_directions()
    block_sizes = jnp.array([size_x, size_y, size_z], dtype=jnp.int32)
    coordinates = (cells - anchor[:, None]).astype(jnp.float32)
    tables_all, tags = surround(jnp.concatenate([coordinates, offsets], axis=0))
    neighbour_local = (
        tables_all[:, :3].astype(jnp.int32) - (tags * block_sizes[None, :])[:, :, None]
    )
    neighbour_local = jnp.transpose(neighbour_local, (1, 0, 2)).reshape(3, -1)
    neighbour_fractions = jnp.transpose(tables_all[:, 3:], (1, 0, 2)).reshape(3, -1)
    neighbour_tables = make_tables(
        neighbour_local, neighbour_fractions, 2, (size_x + 6, size_y + 6, size_z + 6)
    )

    def spread_markers(vector):
        vectors_all, unused = surround(vector)
        flat_vectors = jnp.transpose(vectors_all, (1, 0, 2)).reshape(3, -1)
        return spread_dense(flat_vectors, neighbour_tables)

    def stream_wide(wide):
        post = jnp.zeros((3, size_x + 4, size_y + 4, size_z + 4), jnp.float32)
        for along_x, along_y, along_z, share in directions:
            piece = wide[
                :,
                1 - along_x : 5 - along_x + size_x,
                1 - along_y : 5 - along_y + size_y,
                1 - along_z : 5 - along_z + size_z,
            ]
            population = (
                3.0 * share * (along_x * piece[0] + along_y * piece[1] + along_z * piece[2])
            )
            post = post + jnp.stack(
                [along_x * population, along_y * population, along_z * population]
            )
        return scale_wide * (wide[:, 1 : size_x + 5, 1 : size_y + 5, 1 : size_z + 5] + post) * 0.5

    def apply(vector):
        wide = scale_full * spread_markers(vector)
        velocity_wide = stream_wide(wide)
        return live * (interpolate_dense(velocity_wide, own_tables) + stiffness * vector)

    def both_products(vector, image):
        return (
            one_axis_at_a_time(jnp.sum(vector * vector), GX_GY_GZ),
            one_axis_at_a_time(jnp.sum(vector * image), GX_GY_GZ),
        )

    right = live * (target - interpolate_dense(base_wide, own_tables))
    solution = jnp.zeros_like(right)
    residual = right
    image = apply(residual)
    norm_now, product = both_products(residual, image)
    alpha = norm_now / product
    direction = residual
    along = image
    for step in range(ITERS):
        solution = solution + alpha * direction
        residual = residual - alpha * along
        if step + 1 < ITERS:
            image = apply(residual)
            norm_next, product = both_products(residual, image)
            ratio = norm_next / norm_now
            alpha = norm_next / (product - ratio * norm_next / alpha)
            direction = residual + ratio * direction
            along = image + ratio * along
            norm_now = norm_next
    return solution


def solution(mesh):
    finer = Mesh(
        mesh.devices.reshape(mesh.shape["gx"], 4, 2, mesh.shape["gz"]), ("gx", "gy_0", "gy_1", "gz")
    )
    return jax.shard_map(
        body,
        mesh=finer,
        in_specs=(
            P("gx", GY, "gz"),
            P(None, "gx", GY, "gz"),
            P(None, GX_GY_GZ),
            P(None, GX_GY_GZ),
            P(None, GX_GY_GZ),
            P(GX_GY_GZ),
            P(GX_GY_GZ),
        ),
        out_specs=P(None, GX_GY_GZ),
        check_vma=False,
    )
```

profile of v0, /device:TPU:1, one launch (start us, length us, event | category | flops | bytes accessed | tf_op | source)
XLA Modules:
  0.0 326.5 jit_solution(7431941897793863222)
XLA Ops:
  4.0 4.0 %collective-permute-start.12 = (f32[1,6,256]{2,1,0:T(8,128)S(1)}, f32[1,6,256]{2,1,0:T(8,128)S(1)}, u32[]{:S(2)}, u32[]{:S(2)}) collective-permute-start(f32[1,6,256]{2,1,0:T(8,128)S(1)} %maximum_bitcast_fusion), channel_id=1, source_target_pairs={{0,224},{32,0},{64,32},{96,64},{128,96},{160,128},{192,160},{224,1... | collective-permute-start | bytes 18440 | tf_op jit(solution)/shard_map/ppermute | solution.py:14
  9.7 2.7 collective-permute-start.1
  15.2 2.7 collective-permute-start.15
  17.9 3.2 collective-permute-done.14
  29.1 34.5 %select_reduce_fusion = f32[6912,134]{0,1:T(8,128)S(1)} fusion(f32[4,6912]{1,0:T(4,128)S(1)} %pad_maximum_fusion.5, s32[4,6912]{1,0:T(4,128)S(1)} %add_add_fusion), kind=kLoop, calls=%fused_computation.6 | loop fusion | flops 10188288 | bytes 3926016 | tf_op jit(solution)/shard_map/reduce_sum | solution.py:70
  69.0 7.2 %collective-permute-done.4 = f32[4,14,14,3]{3,2,1,0:T(8,128)S(1)} collective-permute-done((f32[4,14,14,3]{3,2,1,0:T(8,128)S(1)}, f32[4,14,14,3]{3,2,1,0:T(8,128)S(1)}, u32[]{:S(2)}, u32[]{:S(2)}) %collective-permute-start.4) | collective-permute-done | bytes 9440 | tf_op jit(solution)/shard_map/ppermute | solution.py:24
  78.4 2.7 collective-permute-start.6
  82.1 5.1 %collective-permute-start.9 = (f32[3,3,256]{2,1,0:T(4,128)S(1)}, f32[3,3,256]{2,1,0:T(4,128)S(1)}, u32[]{:S(2)}, u32[]{:S(2)}) collective-permute-start(f32[3,3,256]{2,1,0:T(4,128)S(1)} %pad_maximum_fusion.9), channel_id=1, source_target_pairs={{0,4},{4,8},{8,12},{12,16},{16,20},{20,24},{24,28},{28,0},{1,5},{5... | collective-permute-start | bytes 27656 | tf_op jit(solution)/shard_map/ppermute | solution.py:14
  87.2 3.1 collective-permute-done.8
  94.0 3.5 %collective-permute-done.11 = f32[9,3,256]{2,1,0:T(4,128)S(1)} collective-permute-done((f32[9,3,256]{2,1,0:T(4,128)S(1)}, f32[9,3,256]{2,1,0:T(4,128)S(1)}, u32[]{:S(2)}, u32[]{:S(2)}) %collective-permute-start.11) | collective-permute-done | bytes 27680 | tf_op jit(solution)/shard_map/ppermute | solution.py:14
  97.6 14.8 %fusion.15 = f32[3,14,14,134]{3,2,1,0:T(8,128)S(1)} fusion(f32[6912,134]{0,1:T(8,128)S(1)} %select_reduce_fusion, f32[14,6912]{1,0:T(8,128)S(1)} %bitcast.78, f32[3,14,6912]{2,1,0:T(8,128)S(1)} %broadcast_multiply_fusion.2, f32[14,14,134]{2,1,0:T(8,128)S(1)} %slice_bitcast_fusion), kind=kOutput, calls=%fused_computation.21 | convolution fusion | flops 6539466752 | bytes 5673344 | tf_op jit(solution)/shard_map/cxym,mz->cxyz/dot_general | solution.py:83
  119.0 14.3 %all-reduce.2 = (f32[]{:T(128)}, f32[]{:T(128)}) all-reduce(f32[]{:T(128)} %get-tuple-element.13, f32[]{:T(128)} %get-tuple-element.12), channel_id=1, replica_groups=mesh['gx'=8,'gy_0'=4,'gy_1'=2,'gz'=4] {'gx'}, use_global_device_ids=true, to_apply=%region_5.0 | all-reduce | flops 2 | bytes 16 | tf_op jit(solution)/shard_map/psum | solution.py:35
  133.3 9.5 %all-reduce.8 = (f32[]{:T(128)}, f32[]{:T(128)}) all-reduce(f32[]{:T(128)} %get-tuple-element.18, f32[]{:T(128)} %get-tuple-element.19), channel_id=1, replica_groups=mesh['gx'=8,'gy_0'=4,'gy_1'=2,'gz'=4] {'gy_0'}, use_global_device_ids=true, to_apply=%region_6.0 | all-reduce | flops 2 | bytes 16 | tf_op jit(solution)/shard_map/psum | solution.py:35
  142.7 8.9 %all-reduce.11 = (f32[]{:T(128)}, f32[]{:T(128)}) all-reduce(f32[]{:T(128)} %get-tuple-element.30, f32[]{:T(128)} %get-tuple-element.31), channel_id=1, replica_groups=mesh['gx'=8,'gy_0'=4,'gy_1'=2,'gz'=4] {'gy_1'}, use_global_device_ids=true, to_apply=%region_7.0 | all-reduce | flops 2 | bytes 16 | tf_op jit(solution)/shard_map/psum | solution.py:35
  151.7 6.7 %all-reduce.5 = (f32[]{:T(128)}, f32[]{:T(128)}) all-reduce(f32[]{:T(128)} %get-tuple-element.36, f32[]{:T(128)} %get-tuple-element.37), channel_id=1, replica_groups=mesh['gx'=8,'gy_0'=4,'gy_1'=2,'gz'=4] {'gz'}, use_global_device_ids=true, to_apply=%region_8.0 | all-reduce | flops 2 | bytes 16 | tf_op jit(solution)/shard_map/psum | solution.py:35
  159.8 2.7 collective-permute-start.18
  163.5 2.8 collective-permute-start.21
  166.7 2.7 collective-permute-done.20
  172.6 2.8 collective-permute-done.23
  175.6 17.1 %fusion.20 = f32[3,14,14,134]{3,2,1,0:T(8,128)S(1)} fusion(f32[6912,134]{0,1:T(8,128)} %copy-done, f32[3,14,6912]{2,1,0:T(8,128)S(1)} %broadcast_multiply_fusion.1, f32[14,6912]{1,0:T(8,128)S(1)} %bitcast.79, f32[14,14,134]{2,1,0:T(8,128)S(1)} %slice_bitcast_fusion), kind=kOutput, calls=%fused_computation.22 | convolution fusion | flops 6539466752 | bytes 5673344 | tf_op jit(solution)/shard_map/cxym,mz->cxyz/dot_general | solution.py:83
  199.1 14.3 %all-reduce.1 = (f32[]{:T(128)}, f32[]{:T(128)}) all-reduce(f32[]{:T(128)} %get-tuple-element.11, f32[]{:T(128)} %get-tuple-element.10), channel_id=1, replica_groups=mesh['gx'=8,'gy_0'=4,'gy_1'=2,'gz'=4] {'gx'}, use_global_device_ids=true, to_apply=%region_19.0 | all-reduce | flops 2 | bytes 16 | tf_op jit(solution)/shard_map/psum | solution.py:35
  213.4 10.8 %all-reduce.7 = (f32[]{:T(128)}, f32[]{:T(128)}) all-reduce(f32[]{:T(128)} %get-tuple-element.16, f32[]{:T(128)} %get-tuple-element.17), channel_id=1, replica_groups=mesh['gx'=8,'gy_0'=4,'gy_1'=2,'gz'=4] {'gy_0'}, use_global_device_ids=true, to_apply=%region_20.0 | all-reduce | flops 2 | bytes 16 | tf_op jit(solution)/shard_map/psum | solution.py:35
  224.2 7.2 %all-reduce.10 = (f32[]{:T(128)}, f32[]{:T(128)}) all-reduce(f32[]{:T(128)} %get-tuple-element.28, f32[]{:T(128)} %get-tuple-element.29), channel_id=1, replica_groups=mesh['gx'=8,'gy_0'=4,'gy_1'=2,'gz'=4] {'gy_1'}, use_global_device_ids=true, to_apply=%region_21.0 | all-reduce | flops 2 | bytes 16 | tf_op jit(solution)/shard_map/psum | solution.py:35
  231.4 6.8 %all-reduce.4 = (f32[]{:T(128)}, f32[]{:T(128)}) all-reduce(f32[]{:T(128)} %get-tuple-element.34, f32[]{:T(128)} %get-tuple-element.35), channel_id=1, replica_groups=mesh['gx'=8,'gy_0'=4,'gy_1'=2,'gz'=4] {'gz'}, use_global_device_ids=true, to_apply=%region_22.0 | all-reduce | flops 2 | bytes 16 | tf_op jit(solution)/shard_map/psum | solution.py:35
  246.5 4.8 %collective-permute-start.27 = (f32[3,3,256]{2,1,0:T(4,128)S(1)}, f32[3,3,256]{2,1,0:T(4,128)S(1)}, u32[]{:S(2)}, u32[]{:S(2)}) collective-permute-start(f32[3,3,256]{2,1,0:T(4,128)S(1)} %pad_maximum_fusion.11), channel_id=1, source_target_pairs={{0,4},{4,8},{8,12},{12,16},{16,20},{20,24},{24,28},{28,0},{1,5},{5... | collective-permute-start | bytes 27656 | tf_op jit(solution)/shard_map/ppermute | solution.py:14
  251.3 3.1 collective-permute-done.26
  258.0 2.8 collective-permute-done.29
  260.9 16.9 %fusion.25 = f32[3,14,14,134]{3,2,1,0:T(8,128)S(1)} fusion(f32[6912,134]{0,1:T(8,128)} %copy-done, f32[3,14,6912]{2,1,0:T(8,128)S(1)} %broadcast_multiply_fusion, f32[14,6912]{1,0:T(8,128)S(1)} %bitcast.80, f32[14,14,134]{2,1,0:T(8,128)S(1)} %slice_bitcast_fusion), kind=kOutput, calls=%fused_computation.23 | convolution fusion | flops 6539466752 | bytes 5673344 | tf_op jit(solution)/shard_map/cxym,mz->cxyz/dot_general | solution.py:83
  284.3 14.2 %all-reduce = (f32[]{:T(128)}, f32[]{:T(128)}) all-reduce(f32[]{:T(128)} %get-tuple-element.9, f32[]{:T(128)} %get-tuple-element.8), channel_id=1, replica_groups=mesh['gx'=8,'gy_0'=4,'gy_1'=2,'gz'=4] {'gx'}, use_global_device_ids=true, to_apply=%region_30.0 | all-reduce | flops 2 | bytes 16 | tf_op jit(solution)/shard_map/psum | solution.py:35
  298.5 8.6 %all-reduce.6 = (f32[]{:T(128)}, f32[]{:T(128)}) all-reduce(f32[]{:T(128)} %get-tuple-element.14, f32[]{:T(128)} %get-tuple-element.15), channel_id=1, replica_groups=mesh['gx'=8,'gy_0'=4,'gy_1'=2,'gz'=4] {'gy_0'}, use_global_device_ids=true, to_apply=%region_31.0 | all-reduce | flops 2 | bytes 16 | tf_op jit(solution)/shard_map/psum | solution.py:35
  307.2 7.8 %all-reduce.9 = (f32[]{:T(128)}, f32[]{:T(128)}) all-reduce(f32[]{:T(128)} %get-tuple-element.26, f32[]{:T(128)} %get-tuple-element.27), channel_id=1, replica_groups=mesh['gx'=8,'gy_0'=4,'gy_1'=2,'gz'=4] {'gy_1'}, use_global_device_ids=true, to_apply=%region_32.0 | all-reduce | flops 2 | bytes 16 | tf_op jit(solution)/shard_map/psum | solution.py:35
  314.9 6.7 %all-reduce.3 = (f32[]{:T(128)}, f32[]{:T(128)}) all-reduce(f32[]{:T(128)} %get-tuple-element.32, f32[]{:T(128)} %get-tuple-element.33), channel_id=1, replica_groups=mesh['gx'=8,'gy_0'=4,'gy_1'=2,'gz'=4] {'gz'}, use_global_device_ids=true, to_apply=%region_33.0 | all-reduce | flops 2 | bytes 16 | tf_op jit(solution)/shard_map/psum | solution.py:35
  (173 shorter events, 60.0 us)
Async XLA Ops:
  1.5 13.6 %collective-permute-start.13 = (f32[1,6,256]{2,1,0:T(8,128)S(1)}, f32[1,6,256]{2,1,0:T(8,128)S(1)}, u32[]{:S(2)}, u32[]{:S(2)}) collective-permute-start(f32[1,6,256]{2,1,0:T(8,128)S(1)} %maximum_bitcast_fusion), channel_id=1, source_target_pairs={{0,32},{32,64},{64,96},{96,128},{128,160},{160,192},{192,224},{224... | collective-permute-start | bytes 18440 | tf_op jit(solution)/shard_map/ppermute | solution.py:14
  4.0 11.2 %collective-permute-start.12 = (f32[1,6,256]{2,1,0:T(8,128)S(1)}, f32[1,6,256]{2,1,0:T(8,128)S(1)}, u32[]{:S(2)}, u32[]{:S(2)}) collective-permute-start(f32[1,6,256]{2,1,0:T(8,128)S(1)} %maximum_bitcast_fusion), channel_id=1, source_target_pairs={{0,224},{32,0},{64,32},{96,64},{128,96},{160,128},{192,160},{224,1... | collective-permute-start | bytes 18440 | tf_op jit(solution)/shard_map/ppermute | solution.py:14
  9.6 14.5 %collective-permute-start = (f32[4,3,8,128]{3,2,1,0:T(8,128)S(1)}, f32[4,3,8,128]{3,2,1,0:T(8,128)S(1)}, u32[]{:S(2)}, u32[]{:S(2)}) collective-permute-start(f32[4,3,8,128]{3,2,1,0:T(8,128)S(1)} %get-tuple-element.221), channel_id=1, source_target_pairs={{0,32},{32,64},{64,96},{96,128},{128,160},{160,192},{192,224},{224... | collective-permute-start | bytes 147464 | tf_op jit(solution)/shard_map/ppermute | solution.py:24
  9.7 14.4 %collective-permute-start.1 = (f32[4,3,8,128]{3,2,1,0:T(8,128)S(1)}, f32[4,3,8,128]{3,2,1,0:T(8,128)S(1)}, u32[]{:S(2)}, u32[]{:S(2)}) collective-permute-start(f32[4,3,8,128]{3,2,1,0:T(8,128)S(1)} %get-tuple-element.222), channel_id=1, source_target_pairs={{32,0},{64,32},{96,64},{128,96},{160,128},{192,160},{224,192},{0,2... | collective-permute-start | bytes 147464 | tf_op jit(solution)/shard_map/ppermute | solution.py:26
  15.2 6.0 %collective-permute-start.15 = (f32[3,6,256]{2,1,0:T(8,128)S(1)}, f32[3,6,256]{2,1,0:T(8,128)S(1)}, u32[]{:S(2)}, u32[]{:S(2)}) collective-permute-start(f32[3,6,256]{2,1,0:T(8,128)S(1)} %pad_maximum_fusion.8), channel_id=1, source_target_pairs={{0,4},{4,8},{8,12},{12,16},{16,20},{20,24},{24,28},{28,0},{1,5},{5... | collective-permute-start | bytes 55304 | tf_op jit(solution)/shard_map/ppermute | solution.py:14
  17.9 3.3 collective-permute-start.14
  21.2 5.1 %collective-permute-start.17 = (f32[9,6,256]{2,1,0:T(8,128)S(1)}, f32[9,6,256]{2,1,0:T(8,128)S(1)}, u32[]{:S(2)}, u32[]{:S(2)}) collective-permute-start(f32[9,6,256]{2,1,0:T(8,128)S(1)} %get-tuple-element.238), channel_id=1, source_target_pairs={{0,1},{1,2},{2,3},{3,0},{4,5},{5,6},{6,7},{7,4},{8,9},{9,10},{10,1... | collective-permute-start | bytes 165896 | tf_op jit(solution)/shard_map/ppermute | solution.py:14
  22.4 3.7 %collective-permute-start.16 = (f32[9,6,256]{2,1,0:T(8,128)S(1)}, f32[9,6,256]{2,1,0:T(8,128)S(1)}, u32[]{:S(2)}, u32[]{:S(2)}) collective-permute-start(f32[9,6,256]{2,1,0:T(8,128)S(1)} %get-tuple-element.238), channel_id=1, source_target_pairs={{0,3},{1,0},{2,1},{3,2},{4,7},{5,4},{6,5},{7,6},{8,11},{9,8},{10,9... | collective-permute-start | bytes 165896 | tf_op jit(solution)/shard_map/ppermute | solution.py:14
  25.0 39.9 %collective-permute-start.2 = (f32[4,14,3,128]{3,2,1,0:T(4,128)S(1)}, f32[4,14,3,128]{3,2,1,0:T(4,128)S(1)}, u32[]{:S(2)}, u32[]{:S(2)}) collective-permute-start(f32[4,14,3,128]{3,2,1,0:T(4,128)S(1)} %get-tuple-element.183), channel_id=1, source_target_pairs={{0,4},{4,8},{8,12},{12,16},{16,20},{20,24},{24,28},{28,0},{1,5},{5... | collective-permute-start | bytes 258056 | tf_op jit(solution)/shard_map/ppermute | solution.py:24
  25.6 39.3 %collective-permute-start.3 = (f32[4,14,3,128]{3,2,1,0:T(4,128)S(1)}, f32[4,14,3,128]{3,2,1,0:T(4,128)S(1)}, u32[]{:S(2)}, u32[]{:S(2)}) collective-permute-start(f32[4,14,3,128]{3,2,1,0:T(4,128)S(1)} %get-tuple-element.184), channel_id=1, source_target_pairs={{4,0},{8,4},{12,8},{16,12},{20,16},{24,20},{28,24},{0,28},{5,1},{9... | collective-permute-start | bytes 258056 | tf_op jit(solution)/shard_map/ppermute | solution.py:26
  26.1 38.8 %copy-start.1 = (f32[3,8,8,128]{3,2,1,0:T(8,128)S(1)}, f32[3,8,8,128]{3,2,1,0:T(8,128)}, u32[]{:S(2)}) copy-start(f32[3,8,8,128]{3,2,1,0:T(8,128)} %param.10) | copy-start | bytes 294916
  63.6 34.0 %copy-start = (f32[6912,134]{0,1:T(8,128)}, f32[6912,134]{0,1:T(8,128)S(1)}, u32[]{:S(2)}) copy-start(f32[6912,134]{0,1:T(8,128)S(1)} %select_reduce_fusion) | copy-start | bytes 11114500
  65.2 11.0 %collective-permute-start.4 = (f32[4,14,14,3]{3,2,1,0:T(8,128)S(1)}, f32[4,14,14,3]{3,2,1,0:T(8,128)S(1)}, u32[]{:S(2)}, u32[]{:S(2)}) collective-permute-start(f32[4,14,14,3]{3,2,1,0:T(8,128)S(1)} %get-tuple-element.181), channel_id=1, source_target_pairs={{0,1},{1,2},{2,3},{3,0},{4,5},{5,6},{6,7},{7,4},{8,9},{9,10},{10,1... | collective-permute-start | bytes 28232 | tf_op jit(solution)/shard_map/ppermute | solution.py:24
  66.4 10.5 %collective-permute-start.5 = (f32[4,14,14,3]{3,2,1,0:T(8,128)S(1)}, f32[4,14,14,3]{3,2,1,0:T(8,128)S(1)}, u32[]{:S(2)}, u32[]{:S(2)}) collective-permute-start(f32[4,14,14,3]{3,2,1,0:T(8,128)S(1)} %get-tuple-element.182), channel_id=1, source_target_pairs={{1,0},{2,1},{3,2},{0,3},{5,4},{6,5},{7,6},{4,7},{9,8},{10,9},{11,1... | collective-permute-start | bytes 28232 | tf_op jit(solution)/shard_map/ppermute | solution.py:26
  78.3 3.7 %collective-permute-start.7 = (f32[1,3,256]{2,1,0:T(4,128)S(1)}, f32[1,3,256]{2,1,0:T(4,128)S(1)}, u32[]{:S(2)}, u32[]{:S(2)}) collective-permute-start(f32[1,3,256]{2,1,0:T(4,128)S(1)} %bitcast.81), channel_id=1, source_target_pairs={{0,32},{32,64},{64,96},{96,128},{128,160},{160,192},{192,224},{224... | collective-permute-start | bytes 9224 | tf_op jit(solution)/shard_map/ppermute | solution.py:14
  78.4 3.7 %collective-permute-start.6 = (f32[1,3,256]{2,1,0:T(4,128)S(1)}, f32[1,3,256]{2,1,0:T(4,128)S(1)}, u32[]{:S(2)}, u32[]{:S(2)}) collective-permute-start(f32[1,3,256]{2,1,0:T(4,128)S(1)} %bitcast.82), channel_id=1, source_target_pairs={{0,224},{32,0},{64,32},{96,64},{128,96},{160,128},{192,160},{224,1... | collective-permute-start | bytes 9224 | tf_op jit(solution)/shard_map/ppermute | solution.py:14
  82.1 8.2 %collective-permute-start.9 = (f32[3,3,256]{2,1,0:T(4,128)S(1)}, f32[3,3,256]{2,1,0:T(4,128)S(1)}, u32[]{:S(2)}, u32[]{:S(2)}) collective-permute-start(f32[3,3,256]{2,1,0:T(4,128)S(1)} %pad_maximum_fusion.9), channel_id=1, source_target_pairs={{0,4},{4,8},{8,12},{12,16},{16,20},{20,24},{24,28},{28,0},{1,5},{5... | collective-permute-start | bytes 27656 | tf_op jit(solution)/shard_map/ppermute | solution.py:14
  87.2 3.1 collective-permute-start.8
  90.3 3.6 %collective-permute-start.10 = (f32[9,3,256]{2,1,0:T(4,128)S(1)}, f32[9,3,256]{2,1,0:T(4,128)S(1)}, u32[]{:S(2)}, u32[]{:S(2)}) collective-permute-start(f32[9,3,256]{2,1,0:T(4,128)S(1)} %get-tuple-element.250), channel_id=1, source_target_pairs={{0,3},{1,0},{2,1},{3,2},{4,7},{5,4},{6,5},{7,6},{8,11},{9,8},{10,9... | collective-permute-start | bytes 82952 | tf_op jit(solution)/shard_map/ppermute | solution.py:14
  93.0 4.5 %collective-permute-start.11 = (f32[9,3,256]{2,1,0:T(4,128)S(1)}, f32[9,3,256]{2,1,0:T(4,128)S(1)}, u32[]{:S(2)}, u32[]{:S(2)}) collective-permute-start(f32[9,3,256]{2,1,0:T(4,128)S(1)} %get-tuple-element.250), channel_id=1, source_target_pairs={{0,1},{1,2},{2,3},{3,0},{4,5},{5,6},{6,7},{7,4},{8,9},{9,10},{10,1... | collective-permute-start | bytes 82952 | tf_op jit(solution)/shard_map/ppermute | solution.py:14
  159.8 3.7 %collective-permute-start.19 = (f32[1,3,256]{2,1,0:T(4,128)S(1)}, f32[1,3,256]{2,1,0:T(4,128)S(1)}, u32[]{:S(2)}, u32[]{:S(2)}) collective-permute-start(f32[1,3,256]{2,1,0:T(4,128)S(1)} %bitcast.84), channel_id=1, source_target_pairs={{0,32},{32,64},{64,96},{96,128},{128,160},{160,192},{192,224},{224... | collective-permute-start | bytes 9224 | tf_op jit(solution)/shard_map/ppermute | solution.py:14
  159.8 3.7 %collective-permute-start.18 = (f32[1,3,256]{2,1,0:T(4,128)S(1)}, f32[1,3,256]{2,1,0:T(4,128)S(1)}, u32[]{:S(2)}, u32[]{:S(2)}) collective-permute-start(f32[1,3,256]{2,1,0:T(4,128)S(1)} %bitcast.85), channel_id=1, source_target_pairs={{0,224},{32,0},{64,32},{96,64},{128,96},{160,128},{192,160},{224,1... | collective-permute-start | bytes 9224 | tf_op jit(solution)/shard_map/ppermute | solution.py:14
  163.5 5.9 %collective-permute-start.21 = (f32[3,3,256]{2,1,0:T(4,128)S(1)}, f32[3,3,256]{2,1,0:T(4,128)S(1)}, u32[]{:S(2)}, u32[]{:S(2)}) collective-permute-start(f32[3,3,256]{2,1,0:T(4,128)S(1)} %pad_maximum_fusion.10), channel_id=1, source_target_pairs={{0,4},{4,8},{8,12},{12,16},{16,20},{20,24},{24,28},{28,0},{1,5},{5... | collective-permute-start | bytes 27656 | tf_op jit(solution)/shard_map/ppermute | solution.py:14
  166.3 3.1 collective-permute-start.20
  169.4 3.2 collective-permute-start.22
  171.2 4.2 %collective-permute-start.23 = (f32[9,3,256]{2,1,0:T(4,128)S(1)}, f32[9,3,256]{2,1,0:T(4,128)S(1)}, u32[]{:S(2)}, u32[]{:S(2)}) collective-permute-start(f32[9,3,256]{2,1,0:T(4,128)S(1)} %get-tuple-element.246), channel_id=1, source_target_pairs={{0,1},{1,2},{2,3},{3,0},{4,5},{5,6},{6,7},{7,4},{8,9},{9,10},{10,1... | collective-permute-start | bytes 82952 | tf_op jit(solution)/shard_map/ppermute | solution.py:14
  242.8 3.7 %collective-permute-start.25 = (f32[1,3,256]{2,1,0:T(4,128)S(1)}, f32[1,3,256]{2,1,0:T(4,128)S(1)}, u32[]{:S(2)}, u32[]{:S(2)}) collective-permute-start(f32[1,3,256]{2,1,0:T(4,128)S(1)} %bitcast.93), channel_id=1, source_target_pairs={{0,32},{32,64},{64,96},{96,128},{128,160},{160,192},{192,224},{224... | collective-permute-start | bytes 9224 | tf_op jit(solution)/shard_map/ppermute | solution.py:14
  242.9 3.7 %collective-permute-start.24 = (f32[1,3,256]{2,1,0:T(4,128)S(1)}, f32[1,3,256]{2,1,0:T(4,128)S(1)}, u32[]{:S(2)}, u32[]{:S(2)}) collective-permute-start(f32[1,3,256]{2,1,0:T(4,128)S(1)} %bitcast.94), channel_id=1, source_target_pairs={{0,224},{32,0},{64,32},{96,64},{128,96},{160,128},{192,160},{224,1... | collective-permute-start | bytes 9224 | tf_op jit(solution)/shard_map/ppermute | solution.py:14
  246.5 7.9 %collective-permute-start.27 = (f32[3,3,256]{2,1,0:T(4,128)S(1)}, f32[3,3,256]{2,1,0:T(4,128)S(1)}, u32[]{:S(2)}, u32[]{:S(2)}) collective-permute-start(f32[3,3,256]{2,1,0:T(4,128)S(1)} %pad_maximum_fusion.11), channel_id=1, source_target_pairs={{0,4},{4,8},{8,12},{12,16},{16,20},{20,24},{24,28},{28,0},{1,5},{5... | collective-permute-start | bytes 27656 | tf_op jit(solution)/shard_map/ppermute | solution.py:14
  251.3 3.1 collective-permute-start.26
  254.5 3.5 %collective-permute-start.28 = (f32[9,3,256]{2,1,0:T(4,128)S(1)}, f32[9,3,256]{2,1,0:T(4,128)S(1)}, u32[]{:S(2)}, u32[]{:S(2)}) collective-permute-start(f32[9,3,256]{2,1,0:T(4,128)S(1)} %get-tuple-element.242), channel_id=1, source_target_pairs={{0,3},{1,0},{2,1},{3,2},{4,7},{5,4},{6,5},{7,6},{8,11},{9,8},{10,9... | collective-permute-start | bytes 82952 | tf_op jit(solution)/shard_map/ppermute | solution.py:14
  256.3 4.5 %collective-permute-start.29 = (f32[9,3,256]{2,1,0:T(4,128)S(1)}, f32[9,3,256]{2,1,0:T(4,128)S(1)}, u32[]{:S(2)}, u32[]{:S(2)}) collective-permute-start(f32[9,3,256]{2,1,0:T(4,128)S(1)} %get-tuple-element.242), channel_id=1, source_target_pairs={{0,1},{1,2},{2,3},{3,0},{4,5},{5,6},{6,7},{7,4},{8,9},{9,10},{10,1... | collective-permute-start | bytes 82952 | tf_op jit(solution)/shard_map/ppermute | solution.py:14
  (2 other events, 16.2 us)
where the time goes:
time: 333 us; the launch traced here: 326 us
  blocking collectives  116 us (35%)
  other arithmetic  60.4 us (18%)
  matrix products  54.6 us (16%)
  starting transfers between devices  46.7 us (14%)
  waiting for transfers between devices  35.7 us (11%)
  between operations  11.6 us (3%)
    psum x12, blocking collectives, one_axis_at_a_time(): shard = lax.psum(shard, axis)  116 us
    dot_general x3, matrix products, spread_dense(): jnp.einsum('cxym,mz->cxyz', weighted, table_z, precision=lax.Precision.HI...  48.7 us
    ppermute x24, starting transfers between devices, shifted(): lax.ppermute(shard, axis, [(i, (i + by) % length) for i in range(length)])  40.6 us
    reduce_sum x6, other arithmetic, axis_rows(): return jnp.sum(delta_weights(fraction)[:, :, None] * hits, axis=0)  37 us
    ppermute x24, waiting for transfers between devices, shifted(): lax.ppermute(shard, axis, [(i, (i + by) % length) for i in range(length)])  27.7 us
    mul x15, other arithmetic, stream_wide(): 3.0 * share * (along_x * piece[0] + along_y * piece[1] + along_z * piece[2])  7.43 us
    ppermute x3, waiting for transfers between devices, extended(): lax.ppermute(tail, axis, [(i, (i + 1) % count) for i in range(count)])  7.18 us
  transfers between devices with their start and end apart: 30, of which 17 were waited for; matrix products, arithmetic and copies ran while one was open for 14% of the time, Pallas kernels for 0%

commit v1 on v0

v1 whole, which is shorter than its diff:
```python
import jax
import jax.numpy as jnp
from jax import lax
from jax.experimental import pallas as pl
from jax.experimental.pallas import tpu as pltpu
from jax.sharding import Mesh
from jax.sharding import PartitionSpec as P

GY = ("gy_0", "gy_1")
GX_GY_GZ = ("gx", "gy_0", "gy_1", "gz")

PLANES = 13
YPAD = 16
ROWS = PLANES * YPAD
INNER = 11 * YPAD
LANES = 256
BLOCKS = 9
MARKERS = 256
COLS = BLOCKS * MARKERS
F32 = jnp.float32
BF16 = jnp.bfloat16
PARAMS = pltpu.CompilerParams(vmem_limit_bytes=48 * 1024 * 1024)


def shifted(shard, axis, by):
    length = lax.axis_size(axis)
    return lax.ppermute(shard, axis, [(i, (i + by) % length) for i in range(length)])


def halves(value):
    high = value.astype(BF16)
    return high, (value - high.astype(F32)).astype(BF16)


def transposed_dot(left, right):
    return lax.dot_general(left, right, (((1,), (1,)), ((), ())), preferred_element_type=F32)


def plain_dot(left, right):
    return lax.dot_general(left, right, (((1,), (0,)), ((), ())), preferred_element_type=F32)


def delta_rows(extent, cell, fraction):
    step = lax.broadcasted_iota(jnp.int32, (extent, cell.shape[1]), 0).astype(F32) - cell
    radius = jnp.abs(step - fraction)
    near = (step == 0.0) | (step == 1.0)
    far = (step == -1.0) | (step == 2.0)
    inner = (3.0 - 2.0 * radius + jnp.sqrt(jnp.maximum(1.0 + 4.0 * radius - 4.0 * radius * radius, 0.0))) / 8.0
    outer = (5.0 - 2.0 * radius - jnp.sqrt(jnp.maximum(-7.0 + 12.0 * radius - 4.0 * radius * radius, 0.0))) / 8.0
    return jnp.where(near, inner, jnp.where(far, outer, 0.0))


def assemble_kernel(own, below_x, above_x, below_y, above_y, main, low, high):
    main[...] = jnp.ones(main.shape, F32)
    for field in range(4):
        for plane in range(PLANES):
            row = field * ROWS + plane * YPAD
            if plane < 2:
                piece = below_x[field, plane]
            elif plane < 10:
                piece = own[field, plane - 2]
            else:
                piece = above_x[field, plane - 10]
            main[row + 2 : row + 10, :] = piece
            main[row : row + 2, :] = below_y[field, plane]
            main[row + 10 : row + 13, :] = above_y[field, plane]
    for block in range(7):
        turned = main[block * 128 : block * 128 + 128, :].T
        low[:, block * 128 : block * 128 + 128] = turned[0:8]
        high[:, block * 128 : block * 128 + 128] = turned[120:128]


def tables_kernel(own, below_x, above_x, below_y, above_y, plane_weights, z_high, z_low):
    pieces = [(own, 0, 0.0, 0.0), (below_x, 0, -8.0, 0.0), (above_x, 0, 8.0, 0.0)]
    for group, along_y in ((below_y, -8.0), (above_y, 8.0)):
        for part, along_x in enumerate((0.0, -8.0, 8.0)):
            pieces.append((group, 16 * part, along_x, along_y))
    for block, (ref, first, along_x, along_y) in enumerate(pieces):
        for half in range(2):
            row = lambda k: ref[first + 2 * k + half : first + 2 * k + half + 1, :]
            place = slice(block * 256 + half * 128, block * 256 + half * 128 + 128)
            plane_weights[0:16, place] = delta_rows(16, row(0) + (along_x + 2.0), row(3))
            plane_weights[16:32, place] = delta_rows(16, row(1) + (along_y + 2.0), row(4))
            high, rest = halves(delta_rows(144, row(2) + 2.0, row(5)))
            z_high[0:144, place] = high
            z_low[0:144, place] = rest
    z_high[144:256, :] = jnp.zeros((112, COLS), BF16)
    z_low[144:256, :] = jnp.zeros((112, COLS), BF16)


def interpolated(velocity, plane_weights, z_high, z_low):
    rows = []
    for field in velocity:
        high, rest = halves(field)
        partial = plain_dot(high, z_high) + plain_dot(rest, z_high) + plain_dot(high, z_low)
        total = jnp.zeros((YPAD, MARKERS), F32)
        for plane in range(11):
            total = total + partial[plane * YPAD : plane * YPAD + YPAD] * plane_weights[plane + 1 : plane + 2, 0:MARKERS]
        line = jnp.sum(total * plane_weights[16:32, 0:MARKERS], axis=0, keepdims=True)
        rows += [line[:, 0:128], line[:, 128:256]]
    rows.append(jnp.zeros((2, 128), F32))
    return jnp.concatenate(rows, axis=0)


def setup_kernel(main, low, high, plane_weights, z_high, z_low, aux, scale, start, wide):
    lane = lax.broadcasted_iota(jnp.int32, (128, 128), 1)
    row8 = lax.broadcasted_iota(jnp.int32, (8, 128), 0)
    for block in range(7):
        place = slice(block * 128, block * 128 + 128)
        edge = jnp.where(row8 < 2, pltpu.roll(high[:, place], 2, 0), pltpu.roll(low[:, place], 2, 0))
        edge = jnp.concatenate([edge, jnp.zeros((120, 128), F32)], axis=0).T
        body_rows = pltpu.roll(main[place, :], 2, 1)
        wide[place, 0:128] = jnp.where(lane < 2, edge, body_rows)
        wide[place, 128:256] = jnp.where(lane < 2, body_rows, jnp.where(lane < 5, edge, 1.0))
    scale[...] = lax.rsqrt(wide[3 * ROWS : 4 * ROWS, :])
    velocity = [wide[c * ROWS + YPAD : c * ROWS + YPAD + INNER, :] for c in range(3)]
    image = interpolated(velocity, plane_weights, z_high[:, 0:MARKERS], z_low[:, 0:MARKERS])
    start[...] = aux[0:8, :] * (aux[16:24, :] - image)


def spread_kernel(
    own, below_x, above_x, below_y, above_y, plane_weights, z_high, z_low, scale, velocity, low, high, left_high, left_low, field, edges
):
    pieces = [(own, 0), (below_x, 0), (above_x, 0)]
    pieces += [(below_y, 8 * part) for part in range(3)] + [(above_y, 8 * part) for part in range(3)]
    for block, (ref, first) in enumerate(pieces):
        for half in range(2):
            place = slice(block * 256 + half * 128, block * 256 + half * 128 + 128)
            along_y = plane_weights[16:32, place]
            vector = [ref[first + 2 * c + half : first + 2 * c + half + 1, :] * along_y for c in range(3)]
            for plane in range(PLANES):
                along_x = plane_weights[plane : plane + 1, place]
                for c in range(3):
                    top, rest = halves(vector[c] * along_x)
                    row = c * ROWS + plane * YPAD
                    left_high[row : row + YPAD, place] = top
                    left_low[row : row + YPAD, place] = rest
    for c in range(3):
        rows = slice(c * ROWS, c * ROWS + ROWS)
        moved = transposed_dot(left_high[rows, :], z_high[...])
        moved += transposed_dot(left_low[rows, :], z_high[...])
        moved += transposed_dot(left_high[rows, :], z_low[...])
        field[rows, :] = moved * scale[...]
    axial, diagonal = 1.0 / 6.0, 1.0 / 12.0
    up_y = lambda a: pltpu.roll(a, 1, 0)
    down_y = lambda a: pltpu.roll(a, YPAD - 1, 0)
    up_z = lambda a: pltpu.roll(a, 1, 1)
    down_z = lambda a: pltpu.roll(a, LANES - 1, 1)
    onward = [None] * PLANES
    back = [None] * PLANES
    still = [None] * PLANES
    lane = lax.broadcasted_iota(jnp.int32, (YPAD, 128), 1)
    edges[INNER:256, :] = jnp.zeros((256 - INNER, 128), F32)
    for plane in range(PLANES):
        gx, gy, gz = (field[c * ROWS + plane * YPAD : c * ROWS + plane * YPAD + YPAD, :] for c in range(3))
        hx, hy, hz = gx * diagonal, gy * diagonal, gz * diagonal
        sum_xy, dif_xy = hx + hy, hx - hy
        zx_up, zy_up, zz_up = up_z(hx), up_z(hy), up_z(hz)
        zx_dn, zy_dn, zz_dn = down_z(hx), down_z(hy), down_z(hz)
        xz_sum_up, xz_sum_dn, xz_dif_up, xz_dif_dn = zx_up + zz_up, zx_dn + zz_dn, zx_up - zz_up, zx_dn - zz_dn
        xy_sum_up, xy_sum_dn, xy_dif_up, xy_dif_dn = up_y(sum_xy), down_y(sum_xy), up_y(dif_xy), down_y(dif_xy)
        ax = gx * axial
        onward[plane] = (
            ax + ((xy_sum_up + xy_dif_dn) + (xz_sum_up + xz_dif_dn)),
            xy_sum_up - xy_dif_dn,
            xz_sum_up - xz_dif_dn,
        )
        back[plane] = (
            ax + ((xy_sum_dn + xy_dif_up) + (xz_sum_dn + xz_dif_up)),
            xy_sum_dn - xy_dif_up,
            xz_sum_dn - xz_dif_up,
        )
        yz_same = up_y(zy_up + zz_up)
        yz_same_dn = down_y(zy_dn + zz_dn)
        yz_cross = up_y(zy_dn - zz_dn)
        yz_cross_dn = down_y(zy_up - zz_up)
        same, cross = yz_same + yz_same_dn, yz_cross + yz_cross_dn
        still[plane] = (
            gx,
            gy + ((up_y(hy) + down_y(hy)) * 2.0 + (same + cross)),
            gz + ((zz_up + zz_dn) * 2.0 + (same - cross)),
        )
        if plane >= 2:
            out = plane - 1
            factor = scale[out * YPAD : out * YPAD + YPAD, :] * 0.5
            first = (out - 1) * YPAD
            packed = jnp.zeros((YPAD, 128), F32)
            for c in range(3):
                value = (still[out][c] + (onward[out - 1][c] + back[out + 1][c])) * factor
                velocity[c * INNER + first : c * INNER + first + YPAD, :] = value
                near = value[:, 0:128]
                beyond = value[:, 128:256]
                near = pltpu.roll(near, 4 * c, 1) if c else near
                packed = jnp.where((lane >= 4 * c) & (lane < 4 * c + 4), near, packed)
                at = 16 + 4 * c
                packed = jnp.where((lane >= at) & (lane < at + 4), pltpu.roll(beyond, at - 1, 1), packed)
            edges[first : first + YPAD, :] = packed
    for block in range(2):
        place = slice(block * 128, block * 128 + 128)
        turned = edges[place, :].T
        low[:, place] = turned[0:16]
        high[:, place] = turned[16:32]


def apply_image(velocity, low, high, plane_weights, z_high, z_low, aux, vector):
    lane = lax.broadcasted_iota(jnp.int32, (INNER, 128), 1)
    columns = []
    for block in range(2):
        place = slice(block * 128, block * 128 + 128)
        columns.append(jnp.concatenate([high[:, place], low[:, place], jnp.zeros((96, 128), F32)], axis=0).T)
    edge = jnp.concatenate(columns, axis=0)[0:INNER]
    fields = []
    for c in range(3):
        mine = velocity[c * INNER : c * INNER + INNER, :]
        near = jnp.where((lane >= 1) & (lane < 5), pltpu.roll(edge, (1 - 4 * c) % 128, 1), 0.0)
        beyond = jnp.where(lane < 4, pltpu.roll(edge, (112 - 4 * c) % 128, 1), 0.0)
        fields.append(mine + jnp.concatenate([near, beyond], axis=1))
    image = interpolated(fields, plane_weights, z_high[:, 0:MARKERS], z_low[:, 0:MARKERS])
    return aux[0:8, :] * (image + aux[8:16, :] * vector[...])


def image_kernel(velocity, low, high, plane_weights, z_high, z_low, aux, vector, result):
    result[...] = apply_image(velocity, low, high, plane_weights, z_high, z_low, aux, vector)


def two_sum(a, b):
    total = a + b
    part = total - a
    return total, (a - (total - part)) + (b - part)


def fast_two_sum(a, b):
    total = a + b
    return total, b - (total - a)


def split(a):
    scaled = a * 4097.0
    high = scaled - (scaled - a)
    return high, a - high


def two_product(a, b):
    product = a * b
    a_high, a_low = split(a)
    b_high, b_low = split(b)
    return product, ((a_high * b_high - product) + a_high * b_low + a_low * b_high) + a_low * b_low


def pair_add(a, b):
    head, tail = two_sum(a[0], b[0])
    return fast_two_sum(head, tail + (a[1] + b[1]))


def pair_negative(a):
    return (-a[0], -a[1])


def pair_multiply(a, b):
    head, tail = two_product(a[0], b[0])
    return fast_two_sum(head, tail + (a[0] * b[1] + a[1] * b[0]))


def pair_divide(a, b):
    first = a[0] / b[0]
    rest = pair_add(a, pair_negative(pair_multiply((first, jnp.zeros_like(first)), b)))
    return fast_two_sum(first, rest[0] / b[0])


ENTRIES = ((0, 0), (0, 1), (0, 2), (0, 3), (1, 1), (1, 2), (1, 3), (2, 2), (2, 3))


def last_kernel(velocity, low, high, plane_weights, z_high, z_low, aux, first, second, third, sums):
    fourth = apply_image(velocity, low, high, plane_weights, z_high, z_low, aux, third)
    vectors = [first[...], second[...], third[...], fourth]
    lane = lax.broadcasted_iota(jnp.int32, (8, 128), 1)
    packed = jnp.zeros((8, 128), F32)
    for at, (i, j) in enumerate(ENTRIES):
        value = two_product(vectors[i], vectors[j])
        for axis, steps in ((0, (4, 2, 1)), (1, (64, 32, 16, 8, 4, 2, 1))):
            for step in steps:
                value = pair_add(value, (pltpu.roll(value[0], step, axis), pltpu.roll(value[1], step, axis)))
        packed = jnp.where(lane == at, value[0], jnp.where(lane == 16 + at, value[1], packed))
    for block in range(sums.shape[0] // 8):
        sums[block * 8 : block * 8 + 8, :] = packed


def finish_kernel(gathered, first, second, third, forces):
    a = gathered[...]
    count = a.shape[0]
    value = (a, pltpu.roll(a, 112, 1))
    while count > 8:
        count //= 2
        value = pair_add(
            (value[0][0:count], value[1][0:count]), (value[0][count : 2 * count], value[1][count : 2 * count])
        )
    for step in (4, 2, 1):
        value = pair_add(value, (pltpu.roll(value[0], step, 0), pltpu.roll(value[1], step, 0)))
    lane = lax.broadcasted_iota(jnp.int32, (8, 128), 1)
    gram = {}
    for at, (i, j) in enumerate(ENTRIES):
        entry = tuple(
            jnp.broadcast_to(jnp.sum(jnp.where(lane == at, v, 0.0), axis=1, keepdims=True), (8, 128)) for v in value
        )
        gram[i, j] = entry
        gram[j, i] = entry
    add, times = pair_add, pair_multiply
    minus = lambda a, b: pair_add(a, pair_negative(b))

    def form(left, right, shift):
        total = None
        for i, a in enumerate(left):
            for j, b in enumerate(right):
                term = times(times(a, b), gram[i, j + shift])
                total = term if total is None else add(total, term)
        return total

    one = (jnp.ones((8, 128), F32), jnp.zeros((8, 128), F32))
    alpha0 = pair_divide(gram[0, 0], gram[0, 1])
    residual = [one, pair_negative(alpha0)]
    norm1 = form(residual, residual, 0)
    beta0 = pair_divide(norm1, gram[0, 0])
    along1 = [add(one, beta0), pair_negative(alpha0)]
    alpha1 = pair_divide(norm1, form(along1, along1, 1))
    residual = [one, minus(residual[1], times(alpha1, along1[0])), pair_negative(times(alpha1, along1[1]))]
    norm2 = form(residual, residual, 0)
    beta1 = pair_divide(norm2, norm1)
    along2 = [add(one, times(beta1, along1[0])), add(residual[1], times(beta1, along1[1])), residual[2]]
    alpha2 = pair_divide(norm2, form(along2, along2, 1))
    weight0 = add(alpha0, add(times(alpha1, along1[0]), times(alpha2, along2[0])))
    weight1 = add(times(alpha1, along1[1]), times(alpha2, along2[1]))
    weight2 = times(alpha2, along2[2])
    total = weight0[0] * first[...] + (weight1[0] * second[...] + weight2[0] * third[...])
    for c in range(3):
        forces[c : c + 1, 0:128] = total[2 * c : 2 * c + 1, :]
        forces[c : c + 1, 128:256] = total[2 * c + 1 : 2 * c + 2, :]


def call(kernel, name, outs, *operands, scratch=()):
    whole = pl.BlockSpec(memory_space=pltpu.VMEM)
    return pl.pallas_call(
        kernel,
        name=name,
        out_shape=[jax.ShapeDtypeStruct(shape, kind) for shape, kind in outs],
        in_specs=[whole] * len(operands),
        out_specs=[whole] * len(outs),
        scratch_shapes=list(scratch),
        compiler_params=PARAMS,
    )(*operands)


def body(density, base_velocity, cells, offsets, target, stiffness, counts):
    anchor = jnp.stack([lax.axis_index("gx") * 8, lax.axis_index(GY) * 8, lax.axis_index("gz") * 128])
    local = (cells - anchor[:, None]).astype(F32)
    lines = lambda a: a.reshape(-1, 128)
    zeros = lambda n: jnp.zeros((n, 128), F32)
    markers = jnp.concatenate([lines(local), lines(offsets), zeros(4)], axis=0)
    live = lines((jnp.arange(MARKERS, dtype=jnp.int32) < counts[0]).astype(F32))
    stiff = lines(stiffness)
    aux = jnp.concatenate(
        [live, live, live, zeros(2), stiff, stiff, stiff, zeros(2), lines(target), zeros(2)], axis=0
    )
    fields = jnp.concatenate([base_velocity, density[None]], axis=0)

    below_x = shifted(fields[:, 6:8], "gx", 1)
    above_x = shifted(fields[:, 0:3], "gx", -1)
    marks_below_x, marks_above_x = shifted(markers, "gx", 1), shifted(markers, "gx", -1)
    deep = jnp.concatenate([below_x, fields, above_x], axis=1)
    below_y = shifted(deep[:, :, 6:8], GY, 1)
    above_y = shifted(deep[:, :, 0:3], GY, -1)
    marks = jnp.concatenate([markers, marks_below_x, marks_above_x], axis=0)
    marks_below_y, marks_above_y = shifted(marks, GY, 1), shifted(marks, GY, -1)
    main, low, high = call(
        assemble_kernel, "assemble", [((896, 128), F32), ((8, 896), F32), ((8, 896), F32)],
        fields, below_x, above_x, below_y, above_y,
    )
    plane_weights, z_high, z_low = call(
        tables_kernel, "tables", [((32, COLS), F32), ((256, COLS), BF16), ((256, COLS), BF16)],
        markers, marks_below_x, marks_above_x, marks_below_y, marks_above_y,
    )
    from_above = shifted(low, "gz", -1)
    from_below = shifted(high, "gz", 1)
    tables = (plane_weights, z_high, z_low)
    scale, start = call(
        setup_kernel, "setup", [((ROWS, LANES), F32), ((8, 128), F32)],
        main, from_above, from_below, *tables, aux,
        scratch=[pltpu.VMEM((896, LANES), F32)],
    )

    def spread(vector):
        below, above = shifted(vector, "gx", 1), shifted(vector, "gx", -1)
        three = jnp.concatenate([vector, below, above], axis=0)
        below_three, above_three = shifted(three, GY, 1), shifted(three, GY, -1)
        velocity, low, high = call(
            spread_kernel, "spread", [((3 * INNER, LANES), F32), ((16, 256), F32), ((16, 256), F32)],
            vector, below, above, below_three, above_three, *tables, scale,
            scratch=[
                pltpu.VMEM((3 * ROWS, COLS), BF16), pltpu.VMEM((3 * ROWS, COLS), BF16),
                pltpu.VMEM((3 * ROWS, LANES), F32), pltpu.VMEM((256, 128), F32),
            ],
        )
        return velocity, shifted(low, "gz", -1), shifted(high, "gz", 1)

    vectors = [start]
    for step in range(2):
        (image,) = call(
            image_kernel, "image", [((8, 128), F32)],
            *spread(vectors[-1]), *tables, aux, vectors[-1],
        )
        vectors.append(image)
    (sums,) = call(
        last_kernel, "last", [((256, 128), F32)],
        *spread(vectors[-1]), *tables, aux, *vectors,
    )
    gathered = lax.all_to_all(sums, GX_GY_GZ, 0, 0, tiled=True)
    (forces,) = call(finish_kernel, "finish", [((3, MARKERS), F32)], gathered, *vectors)
    return forces


def solution(mesh):
    finer = Mesh(
        mesh.devices.reshape(mesh.shape["gx"], 4, 2, mesh.shape["gz"]), ("gx", "gy_0", "gy_1", "gz")
    )
    return jax.shard_map(
        body,
        mesh=finer,
        in_specs=(
            P("gx", GY, "gz"),
            P(None, "gx", GY, "gz"),
            P(None, GX_GY_GZ),
            P(None, GX_GY_GZ),
            P(None, GX_GY_GZ),
            P(GX_GY_GZ),
            P(GX_GY_GZ),
        ),
        out_specs=P(None, GX_GY_GZ),
        check_vma=False,
    )
```

time: 333 us -> 114 us (0.34); the launches traced: 326 us -> 113 us
  blocking collectives: 116 us -> 23.5 us
  other arithmetic: 60.4 us -> 5.19 us
  matrix products: 54.6 us -> 0 us
  Pallas kernels: 0 us -> 20 us
  waiting for transfers between devices: 35.7 us -> 21 us
  between operations: 11.6 us -> 0.84 us
  starting transfers between devices: 46.7 us -> 42 us
    psum x12 -> x0, blocking collectives: 116 us -> none  [one_axis_at_a_time(): shard = lax.psum(shard, axis)]
    dot_general x7 -> x0, matrix products: 54.6 us -> none  [the longest x3 48.7 us: spread_dense(): jnp.einsum('cxym,mz->cxyz', weighted, table_z, precision=lax.Precision.HI...]
    reduce_sum x9 -> x0, other arithmetic: 39 us -> none  [the longest x6 37 us: axis_rows(): return jnp.sum(delta_weights(fraction)[:, :, None] * hits, axis=0)]
    all_to_all x0 -> x1, blocking collectives: none -> 23.5 us  [body(): gathered = lax.all_to_all(sums, GX_GY_GZ, 0, 0, tiled=True)]
    pallas_call x0 -> x10, Pallas kernels: none -> 20 us  [call(): pl.pallas_call(kernel, name=name, out_shape=[jax.ShapeDtypeStruct(shape,...]
    mul x37 -> x0, other arithmetic: 12.5 us -> none  [the longest x15 7.43 us: stream_wide(): 3.0 * share * (along_x * piece[0] + along_y * piece[1] + along_z * piece[2])]
    ppermute x6 -> x0, waiting for transfers between devices: 7.94 us -> none  [the longest x3 7.18 us: extended(): lax.ppermute(tail, axis, [(i, (i + 1) % count) for i in range(count)])]
    ppermute x24 -> x28, waiting for transfers between devices: 27.7 us -> 21 us  [shifted(): lax.ppermute(shard, axis, [(i, (i + by) % length) for i in range(length)])]
  transfers between devices with their start and end apart: 30 -> 28, of which waited for: 17 -> 19; matrix products, arithmetic and copies ran while one was open for 14% -> 5% of each run, Pallas kernels for 0% -> 2%
where the time goes in v1:
time: 114 us; the launch traced here: 113 us
  starting transfers between devices  42 us (37%)
  blocking collectives  23.5 us (21%)
  waiting for transfers between devices  21 us (18%)
  Pallas kernels  20 us (18%)
  other arithmetic  5.19 us (5%)
    ppermute x28, starting transfers between devices, shifted(): lax.ppermute(shard, axis, [(i, (i + by) % length) for i in range(length)])  42 us
    all_to_all x1, blocking collectives, body(): gathered = lax.all_to_all(sums, GX_GY_GZ, 0, 0, tiled=True)  23.5 us
    ppermute x28, waiting for transfers between devices, shifted(): lax.ppermute(shard, axis, [(i, (i + by) % length) for i in range(length)])  21 us
    pallas_call x10, Pallas kernels, call(): pl.pallas_call(kernel, name=name, out_shape=[jax.ShapeDtypeStruct(shape,...  20 us
    concatenate x3, other arithmetic, body(): fields = jnp.concatenate([base_velocity, density[None]], axis=0)  2.47 us
  transfers between devices with their start and end apart: 28, of which 19 were waited for; matrix products, arithmetic and copies ran while one was open for 5% of the time, Pallas kernels for 2%

profile of v1, /device:TPU:1, one launch (start us, length us, event | category | flops | bytes accessed | tf_op | source)
XLA Modules:
  0.0 113.4 jit_solution(5379599864867979339)
XLA Ops:
  0.8 2.5 %collective-permute-start = (f32[4,2,8,128]{3,2,1,0:T(8,128)S(1)}, f32[4,2,8,128]{3,2,1,0:T(8,128)S(1)}, u32[]{:S(2)}, u32[]{:S(2)}) collective-permute-start(f32[4,2,8,128]{3,2,1,0:T(8,128)S(1)} %fusion.1), channel_id=1, source_target_pairs={{0,32},{32,64},{64,96},{96,128},{128,160},{160,192},{192,224},{224... | collective-permute-start | bytes 98312 | tf_op jit(solution)/shard_map/ppermute | solution.py:27
  4.0 3.9 %collective-permute-start.1 = (f32[4,3,8,128]{3,2,1,0:T(8,128)S(1)}, f32[4,3,8,128]{3,2,1,0:T(8,128)S(1)}, u32[]{:S(2)}, u32[]{:S(2)}) collective-permute-start(f32[4,3,8,128]{3,2,1,0:T(8,128)S(1)} %fusion), channel_id=1, source_target_pairs={{0,224},{32,0},{64,32},{96,64},{128,96},{160,128},{192,160},{224,1... | collective-permute-start | bytes 147464 | tf_op jit(solution)/shard_map/ppermute | solution.py:27
  9.5 1.5 %collective-permute-start.7 = (f32[16,128]{1,0:T(8,128)S(1)}, f32[16,128]{1,0:T(8,128)S(1)}, u32[]{:S(2)}, u32[]{:S(2)}) collective-permute-start(f32[16,128]{1,0:T(8,128)S(1)} %pad_maximum_fusion.7.own), channel_id=1, source_target_pairs={{0,224},{32,0},{64,32},{96,64},{128,96},{160,128},{192,160},{224,1... | collective-permute-start | bytes 24584 | tf_op jit(solution)/shard_map/ppermute | solution.py:27
  12.0 2.7 %collective-permute-start.2 = (f32[4,13,2,128]{3,2,1,0:T(2,128)S(1)}, f32[4,13,2,128]{3,2,1,0:T(2,128)S(1)}, u32[]{:S(2)}, u32[]{:S(2)}) collective-permute-start(f32[4,13,2,128]{3,2,1,0:T(2,128)S(1)} %pad_maximum_fusion.4), channel_id=1, source_target_pairs={{0,4},{4,8},{8,12},{12,16},{16,20},{20,24},{24,28},{28,0},{1,5},{5... | collective-permute-start | bytes 159752 | tf_op jit(solution)/shard_map/ppermute | solution.py:27
  17.4 1.8 %collective-permute-start.9 = (f32[48,128]{1,0:T(8,128)S(1)}, f32[48,128]{1,0:T(8,128)S(1)}, u32[]{:S(2)}, u32[]{:S(2)}) collective-permute-start(f32[48,128]{1,0:T(8,128)S(1)} %concatenate.28), channel_id=1, source_target_pairs={{0,28},{4,0},{8,4},{12,8},{16,12},{20,16},{24,20},{28,24},{1,29},{... | collective-permute-start | bytes 73736 | tf_op jit(solution)/shard_map/ppermute | solution.py:27
  20.0 2.6 %collective-permute-start.4 = (f32[8,896]{1,0:T(8,128)S(1)}, f32[8,896]{1,0:T(8,128)S(1)}, u32[]{:S(2)}, u32[]{:S(2)}) collective-permute-start(f32[8,896]{1,0:T(8,128)S(1)} %get-tuple-element.23), channel_id=1, source_target_pairs={{0,3},{1,0},{2,1},{3,2},{4,7},{5,4},{6,5},{7,6},{8,11},{9,8},{10,9... | collective-permute-start | bytes 86024 | tf_op jit(solution)/shard_map/ppermute | solution.py:27
  22.7 2.3 %tables.1 = (f32[32,2304]{1,0:T(8,128)S(1)}, bf16[256,2304]{1,0:T(8,128)(2,1)S(1)}, bf16[256,2304]{1,0:T(8,128)(2,1)S(1)}) custom-call(f32[16,128]{1,0:T(8,128)S(1)} %pad_maximum_fusion.7.own, f32[16,128]{1,0:T(8,128)S(1)} %collective-permute-done.6.below_x, f32[16,128]{1,0:T(8,128)S(1)} %collective-permute-done.7.above_x, ...), custom_call_target="tpu_custom_call" | custom-call | tf_op jit(solution)/shard_map/tables/pallas_call | solution.py:341
  25.0 1.5 %collective-permute-done.5.high = f32[8,896]{1,0:T(8,128)S(1)} collective-permute-done((f32[8,896]{1,0:T(8,128)S(1)}, f32[8,896]{1,0:T(8,128)S(1)}, u32[]{:S(2)}, u32[]{:S(2)}) %collective-permute-start.5) | collective-permute-done | bytes 28704 | tf_op jit(solution)/shard_map/ppermute | solution.py:27
  27.1 3.2 %collective-permute-start.11 = (f32[8,128]{1,0:T(8,128)S(1)}, f32[8,128]{1,0:T(8,128)S(1)}, u32[]{:S(2)}, u32[]{:S(2)}) collective-permute-start(f32[8,128]{1,0:T(8,128)S(1)} %get-tuple-element.28.own.vector.first), channel_id=1, source_target_pairs={{0,224},{32,0},{64,32},{96,64},{128,96},{160,128},{192,160},{224,1... | collective-permute-start | bytes 12296 | tf_op jit(solution)/shard_map/ppermute | solution.py:27
  31.1 2.2 %collective-permute-start.13 = (f32[24,128]{1,0:T(8,128)S(1)}, f32[24,128]{1,0:T(8,128)S(1)}, u32[]{:S(2)}, u32[]{:S(2)}) collective-permute-start(f32[24,128]{1,0:T(8,128)S(1)} %constant_dynamic-update-slice_fusion), channel_id=1, source_target_pairs={{0,28},{4,0},{8,4},{12,8},{16,12},{20,16},{24,20},{28,24},{1,29},{... | collective-permute-start | bytes 36872 | tf_op jit(solution)/shard_map/ppermute | solution.py:27
  33.3 1.3 %collective-permute-done.13.above_y = f32[24,128]{1,0:T(8,128)S(1)} collective-permute-done((f32[24,128]{1,0:T(8,128)S(1)}, f32[24,128]{1,0:T(8,128)S(1)}, u32[]{:S(2)}, u32[]{:S(2)}) %collective-permute-start.13) | collective-permute-done | bytes 12320 | tf_op jit(solution)/shard_map/ppermute | solution.py:27
  34.7 4.4 %spread.3 = (f32[528,256]{1,0:T(8,128)S(1)}, f32[16,256]{1,0:T(8,128)S(1)}, f32[16,256]{1,0:T(8,128)S(1)}) custom-call(f32[8,128]{1,0:T(8,128)S(1)} %get-tuple-element.28.own.vector.first, f32[8,128]{1,0:T(8,128)S(1)} %collective-permute-done.10.below_x, f32[8,128]{1,0:T(8,128)S(1)} %collective-permute-done.11.above_x, ...), custom_call_target="tpu_custom_call" | custom-call | tf_op jit(solution)/shard_map/spread/pallas_call | solution.py:341
  39.1 1.3 %collective-permute-start.14 = (f32[16,256]{1,0:T(8,128)S(1)}, f32[16,256]{1,0:T(8,128)S(1)}, u32[]{:S(2)}, u32[]{:S(2)}) collective-permute-start(f32[16,256]{1,0:T(8,128)S(1)} %get-tuple-element.31), channel_id=1, source_target_pairs={{0,3},{1,0},{2,1},{3,2},{4,7},{5,4},{6,5},{7,6},{8,11},{9,8},{10,9... | collective-permute-start | bytes 49160 | tf_op jit(solution)/shard_map/ppermute | solution.py:27
  40.7 1.1 collective-permute-done.14.low
  41.8 2.4 %collective-permute-done.15.high = f32[16,256]{1,0:T(8,128)S(1)} collective-permute-done((f32[16,256]{1,0:T(8,128)S(1)}, f32[16,256]{1,0:T(8,128)S(1)}, u32[]{:S(2)}, u32[]{:S(2)}) %collective-permute-start.15) | collective-permute-done | bytes 16416 | tf_op jit(solution)/shard_map/ppermute | solution.py:27
  44.8 3.2 %collective-permute-start.17 = (f32[8,128]{1,0:T(8,128)S(1)}, f32[8,128]{1,0:T(8,128)S(1)}, u32[]{:S(2)}, u32[]{:S(2)}) collective-permute-start(f32[8,128]{1,0:T(8,128)S(1)} %image.2.own.vector.second), channel_id=1, source_target_pairs={{0,224},{32,0},{64,32},{96,64},{128,96},{160,128},{192,160},{224,1... | collective-permute-start | bytes 12296 | tf_op jit(solution)/shard_map/ppermute | solution.py:27
  48.8 2.9 %collective-permute-done.16.below_x = f32[8,128]{1,0:T(8,128)S(1)} collective-permute-done((f32[8,128]{1,0:T(8,128)S(1)}, f32[8,128]{1,0:T(8,128)S(1)}, u32[]{:S(2)}, u32[]{:S(2)}) %collective-permute-start.16) | collective-permute-done | bytes 4128 | tf_op jit(solution)/shard_map/ppermute | solution.py:27
  51.7 6.5 %collective-permute-start.19 = (f32[24,128]{1,0:T(8,128)S(1)}, f32[24,128]{1,0:T(8,128)S(1)}, u32[]{:S(2)}, u32[]{:S(2)}) collective-permute-start(f32[24,128]{1,0:T(8,128)S(1)} %pad_maximum_fusion.5), channel_id=1, source_target_pairs={{0,28},{4,0},{8,4},{12,8},{16,12},{20,16},{24,20},{28,24},{1,29},{... | collective-permute-start | bytes 36872 | tf_op jit(solution)/shard_map/ppermute | solution.py:27
  59.4 4.4 %spread.4 = (f32[528,256]{1,0:T(8,128)S(1)}, f32[16,256]{1,0:T(8,128)S(1)}, f32[16,256]{1,0:T(8,128)S(1)}) custom-call(f32[8,128]{1,0:T(8,128)S(1)} %image.2.own.vector.second, f32[8,128]{1,0:T(8,128)S(1)} %collective-permute-done.16.below_x, f32[8,128]{1,0:T(8,128)S(1)} %collective-permute-done.17.above_x, f32[24,128]{1,0:T(8,128)S(1)} %collective-permute-done.18.below_y, ...), custom_call_target="tpu_custom_call" | custom-call | tf_op jit(solution)/shard_map/spread/pallas_call | solution.py:341
  63.8 1.5 %collective-permute-start.21 = (f32[16,256]{1,0:T(8,128)S(1)}, f32[16,256]{1,0:T(8,128)S(1)}, u32[]{:S(2)}, u32[]{:S(2)}) collective-permute-start(f32[16,256]{1,0:T(8,128)S(1)} %get-tuple-element.35), channel_id=1, source_target_pairs={{0,1},{1,2},{2,3},{3,0},{4,5},{5,6},{6,7},{7,4},{8,9},{9,10},{10,1... | collective-permute-start | bytes 49160 | tf_op jit(solution)/shard_map/ppermute | solution.py:27
  65.3 1.1 collective-permute-done.20.low
  66.4 1.3 %collective-permute-done.21.high = f32[16,256]{1,0:T(8,128)S(1)} collective-permute-done((f32[16,256]{1,0:T(8,128)S(1)}, f32[16,256]{1,0:T(8,128)S(1)}, u32[]{:S(2)}, u32[]{:S(2)}) %collective-permute-start.21) | collective-permute-done | bytes 16416 | tf_op jit(solution)/shard_map/ppermute | solution.py:27
  68.6 1.5 %collective-permute-start.22 = (f32[8,128]{1,0:T(8,128)S(1)}, f32[8,128]{1,0:T(8,128)S(1)}, u32[]{:S(2)}, u32[]{:S(2)}) collective-permute-start(f32[8,128]{1,0:T(8,128)S(1)} %image.3.own.third), channel_id=1, source_target_pairs={{0,32},{32,64},{64,96},{96,128},{128,160},{160,192},{192,224},{224... | collective-permute-start | bytes 12296 | tf_op jit(solution)/shard_map/ppermute | solution.py:27
  70.1 1.3 %collective-permute-done.23.above_x = f32[8,128]{1,0:T(8,128)S(1)} collective-permute-done((f32[8,128]{1,0:T(8,128)S(1)}, f32[8,128]{1,0:T(8,128)S(1)}, u32[]{:S(2)}, u32[]{:S(2)}) %collective-permute-start.23) | collective-permute-done | bytes 4128 | tf_op jit(solution)/shard_map/ppermute | solution.py:27
  72.4 5.5 %collective-permute-start.25 = (f32[24,128]{1,0:T(8,128)S(1)}, f32[24,128]{1,0:T(8,128)S(1)}, u32[]{:S(2)}, u32[]{:S(2)}) collective-permute-start(f32[24,128]{1,0:T(8,128)S(1)} %pad_maximum_fusion.6), channel_id=1, source_target_pairs={{0,28},{4,0},{8,4},{12,8},{16,12},{20,16},{24,20},{28,24},{1,29},{... | collective-permute-start | bytes 36872 | tf_op jit(solution)/shard_map/ppermute | solution.py:27
  79.1 4.4 %spread.5 = (f32[528,256]{1,0:T(8,128)S(1)}, f32[16,256]{1,0:T(8,128)S(1)}, f32[16,256]{1,0:T(8,128)S(1)}) custom-call(f32[8,128]{1,0:T(8,128)S(1)} %image.3.own.third, f32[8,128]{1,0:T(8,128)S(1)} %collective-permute-done.22.below_x, f32[8,128]{1,0:T(8,128)S(1)} %collective-permute-done.23.above_x, f32[24,128]{1,0:T(8,128)S(1)} %collective-permute-done.24.below_y, ...), custom_call_target="tpu_custom_call" | custom-call | tf_op jit(solution)/shard_map/spread/pallas_call | solution.py:341
  83.5 1.5 %collective-permute-start.27 = (f32[16,256]{1,0:T(8,128)S(1)}, f32[16,256]{1,0:T(8,128)S(1)}, u32[]{:S(2)}, u32[]{:S(2)}) collective-permute-start(f32[16,256]{1,0:T(8,128)S(1)} %get-tuple-element.38), channel_id=1, source_target_pairs={{0,1},{1,2},{2,3},{3,0},{4,5},{5,6},{6,7},{7,4},{8,9},{9,10},{10,1... | collective-permute-start | bytes 49160 | tf_op jit(solution)/shard_map/ppermute | solution.py:27
  85.0 1.1 collective-permute-done.26.low
  86.1 1.3 %collective-permute-done.27.high = f32[16,256]{1,0:T(8,128)S(1)} collective-permute-done((f32[16,256]{1,0:T(8,128)S(1)}, f32[16,256]{1,0:T(8,128)S(1)}, u32[]{:S(2)}, u32[]{:S(2)}) %collective-permute-start.27) | collective-permute-done | bytes 16416 | tf_op jit(solution)/shard_map/ppermute | solution.py:27
  87.4 1.2 %last.1 = f32[256,128]{1,0:T(8,128)S(1)} custom-call(f32[528,256]{1,0:T(8,128)S(1)} %get-tuple-element.36.velocity, f32[16,256]{1,0:T(8,128)S(1)} %collective-permute-done.26.low, f32[16,256]{1,0:T(8,128)S(1)} %collective-permute-done.27.high, f32[32,2304]{1,0:T(8,128)S(1)} %get-tuple-element.25.plane_weights, ...), custom_call_target="tpu_custom_call" | custom-call | tf_op jit(solution)/shard_map/last/pallas_call | solution.py:341
  88.6 23.5 %all_to_all.11 = f32[256,1,128]{2,1,0:T(1,128)S(1)} all-to-all(f32[256,1,128]{2,1,0:T(1,128)S(1)} %bitcast.11), channel_id=1, replica_groups=mesh['gx'=8,'gy_0'=4,'gy_1'=2,'gz'=4] {'gx','gy_0','gy_1','gz'}, dimensions={0} | all-to-all | bytes 262144 | tf_op jit(solution)/shard_map/all_to_all | solution.py:415
  112.1 1.3 %finish.1 = f32[3,256]{1,0:T(4,128)} custom-call(f32[256,128]{1,0:T(8,128)S(1)} %bitcast.12, f32[8,128]{1,0:T(8,128)S(1)} %get-tuple-element.28.own.vector.first, f32[8,128]{1,0:T(8,128)S(1)} %image.2.own.vector.second, f32[8,128]{1,0:T(8,128)S(1)} %image.3.own.third), custom_call_target="tpu_custom_call" | custom-call | tf_op jit(solution)/shard_map/finish/pallas_call | solution.py:341
  (60 shorter events, 14.5 us)
Async XLA Ops:
  0.0 22.6 %copy-start.1 = (f32[3,256]{1,0:T(4,128)S(1)}, f32[3,256]{1,0:T(4,128)}, u32[]{:S(2)}) copy-start(f32[3,256]{1,0:T(4,128)} %param.11) | copy-start | bytes 9220
  0.0 22.6 %copy-start = (f32[256]{0:T(256)S(1)}, f32[256]{0:T(256)}, u32[]{:S(2)}) copy-start(f32[256]{0:T(256)} %param.12) | copy-start | bytes 3076
  0.8 10.3 %collective-permute-start = (f32[4,2,8,128]{3,2,1,0:T(8,128)S(1)}, f32[4,2,8,128]{3,2,1,0:T(8,128)S(1)}, u32[]{:S(2)}, u32[]{:S(2)}) collective-permute-start(f32[4,2,8,128]{3,2,1,0:T(8,128)S(1)} %fusion.1), channel_id=1, source_target_pairs={{0,32},{32,64},{64,96},{96,128},{128,160},{160,192},{192,224},{224... | collective-permute-start | bytes 98312 | tf_op jit(solution)/shard_map/ppermute | solution.py:27
  4.0 7.0 %collective-permute-start.1 = (f32[4,3,8,128]{3,2,1,0:T(8,128)S(1)}, f32[4,3,8,128]{3,2,1,0:T(8,128)S(1)}, u32[]{:S(2)}, u32[]{:S(2)}) collective-permute-start(f32[4,3,8,128]{3,2,1,0:T(8,128)S(1)} %fusion), channel_id=1, source_target_pairs={{0,224},{32,0},{64,32},{96,64},{128,96},{160,128},{192,160},{224,1... | collective-permute-start | bytes 147464 | tf_op jit(solution)/shard_map/ppermute | solution.py:27
  9.5 7.7 %collective-permute-start.7 = (f32[16,128]{1,0:T(8,128)S(1)}, f32[16,128]{1,0:T(8,128)S(1)}, u32[]{:S(2)}, u32[]{:S(2)}) collective-permute-start(f32[16,128]{1,0:T(8,128)S(1)} %pad_maximum_fusion.7.own), channel_id=1, source_target_pairs={{0,224},{32,0},{64,32},{96,64},{128,96},{160,128},{192,160},{224,1... | collective-permute-start | bytes 24584 | tf_op jit(solution)/shard_map/ppermute | solution.py:27
  11.0 6.2 %collective-permute-start.6 = (f32[16,128]{1,0:T(8,128)S(1)}, f32[16,128]{1,0:T(8,128)S(1)}, u32[]{:S(2)}, u32[]{:S(2)}) collective-permute-start(f32[16,128]{1,0:T(8,128)S(1)} %pad_maximum_fusion.7.own), channel_id=1, source_target_pairs={{0,32},{32,64},{64,96},{96,128},{128,160},{160,192},{192,224},{224... | collective-permute-start | bytes 24584 | tf_op jit(solution)/shard_map/ppermute | solution.py:27
  12.0 7.2 %collective-permute-start.2 = (f32[4,13,2,128]{3,2,1,0:T(2,128)S(1)}, f32[4,13,2,128]{3,2,1,0:T(2,128)S(1)}, u32[]{:S(2)}, u32[]{:S(2)}) collective-permute-start(f32[4,13,2,128]{3,2,1,0:T(2,128)S(1)} %pad_maximum_fusion.4), channel_id=1, source_target_pairs={{0,4},{4,8},{8,12},{12,16},{16,20},{20,24},{24,28},{28,0},{1,5},{5... | collective-permute-start | bytes 159752 | tf_op jit(solution)/shard_map/ppermute | solution.py:27
  15.6 4.1 %collective-permute-start.3 = (f32[4,13,3,128]{3,2,1,0:T(4,128)S(1)}, f32[4,13,3,128]{3,2,1,0:T(4,128)S(1)}, u32[]{:S(2)}, u32[]{:S(2)}) collective-permute-start(f32[4,13,3,128]{3,2,1,0:T(4,128)S(1)} %pad_maximum_fusion.1), channel_id=1, source_target_pairs={{0,28},{4,0},{8,4},{12,8},{16,12},{20,16},{24,20},{28,24},{1,29},{... | collective-permute-start | bytes 239624 | tf_op jit(solution)/shard_map/ppermute | solution.py:27
  17.4 5.3 %collective-permute-start.9 = (f32[48,128]{1,0:T(8,128)S(1)}, f32[48,128]{1,0:T(8,128)S(1)}, u32[]{:S(2)}, u32[]{:S(2)}) collective-permute-start(f32[48,128]{1,0:T(8,128)S(1)} %concatenate.28), channel_id=1, source_target_pairs={{0,28},{4,0},{8,4},{12,8},{16,12},{20,16},{24,20},{28,24},{1,29},{... | collective-permute-start | bytes 73736 | tf_op jit(solution)/shard_map/ppermute | solution.py:27
  19.1 3.5 %collective-permute-start.8 = (f32[48,128]{1,0:T(8,128)S(1)}, f32[48,128]{1,0:T(8,128)S(1)}, u32[]{:S(2)}, u32[]{:S(2)}) collective-permute-start(f32[48,128]{1,0:T(8,128)S(1)} %concatenate.28), channel_id=1, source_target_pairs={{0,4},{4,8},{8,12},{12,16},{16,20},{20,24},{24,28},{28,0},{1,5},{5... | collective-permute-start | bytes 73736 | tf_op jit(solution)/shard_map/ppermute | solution.py:27
  20.0 5.0 %collective-permute-start.4 = (f32[8,896]{1,0:T(8,128)S(1)}, f32[8,896]{1,0:T(8,128)S(1)}, u32[]{:S(2)}, u32[]{:S(2)}) collective-permute-start(f32[8,896]{1,0:T(8,128)S(1)} %get-tuple-element.23), channel_id=1, source_target_pairs={{0,3},{1,0},{2,1},{3,2},{4,7},{5,4},{6,5},{7,6},{8,11},{9,8},{10,9... | collective-permute-start | bytes 86024 | tf_op jit(solution)/shard_map/ppermute | solution.py:27
  22.6 3.9 %collective-permute-start.5 = (f32[8,896]{1,0:T(8,128)S(1)}, f32[8,896]{1,0:T(8,128)S(1)}, u32[]{:S(2)}, u32[]{:S(2)}) collective-permute-start(f32[8,896]{1,0:T(8,128)S(1)} %get-tuple-element.24), channel_id=1, source_target_pairs={{0,1},{1,2},{2,3},{3,0},{4,5},{5,6},{6,7},{7,4},{8,9},{9,10},{10,1... | collective-permute-start | bytes 86024 | tf_op jit(solution)/shard_map/ppermute | solution.py:27
  27.0 4.0 %collective-permute-start.10 = (f32[8,128]{1,0:T(8,128)S(1)}, f32[8,128]{1,0:T(8,128)S(1)}, u32[]{:S(2)}, u32[]{:S(2)}) collective-permute-start(f32[8,128]{1,0:T(8,128)S(1)} %get-tuple-element.28.own.vector.first), channel_id=1, source_target_pairs={{0,32},{32,64},{64,96},{96,128},{128,160},{160,192},{192,224},{224... | collective-permute-start | bytes 12296 | tf_op jit(solution)/shard_map/ppermute | solution.py:27
  27.1 4.0 %collective-permute-start.11 = (f32[8,128]{1,0:T(8,128)S(1)}, f32[8,128]{1,0:T(8,128)S(1)}, u32[]{:S(2)}, u32[]{:S(2)}) collective-permute-start(f32[8,128]{1,0:T(8,128)S(1)} %get-tuple-element.28.own.vector.first), channel_id=1, source_target_pairs={{0,224},{32,0},{64,32},{96,64},{128,96},{160,128},{192,160},{224,1... | collective-permute-start | bytes 12296 | tf_op jit(solution)/shard_map/ppermute | solution.py:27
  31.1 3.6 %collective-permute-start.13 = (f32[24,128]{1,0:T(8,128)S(1)}, f32[24,128]{1,0:T(8,128)S(1)}, u32[]{:S(2)}, u32[]{:S(2)}) collective-permute-start(f32[24,128]{1,0:T(8,128)S(1)} %constant_dynamic-update-slice_fusion), channel_id=1, source_target_pairs={{0,28},{4,0},{8,4},{12,8},{16,12},{20,16},{24,20},{28,24},{1,29},{... | collective-permute-start | bytes 36872 | tf_op jit(solution)/shard_map/ppermute | solution.py:27
  33.3 1.4 %collective-permute-start.12 = (f32[24,128]{1,0:T(8,128)S(1)}, f32[24,128]{1,0:T(8,128)S(1)}, u32[]{:S(2)}, u32[]{:S(2)}) collective-permute-start(f32[24,128]{1,0:T(8,128)S(1)} %constant_dynamic-update-slice_fusion), channel_id=1, source_target_pairs={{0,4},{4,8},{8,12},{12,16},{16,20},{20,24},{24,28},{28,0},{1,5},{5... | collective-permute-start | bytes 36872 | tf_op jit(solution)/shard_map/ppermute | solution.py:27
  39.1 2.6 %collective-permute-start.14 = (f32[16,256]{1,0:T(8,128)S(1)}, f32[16,256]{1,0:T(8,128)S(1)}, u32[]{:S(2)}, u32[]{:S(2)}) collective-permute-start(f32[16,256]{1,0:T(8,128)S(1)} %get-tuple-element.31), channel_id=1, source_target_pairs={{0,3},{1,0},{2,1},{3,2},{4,7},{5,4},{6,5},{7,6},{8,11},{9,8},{10,9... | collective-permute-start | bytes 49160 | tf_op jit(solution)/shard_map/ppermute | solution.py:27
  40.4 3.8 %collective-permute-start.15 = (f32[16,256]{1,0:T(8,128)S(1)}, f32[16,256]{1,0:T(8,128)S(1)}, u32[]{:S(2)}, u32[]{:S(2)}) collective-permute-start(f32[16,256]{1,0:T(8,128)S(1)} %get-tuple-element.32), channel_id=1, source_target_pairs={{0,1},{1,2},{2,3},{3,0},{4,5},{5,6},{6,7},{7,4},{8,9},{9,10},{10,1... | collective-permute-start | bytes 49160 | tf_op jit(solution)/shard_map/ppermute | solution.py:27
  44.8 3.9 %collective-permute-start.17 = (f32[8,128]{1,0:T(8,128)S(1)}, f32[8,128]{1,0:T(8,128)S(1)}, u32[]{:S(2)}, u32[]{:S(2)}) collective-permute-start(f32[8,128]{1,0:T(8,128)S(1)} %image.2.own.vector.second), channel_id=1, source_target_pairs={{0,224},{32,0},{64,32},{96,64},{128,96},{160,128},{192,160},{224,1... | collective-permute-start | bytes 12296 | tf_op jit(solution)/shard_map/ppermute | solution.py:27
  48.0 3.7 %collective-permute-start.16 = (f32[8,128]{1,0:T(8,128)S(1)}, f32[8,128]{1,0:T(8,128)S(1)}, u32[]{:S(2)}, u32[]{:S(2)}) collective-permute-start(f32[8,128]{1,0:T(8,128)S(1)} %image.2.own.vector.second), channel_id=1, source_target_pairs={{0,32},{32,64},{64,96},{96,128},{128,160},{160,192},{192,224},{224... | collective-permute-start | bytes 12296 | tf_op jit(solution)/shard_map/ppermute | solution.py:27
  51.7 7.4 %collective-permute-start.19 = (f32[24,128]{1,0:T(8,128)S(1)}, f32[24,128]{1,0:T(8,128)S(1)}, u32[]{:S(2)}, u32[]{:S(2)}) collective-permute-start(f32[24,128]{1,0:T(8,128)S(1)} %pad_maximum_fusion.5), channel_id=1, source_target_pairs={{0,28},{4,0},{8,4},{12,8},{16,12},{20,16},{24,20},{28,24},{1,29},{... | collective-permute-start | bytes 36872 | tf_op jit(solution)/shard_map/ppermute | solution.py:27
  58.2 1.2 %collective-permute-start.18 = (f32[24,128]{1,0:T(8,128)S(1)}, f32[24,128]{1,0:T(8,128)S(1)}, u32[]{:S(2)}, u32[]{:S(2)}) collective-permute-start(f32[24,128]{1,0:T(8,128)S(1)} %pad_maximum_fusion.5), channel_id=1, source_target_pairs={{0,4},{4,8},{8,12},{12,16},{16,20},{20,24},{24,28},{28,0},{1,5},{5... | collective-permute-start | bytes 36872 | tf_op jit(solution)/shard_map/ppermute | solution.py:27
  63.8 2.6 %collective-permute-start.20 = (f32[16,256]{1,0:T(8,128)S(1)}, f32[16,256]{1,0:T(8,128)S(1)}, u32[]{:S(2)}, u32[]{:S(2)}) collective-permute-start(f32[16,256]{1,0:T(8,128)S(1)} %get-tuple-element.34), channel_id=1, source_target_pairs={{0,3},{1,0},{2,1},{3,2},{4,7},{5,4},{6,5},{7,6},{8,11},{9,8},{10,9... | collective-permute-start | bytes 49160 | tf_op jit(solution)/shard_map/ppermute | solution.py:27
  63.8 3.9 %collective-permute-start.21 = (f32[16,256]{1,0:T(8,128)S(1)}, f32[16,256]{1,0:T(8,128)S(1)}, u32[]{:S(2)}, u32[]{:S(2)}) collective-permute-start(f32[16,256]{1,0:T(8,128)S(1)} %get-tuple-element.35), channel_id=1, source_target_pairs={{0,1},{1,2},{2,3},{3,0},{4,5},{5,6},{6,7},{7,4},{8,9},{9,10},{10,1... | collective-permute-start | bytes 49160 | tf_op jit(solution)/shard_map/ppermute | solution.py:27
  68.3 3.1 %collective-permute-start.23 = (f32[8,128]{1,0:T(8,128)S(1)}, f32[8,128]{1,0:T(8,128)S(1)}, u32[]{:S(2)}, u32[]{:S(2)}) collective-permute-start(f32[8,128]{1,0:T(8,128)S(1)} %image.3.own.third), channel_id=1, source_target_pairs={{0,224},{32,0},{64,32},{96,64},{128,96},{160,128},{192,160},{224,1... | collective-permute-start | bytes 12296 | tf_op jit(solution)/shard_map/ppermute | solution.py:27
  68.6 3.7 %collective-permute-start.22 = (f32[8,128]{1,0:T(8,128)S(1)}, f32[8,128]{1,0:T(8,128)S(1)}, u32[]{:S(2)}, u32[]{:S(2)}) collective-permute-start(f32[8,128]{1,0:T(8,128)S(1)} %image.3.own.third), channel_id=1, source_target_pairs={{0,32},{32,64},{64,96},{96,128},{128,160},{160,192},{192,224},{224... | collective-permute-start | bytes 12296 | tf_op jit(solution)/shard_map/ppermute | solution.py:27
  72.4 6.3 %collective-permute-start.25 = (f32[24,128]{1,0:T(8,128)S(1)}, f32[24,128]{1,0:T(8,128)S(1)}, u32[]{:S(2)}, u32[]{:S(2)}) collective-permute-start(f32[24,128]{1,0:T(8,128)S(1)} %pad_maximum_fusion.6), channel_id=1, source_target_pairs={{0,28},{4,0},{8,4},{12,8},{16,12},{20,16},{24,20},{28,24},{1,29},{... | collective-permute-start | bytes 36872 | tf_op jit(solution)/shard_map/ppermute | solution.py:27
  77.9 1.2 %collective-permute-start.24 = (f32[24,128]{1,0:T(8,128)S(1)}, f32[24,128]{1,0:T(8,128)S(1)}, u32[]{:S(2)}, u32[]{:S(2)}) collective-permute-start(f32[24,128]{1,0:T(8,128)S(1)} %pad_maximum_fusion.6), channel_id=1, source_target_pairs={{0,4},{4,8},{8,12},{12,16},{16,20},{20,24},{24,28},{28,0},{1,5},{5... | collective-permute-start | bytes 36872 | tf_op jit(solution)/shard_map/ppermute | solution.py:27
  83.5 2.6 %collective-permute-start.26 = (f32[16,256]{1,0:T(8,128)S(1)}, f32[16,256]{1,0:T(8,128)S(1)}, u32[]{:S(2)}, u32[]{:S(2)}) collective-permute-start(f32[16,256]{1,0:T(8,128)S(1)} %get-tuple-element.37), channel_id=1, source_target_pairs={{0,3},{1,0},{2,1},{3,2},{4,7},{5,4},{6,5},{7,6},{8,11},{9,8},{10,9... | collective-permute-start | bytes 49160 | tf_op jit(solution)/shard_map/ppermute | solution.py:27
  83.5 3.9 %collective-permute-start.27 = (f32[16,256]{1,0:T(8,128)S(1)}, f32[16,256]{1,0:T(8,128)S(1)}, u32[]{:S(2)}, u32[]{:S(2)}) collective-permute-start(f32[16,256]{1,0:T(8,128)S(1)} %get-tuple-element.38), channel_id=1, source_target_pairs={{0,1},{1,2},{2,3},{3,0},{4,5},{5,6},{6,7},{7,4},{8,9},{9,10},{10,1... | collective-permute-start | bytes 49160 | tf_op jit(solution)/shard_map/ppermute | solution.py:27

commit v2 on v1

--- a/solution.py
+++ b/solution.py
@@ -50,42 +50,121 @@
     return jnp.where(near, inner, jnp.where(far, outer, 0.0))
 
 
-def assemble_kernel(own, below_x, above_x, below_y, above_y, main, low, high):
-    main[...] = jnp.ones(main.shape, F32)
+def pack_kernel(
+    density_in, base_in, cells_in, offsets_in, target_in, stiffness_in, counts, fields, marks, aux, upward, downward,
+    density, base, cells, offsets, target, stiffness, arrived,
+):
+    sources = (density_in, base_in, cells_in, offsets_in, target_in, stiffness_in)
+    places = (density, base, cells, offsets, target, stiffness)
+    copies = [pltpu.make_async_copy(a, b, arrived.at[i]) for i, (a, b) in enumerate(zip(sources, places))]
+    for copy in copies:
+        copy.start()
+    for copy in copies:
+        copy.wait()
+    for plane in range(8):
+        for field in range(4):
+            piece = density[plane] if field == 3 else base[field, plane]
+            fields[(field * 8 + plane) * 8 : (field * 8 + plane) * 8 + 8, :] = piece
+            row = (field * 8 + plane) * 2
+            upward[row : row + 2, :] = piece[6:8]
+            row = (field * 8 + plane) * 3
+            downward[row : row + 3, :] = piece[0:3]
+    lane = lax.broadcasted_iota(jnp.int32, (1, 128), 1)
+    marks[12:16, :] = jnp.zeros((4, 128), F32)
+    for group in range(3):
+        aux[8 * group + 6 : 8 * group + 8, :] = jnp.zeros((2, 128), F32)
+    for half in range(2):
+        place = slice(half * 128, half * 128 + 128)
+        live = jnp.where(lane + half * 128 < counts[0], 1.0, 0.0).astype(F32)
+        for k in range(3):
+            inside = cells[k : k + 1, place] & (7, 7, 127)[k]
+            row = 2 * k + half
+            marks[row : row + 1, :] = inside.astype(F32)
+            marks[row + 6 : row + 7, :] = offsets[k : k + 1, place]
+            aux[row : row + 1, :] = live
+            aux[row + 8 : row + 9, :] = stiffness[0:1, place]
+            aux[row + 16 : row + 17, :] = target[k : k + 1, place]
+    upward[64:80, :] = marks[...]
+    downward[96:112, :] = marks[...]
+
+
+def deepen_kernel(fields, marks, below, above, deep, three, upward, downward):
     for field in range(4):
-        for plane in range(PLANES):
-            row = field * ROWS + plane * YPAD
-            if plane < 2:
-                piece = below_x[field, plane]
-            elif plane < 10:
-                piece = own[field, plane - 2]
-            else:
-                piece = above_x[field, plane - 10]
-            main[row + 2 : row + 10, :] = piece
-            main[row : row + 2, :] = below_y[field, plane]
-            main[row + 10 : row + 13, :] = above_y[field, plane]
+        for plane in range(8):
+            at = field * 8 + plane
+            row = at * YPAD
+            deep[row : row + 2, :] = below[at * 2 : at * 2 + 2, :]
+            deep[row + 2 : row + 10, :] = fields[at * 8 : at * 8 + 8, :]
+            deep[row + 10 : row + 13, :] = above[at * 3 : at * 3 + 3, :]
+            deep[row + 13 : row + 16, :] = jnp.ones((3, 128), F32)
+    for field in range(4):
+        upward[field * 32 : field * 32 + 32, :] = deep[field * 128 + 96 : field * 128 + 128, :]
+        downward[field * 48 : field * 48 + 48, :] = deep[field * 128 : field * 128 + 48, :]
+    three[0:16, :] = marks[...]
+    three[16:32, :] = below[64:80, :]
+    three[32:48, :] = above[96:112, :]
+    upward[128:176, :] = three[...]
+    downward[192:240, :] = three[...]
+
+
+def assemble_kernel(deep, below, above, main, low, high):
+    for field in range(4):
+        row = field * ROWS
+        main[row : row + 32, :] = below[field * 32 : field * 32 + 32, :]
+        main[row + 32 : row + 160, :] = deep[field * 128 : field * 128 + 128, :]
+        main[row + 160 : row + 208, :] = above[field * 48 : field * 48 + 48, :]
+    main[4 * ROWS : 896, :] = jnp.ones((896 - 4 * ROWS, 128), F32)
     for block in range(7):
         turned = main[block * 128 : block * 128 + 128, :].T
         low[:, block * 128 : block * 128 + 128] = turned[0:8]
         high[:, block * 128 : block * 128 + 128] = turned[120:128]
 
 
-def tables_kernel(own, below_x, above_x, below_y, above_y, plane_weights, z_high, z_low):
-    pieces = [(own, 0, 0.0, 0.0), (below_x, 0, -8.0, 0.0), (above_x, 0, 8.0, 0.0)]
-    for group, along_y in ((below_y, -8.0), (above_y, 8.0)):
-        for part, along_x in enumerate((0.0, -8.0, 8.0)):
-            pieces.append((group, 16 * part, along_x, along_y))
-    for block, (ref, first, along_x, along_y) in enumerate(pieces):
-        for half in range(2):
-            row = lambda k: ref[first + 2 * k + half : first + 2 * k + half + 1, :]
-            place = slice(block * 256 + half * 128, block * 256 + half * 128 + 128)
-            plane_weights[0:16, place] = delta_rows(16, row(0) + (along_x + 2.0), row(3))
-            plane_weights[16:32, place] = delta_rows(16, row(1) + (along_y + 2.0), row(4))
-            high, rest = halves(delta_rows(144, row(2) + 2.0, row(5)))
-            z_high[0:144, place] = high
-            z_low[0:144, place] = rest
+def tables_kernel(three, below, above, plane_weights, z_high, z_low):
+    for group, (ref, first, along_x) in enumerate(((three, 0, 0.0), (below, 128, -8.0), (above, 192, 8.0))):
+        for part, along_y in enumerate((0.0, -8.0, 8.0)):
+            for half in range(2):
+                top = first + 16 * part + half
+                row = lambda k: ref[top + 2 * k : top + 2 * k + 1, :]
+                start = (3 * group + part) * 256 + half * 128
+                place = slice(start, start + 128)
+                plane_weights[0:16, place] = delta_rows(16, row(0) + (along_x + 2.0), row(3))
+                plane_weights[16:32, place] = delta_rows(16, row(1) + (along_y + 2.0), row(4))
+                high, rest = halves(delta_rows(144, row(2) + 2.0, row(5)))
+                z_high[0:144, place] = high
+                z_low[0:144, place] = rest
     z_high[144:256, :] = jnp.zeros((112, COLS), BF16)
     z_low[144:256, :] = jnp.zeros((112, COLS), BF16)
+
+
+def fill_left(group, refs, planes, plane_weights, left_high, left_low):
+    for part, (ref, first) in enumerate(refs):
+        for half in range(2):
+            column = part * 256 + half * 128
+            place = slice(column, column + 128)
+            weight = slice(group * 768 + column, group * 768 + column + 128)
+            along_y = plane_weights[16:32, weight]
+            vector = [ref[first + 2 * c + half : first + 2 * c + half + 1, :] * along_y for c in range(3)]
+            for at, plane in enumerate(planes):
+                along_x = plane_weights[plane : plane + 1, weight]
+                for c in range(3):
+                    top, rest = halves(vector[c] * along_x)
+                    row = (c * len(planes) + at) * YPAD
+                    left_high[row : row + YPAD, place] = top
+                    left_low[row : row + YPAD, place] = rest
+
+
+def spread_group(group, left_high, left_low, z_high, z_low):
+    columns = slice(group * 768, group * 768 + 768)
+    high = left_high[...]
+    total = transposed_dot(high, z_high[:, columns]) + transposed_dot(left_low[...], z_high[:, columns])
+    return total + transposed_dot(high, z_low[:, columns])
+
+
+def own_spread_kernel(own, below, above, plane_weights, z_high, z_low, moved, left_high, left_low):
+    refs = [(own, 0), (below, 0), (above, 0)]
+    fill_left(0, refs, range(1, 12), plane_weights, left_high, left_low)
+    moved[...] = spread_group(0, left_high, left_low, z_high, z_low)
 
 
 def interpolated(velocity, plane_weights, z_high, z_low):
@@ -119,28 +198,25 @@
 
 
 def spread_kernel(
-    own, below_x, above_x, below_y, above_y, plane_weights, z_high, z_low, scale, velocity, low, high, left_high, left_low, field, edges
+    moved, below, above, plane_weights, z_high, z_low, scale, velocity, low, high, b_high, b_low, a_high, a_low, field, edges
 ):
-    pieces = [(own, 0), (below_x, 0), (above_x, 0)]
-    pieces += [(below_y, 8 * part) for part in range(3)] + [(above_y, 8 * part) for part in range(3)]
-    for block, (ref, first) in enumerate(pieces):
-        for half in range(2):
-            place = slice(block * 256 + half * 128, block * 256 + half * 128 + 128)
-            along_y = plane_weights[16:32, place]
-            vector = [ref[first + 2 * c + half : first + 2 * c + half + 1, :] * along_y for c in range(3)]
-            for plane in range(PLANES):
-                along_x = plane_weights[plane : plane + 1, place]
-                for c in range(3):
-                    top, rest = halves(vector[c] * along_x)
-                    row = c * ROWS + plane * YPAD
-                    left_high[row : row + YPAD, place] = top
-                    left_low[row : row + YPAD, place] = rest
+    fill_left(1, [(below, 8 * part) for part in range(3)], range(0, 4), plane_weights, b_high, b_low)
+    fill_left(2, [(above, 8 * part) for part in range(3)], range(9, 13), plane_weights, a_high, a_low)
+    first = spread_group(1, b_high, b_low, z_high, z_low)
+    final = spread_group(2, a_high, a_low, z_high, z_low)
     for c in range(3):
-        rows = slice(c * ROWS, c * ROWS + ROWS)
-        moved = transposed_dot(left_high[rows, :], z_high[...])
-        moved += transposed_dot(left_low[rows, :], z_high[...])
-        moved += transposed_dot(left_high[rows, :], z_low[...])
-        field[rows, :] = moved * scale[...]
+        for plane in range(PLANES):
+            parts = []
+            if 1 <= plane <= 11:
+                row = c * INNER + (plane - 1) * YPAD
+                parts.append(moved[row : row + YPAD, :])
+            if plane < 4:
+                parts.append(first[c * 64 + plane * YPAD : c * 64 + plane * YPAD + YPAD])
+            if plane >= 9:
+                parts.append(final[c * 64 + (plane - 9) * YPAD : c * 64 + (plane - 9) * YPAD + YPAD])
+            total = parts[0] if len(parts) == 1 else parts[0] + parts[1]
+            row = c * ROWS + plane * YPAD
+            field[row : row + YPAD, :] = total * scale[plane * YPAD : plane * YPAD + YPAD, :]
     axial, diagonal = 1.0 / 6.0, 1.0 / 12.0
     up_y = lambda a: pltpu.roll(a, 1, 0)
     down_y = lambda a: pltpu.roll(a, YPAD - 1, 0)
@@ -336,13 +412,13 @@
         forces[c : c + 1, 128:256] = total[2 * c + 1 : 2 * c + 2, :]
 
 
-def call(kernel, name, outs, *operands, scratch=()):
+def call(kernel, name, outs, *operands, specs=None, scratch=()):
     whole = pl.BlockSpec(memory_space=pltpu.VMEM)
     return pl.pallas_call(
         kernel,
         name=name,
         out_shape=[jax.ShapeDtypeStruct(shape, kind) for shape, kind in outs],
-        in_specs=[whole] * len(operands),
+        in_specs=[whole] * len(operands) if specs is None else specs,
         out_specs=[whole] * len(outs),
         scratch_shapes=list(scratch),
         compiler_params=PARAMS,
@@ -350,36 +426,31 @@
 
 
 def body(density, base_velocity, cells, offsets, target, stiffness, counts):
-    anchor = jnp.stack([lax.axis_index("gx") * 8, lax.axis_index(GY) * 8, lax.axis_index("gz") * 128])
-    local = (cells - anchor[:, None]).astype(F32)
-    lines = lambda a: a.reshape(-1, 128)
-    zeros = lambda n: jnp.zeros((n, 128), F32)
-    markers = jnp.concatenate([lines(local), lines(offsets), zeros(4)], axis=0)
-    live = lines((jnp.arange(MARKERS, dtype=jnp.int32) < counts[0]).astype(F32))
-    stiff = lines(stiffness)
-    aux = jnp.concatenate(
-        [live, live, live, zeros(2), stiff, stiff, stiff, zeros(2), lines(target), zeros(2)], axis=0
-    )
-    fields = jnp.concatenate([base_velocity, density[None]], axis=0)
-
-    below_x = shifted(fields[:, 6:8], "gx", 1)
-    above_x = shifted(fields[:, 0:3], "gx", -1)
-    marks_below_x, marks_above_x = shifted(markers, "gx", 1), shifted(markers, "gx", -1)
-    deep = jnp.concatenate([below_x, fields, above_x], axis=1)
-    below_y = shifted(deep[:, :, 6:8], GY, 1)
-    above_y = shifted(deep[:, :, 0:3], GY, -1)
-    marks = jnp.concatenate([markers, marks_below_x, marks_above_x], axis=0)
-    marks_below_y, marks_above_y = shifted(marks, GY, 1), shifted(marks, GY, -1)
+    fields, marks, aux, upward, downward = call(
+        pack_kernel, "pack",
+        [((256, 128), F32), ((16, 128), F32), ((24, 128), F32), ((80, 128), F32), ((112, 128), F32)],
+        *(pltpu.with_memory_space_constraint(a, pltpu.HBM) for a in (density, base_velocity, cells, offsets, target, stiffness.reshape(1, MARKERS))), counts,
+        specs=[pl.BlockSpec(memory_space=pltpu.HBM)] * 6 + [pl.BlockSpec(memory_space=pltpu.SMEM)],
+        scratch=[
+            pltpu.VMEM((8, 8, 128), F32), pltpu.VMEM((3, 8, 8, 128), F32), pltpu.VMEM((3, MARKERS), jnp.int32),
+            pltpu.VMEM((3, MARKERS), F32), pltpu.VMEM((3, MARKERS), F32), pltpu.VMEM((1, MARKERS), F32),
+            pltpu.SemaphoreType.DMA((6,)),
+        ],
+    )
+    below, above = shifted(upward, GY, 1), shifted(downward, GY, -1)
+    deep, three, upward, downward = call(
+        deepen_kernel, "deepen",
+        [((512, 128), F32), ((48, 128), F32), ((176, 128), F32), ((240, 128), F32)],
+        fields, marks, below, above,
+    )
+    below, above = shifted(upward, "gx", 1), shifted(downward, "gx", -1)
     main, low, high = call(
-        assemble_kernel, "assemble", [((896, 128), F32), ((8, 896), F32), ((8, 896), F32)],
-        fields, below_x, above_x, below_y, above_y,
-    )
+        assemble_kernel, "assemble", [((896, 128), F32), ((8, 896), F32), ((8, 896), F32)], deep, below, above
+    )
+    from_above, from_below = shifted(low, "gz", -1), shifted(high, "gz", 1)
     plane_weights, z_high, z_low = call(
-        tables_kernel, "tables", [((32, COLS), F32), ((256, COLS), BF16), ((256, COLS), BF16)],
-        markers, marks_below_x, marks_above_x, marks_below_y, marks_above_y,
-    )
-    from_above = shifted(low, "gz", -1)
-    from_below = shifted(high, "gz", 1)
+        tables_kernel, "tables", [((32, COLS), F32), ((256, COLS), BF16), ((256, COLS), BF16)], three, below, above
+    )
     tables = (plane_weights, z_high, z_low)
     scale, start = call(
         setup_kernel, "setup", [((ROWS, LANES), F32), ((8, 128), F32)],
@@ -388,16 +459,17 @@
     )
 
     def spread(vector):
-        below, above = shifted(vector, "gx", 1), shifted(vector, "gx", -1)
+        below, above = shifted(vector, GY, 1), shifted(vector, GY, -1)
         three = jnp.concatenate([vector, below, above], axis=0)
-        below_three, above_three = shifted(three, GY, 1), shifted(three, GY, -1)
+        below_three, above_three = shifted(three, "gx", 1), shifted(three, "gx", -1)
+        (moved,) = call(
+            own_spread_kernel, "own_spread", [((3 * INNER, LANES), F32)], vector, below, above, *tables,
+            scratch=[pltpu.VMEM((3 * INNER, 768), BF16)] * 2,
+        )
         velocity, low, high = call(
             spread_kernel, "spread", [((3 * INNER, LANES), F32), ((16, 256), F32), ((16, 256), F32)],
-            vector, below, above, below_three, above_three, *tables, scale,
-            scratch=[
-                pltpu.VMEM((3 * ROWS, COLS), BF16), pltpu.VMEM((3 * ROWS, COLS), BF16),
-                pltpu.VMEM((3 * ROWS, LANES), F32), pltpu.VMEM((256, 128), F32),
-            ],
+            moved, below_three, above_three, *tables, scale,
+            scratch=[pltpu.VMEM((192, 768), BF16)] * 4 + [pltpu.VMEM((3 * ROWS, LANES), F32), pltpu.VMEM((256, 128), F32)],
         )
         return velocity, shifted(low, "gz", -1), shifted(high, "gz", 1)
 

time: 114 us -> 102 us (0.89)
  other arithmetic: 5.19 us -> 0.01 us
  Pallas kernels: 20 us -> 15.4 us
  starting transfers between devices: 42 us -> 39.2 us
  waiting for transfers between devices: 21 us -> 22.6 us
    pallas_call x10 -> x15, Pallas kernels: 20 us -> 15.4 us  [call(): pl.pallas_call(kernel, name=name, out_shape=[jax.ShapeDtypeStruct(shape,...]
    concatenate x5 -> x0, other arithmetic: 3.41 us -> none  [the longest x3 2.47 us: body(): fields = jnp.concatenate([base_velocity, density[None]], axis=0)]
    ppermute x28 -> x24, starting transfers between devices: 42 us -> 39.2 us  [shifted(): lax.ppermute(shard, axis, [(i, (i + by) % length) for i in range(length)])]
    ppermute x28 -> x24, waiting for transfers between devices: 21 us -> 22.6 us  [shifted(): lax.ppermute(shard, axis, [(i, (i + by) % length) for i in range(length)])]
  transfers between devices with their start and end apart: 28 -> 24, of which waited for: 19 -> 21; matrix products, arithmetic and copies ran while one was open for 5% -> 0% of each run, Pallas kernels for 2% -> 5%
where the time goes in v2:
time: 102 us
  starting transfers between devices  39.2 us (38%)
  blocking collectives  23.4 us (23%)
  waiting for transfers between devices  22.6 us (22%)
  Pallas kernels  15.4 us (15%)
    ppermute x24, starting transfers between devices, shifted(): lax.ppermute(shard, axis, [(i, (i + by) % length) for i in range(length)])  39.2 us
    all_to_all x1, blocking collectives, body(): gathered = lax.all_to_all(sums, GX_GY_GZ, 0, 0, tiled=True)  23.4 us
    ppermute x24, waiting for transfers between devices, shifted(): lax.ppermute(shard, axis, [(i, (i + by) % length) for i in range(length)])  22.6 us
    pallas_call x15, Pallas kernels, call(): pl.pallas_call(kernel, name=name, out_shape=[jax.ShapeDtypeStruct(shape,...  15.4 us
  transfers between devices with their start and end apart: 24, of which 21 were waited for; matrix products, arithmetic and copies ran while one was open for 0% of the time, Pallas kernels for 5%

profile of v2, /device:TPU:1, one launch (start us, length us, event | category | flops | bytes accessed | tf_op | source)
XLA Modules:
  0.0 101.5 jit_solution(17435119886998013852)
XLA Ops:
  1.7 3.2 %collective-permute-start.1 = (f32[112,128]{1,0:T(8,128)S(1)}, f32[112,128]{1,0:T(8,128)S(1)}, u32[]{:S(2)}, u32[]{:S(2)}) collective-permute-start(f32[112,128]{1,0:T(8,128)S(1)} %get-tuple-element.34), channel_id=1, source_target_pairs={{0,28},{4,0},{8,4},{12,8},{16,12},{20,16},{24,20},{28,24},{1,29},{... | collective-permute-start | bytes 172040 | tf_op jit(solution)/shard_map/ppermute | solution.py:27
  4.9 1.5 %collective-permute-done.below = f32[80,128]{1,0:T(8,128)S(1)} collective-permute-done((f32[80,128]{1,0:T(8,128)S(1)}, f32[80,128]{1,0:T(8,128)S(1)}, u32[]{:S(2)}, u32[]{:S(2)}) %collective-permute-start) | collective-permute-done | bytes 40992 | tf_op jit(solution)/shard_map/ppermute | solution.py:27
  6.4 5.7 %collective-permute-start.3 = (f32[240,128]{1,0:T(8,128)S(1)}, f32[240,128]{1,0:T(8,128)S(1)}, u32[]{:S(2)}, u32[]{:S(2)}) collective-permute-start(f32[240,128]{1,0:T(8,128)S(1)} %get-tuple-element.37), channel_id=1, source_target_pairs={{0,224},{32,0},{64,32},{96,64},{128,96},{160,128},{192,160},{224,1... | collective-permute-start | bytes 368648 | tf_op jit(solution)/shard_map/ppermute | solution.py:27
  12.1 4.6 %collective-permute-done.2.below = f32[176,128]{1,0:T(8,128)S(1)} collective-permute-done((f32[176,128]{1,0:T(8,128)S(1)}, f32[176,128]{1,0:T(8,128)S(1)}, u32[]{:S(2)}, u32[]{:S(2)}) %collective-permute-start.2) | collective-permute-done | bytes 90144 | tf_op jit(solution)/shard_map/ppermute | solution.py:27
  16.8 2.6 %collective-permute-start.4 = (f32[8,896]{1,0:T(8,128)S(1)}, f32[8,896]{1,0:T(8,128)S(1)}, u32[]{:S(2)}, u32[]{:S(2)}) collective-permute-start(f32[8,896]{1,0:T(8,128)S(1)} %get-tuple-element.39), channel_id=1, source_target_pairs={{0,3},{1,0},{2,1},{3,2},{4,7},{5,4},{6,5},{7,6},{8,11},{9,8},{10,9... | collective-permute-start | bytes 86024 | tf_op jit(solution)/shard_map/ppermute | solution.py:27
  19.4 2.3 %tables.1 = (f32[32,2304]{1,0:T(8,128)S(1)}, bf16[256,2304]{1,0:T(8,128)(2,1)S(1)}, bf16[256,2304]{1,0:T(8,128)(2,1)S(1)}) custom-call(f32[48,128]{1,0:T(8,128)S(1)} %get-tuple-element.41.three, f32[176,128]{1,0:T(8,128)S(1)} %collective-permute-done.2.below, f32[240,128]{1,0:T(8,128)S(1)} %collective-permute-done.3.above), custom_call_target="tpu_custom_call" | custom-call | tf_op jit(solution)/shard_map/tables/pallas_call | solution.py:417
  21.7 1.6 %collective-permute-done.5.high = f32[8,896]{1,0:T(8,128)S(1)} collective-permute-done((f32[8,896]{1,0:T(8,128)S(1)}, f32[8,896]{1,0:T(8,128)S(1)}, u32[]{:S(2)}, u32[]{:S(2)}) %collective-permute-start.5) | collective-permute-done | bytes 28704 | tf_op jit(solution)/shard_map/ppermute | solution.py:27
  23.9 4.3 %collective-permute-start.6 = (f32[8,128]{1,0:T(8,128)S(1)}, f32[8,128]{1,0:T(8,128)S(1)}, u32[]{:S(2)}, u32[]{:S(2)}) collective-permute-start(f32[8,128]{1,0:T(8,128)S(1)} %get-tuple-element.46.own.vector.first), channel_id=1, source_target_pairs={{0,4},{4,8},{8,12},{12,16},{16,20},{20,24},{24,28},{28,0},{1,5},{5... | collective-permute-start | bytes 12296 | tf_op jit(solution)/shard_map/ppermute | solution.py:27
  28.2 2.5 %collective-permute-start.7 = (f32[8,128]{1,0:T(8,128)S(1)}, f32[8,128]{1,0:T(8,128)S(1)}, u32[]{:S(2)}, u32[]{:S(2)}) collective-permute-start(f32[8,128]{1,0:T(8,128)S(1)} %get-tuple-element.46.own.vector.first), channel_id=1, source_target_pairs={{0,28},{4,0},{8,4},{12,8},{16,12},{20,16},{24,20},{28,24},{1,29},{... | collective-permute-start | bytes 12296 | tf_op jit(solution)/shard_map/ppermute | solution.py:27
  31.8 1.2 %collective-permute-start.8 = (f32[24,128]{1,0:T(8,128)S(1)}, f32[24,128]{1,0:T(8,128)S(1)}, u32[]{:S(2)}, u32[]{:S(2)}) collective-permute-start(f32[24,128]{1,0:T(8,128)S(1)} %constant_dynamic-update-slice_fusion), channel_id=1, source_target_pairs={{0,32},{32,64},{64,96},{96,128},{128,160},{160,192},{192,224},{224... | collective-permute-start | bytes 36872 | tf_op jit(solution)/shard_map/ppermute | solution.py:27
  34.4 1.2 %collective-permute-done.8.below = f32[24,128]{1,0:T(8,128)S(1)} collective-permute-done((f32[24,128]{1,0:T(8,128)S(1)}, f32[24,128]{1,0:T(8,128)S(1)}, u32[]{:S(2)}, u32[]{:S(2)}) %collective-permute-start.8) | collective-permute-done | bytes 12320 | tf_op jit(solution)/shard_map/ppermute | solution.py:27
  35.5 1.6 %spread.3 = (f32[528,256]{1,0:T(8,128)S(1)}, f32[16,256]{1,0:T(8,128)S(1)}, f32[16,256]{1,0:T(8,128)S(1)}) custom-call(f32[528,256]{1,0:T(8,128)S(1)} %own_spread.3.moved, f32[24,128]{1,0:T(8,128)S(1)} %collective-permute-done.8.below, f32[24,128]{1,0:T(8,128)S(1)} %collective-permute-done.9.above, f32[32,2304]{1,0:T(8,128)S(1)} %get-tuple-element.42.plane_weights, ...), custom_call_target="tpu_custom_call" | custom-call | tf_op jit(solution)/shard_map/spread/pallas_call | solution.py:417
  37.4 1.2 %collective-permute-start.11 = (f32[16,256]{1,0:T(8,128)S(1)}, f32[16,256]{1,0:T(8,128)S(1)}, u32[]{:S(2)}, u32[]{:S(2)}) collective-permute-start(f32[16,256]{1,0:T(8,128)S(1)} %get-tuple-element.50), channel_id=1, source_target_pairs={{0,1},{1,2},{2,3},{3,0},{4,5},{5,6},{6,7},{7,4},{8,9},{9,10},{10,1... | collective-permute-start | bytes 49160 | tf_op jit(solution)/shard_map/ppermute | solution.py:27
  38.7 1.2 %collective-permute-done.10.low = f32[16,256]{1,0:T(8,128)S(1)} collective-permute-done((f32[16,256]{1,0:T(8,128)S(1)}, f32[16,256]{1,0:T(8,128)S(1)}, u32[]{:S(2)}, u32[]{:S(2)}) %collective-permute-start.10) | collective-permute-done | bytes 16416 | tf_op jit(solution)/shard_map/ppermute | solution.py:27
  39.8 1.4 %collective-permute-done.11.high = f32[16,256]{1,0:T(8,128)S(1)} collective-permute-done((f32[16,256]{1,0:T(8,128)S(1)}, f32[16,256]{1,0:T(8,128)S(1)}, u32[]{:S(2)}, u32[]{:S(2)}) %collective-permute-start.11) | collective-permute-done | bytes 16416 | tf_op jit(solution)/shard_map/ppermute | solution.py:27
  41.9 6.2 %collective-permute-start.13 = (f32[8,128]{1,0:T(8,128)S(1)}, f32[8,128]{1,0:T(8,128)S(1)}, u32[]{:S(2)}, u32[]{:S(2)}) collective-permute-start(f32[8,128]{1,0:T(8,128)S(1)} %image.2.own.vector.second), channel_id=1, source_target_pairs={{0,28},{4,0},{8,4},{12,8},{16,12},{20,16},{24,20},{28,24},{1,29},{... | collective-permute-start | bytes 12296 | tf_op jit(solution)/shard_map/ppermute | solution.py:27
  49.2 1.5 %collective-permute-start.14 = (f32[24,128]{1,0:T(8,128)S(1)}, f32[24,128]{1,0:T(8,128)S(1)}, u32[]{:S(2)}, u32[]{:S(2)}) collective-permute-start(f32[24,128]{1,0:T(8,128)S(1)} %pad_maximum_fusion), channel_id=1, source_target_pairs={{0,32},{32,64},{64,96},{96,128},{128,160},{160,192},{192,224},{224... | collective-permute-start | bytes 36872 | tf_op jit(solution)/shard_map/ppermute | solution.py:27
  51.9 1.1 %collective-permute-done.14.below = f32[24,128]{1,0:T(8,128)S(1)} collective-permute-done((f32[24,128]{1,0:T(8,128)S(1)}, f32[24,128]{1,0:T(8,128)S(1)}, u32[]{:S(2)}, u32[]{:S(2)}) %collective-permute-start.14) | collective-permute-done | bytes 12320 | tf_op jit(solution)/shard_map/ppermute | solution.py:27
  53.0 1.6 %spread.4 = (f32[528,256]{1,0:T(8,128)S(1)}, f32[16,256]{1,0:T(8,128)S(1)}, f32[16,256]{1,0:T(8,128)S(1)}) custom-call(f32[528,256]{1,0:T(8,128)S(1)} %own_spread.4.moved, f32[24,128]{1,0:T(8,128)S(1)} %collective-permute-done.14.below, f32[24,128]{1,0:T(8,128)S(1)} %collective-permute-done.15.above, f32[32,2304]{1,0:T(8,128)S(1)} %get-tuple-element.42.plane_weights, ...), custom_call_target="tpu_custom_call" | custom-call | tf_op jit(solution)/shard_map/spread/pallas_call | solution.py:417
  54.7 1.5 %collective-permute-start.17 = (f32[16,256]{1,0:T(8,128)S(1)}, f32[16,256]{1,0:T(8,128)S(1)}, u32[]{:S(2)}, u32[]{:S(2)}) collective-permute-start(f32[16,256]{1,0:T(8,128)S(1)} %get-tuple-element.53), channel_id=1, source_target_pairs={{0,1},{1,2},{2,3},{3,0},{4,5},{5,6},{6,7},{7,4},{8,9},{9,10},{10,1... | collective-permute-start | bytes 49160 | tf_op jit(solution)/shard_map/ppermute | solution.py:27
  56.1 1.1 %collective-permute-done.16.low = f32[16,256]{1,0:T(8,128)S(1)} collective-permute-done((f32[16,256]{1,0:T(8,128)S(1)}, f32[16,256]{1,0:T(8,128)S(1)}, u32[]{:S(2)}, u32[]{:S(2)}) %collective-permute-start.16) | collective-permute-done | bytes 16416 | tf_op jit(solution)/shard_map/ppermute | solution.py:27
  57.3 1.3 %collective-permute-done.17.high = f32[16,256]{1,0:T(8,128)S(1)} collective-permute-done((f32[16,256]{1,0:T(8,128)S(1)}, f32[16,256]{1,0:T(8,128)S(1)}, u32[]{:S(2)}, u32[]{:S(2)}) %collective-permute-start.17) | collective-permute-done | bytes 16416 | tf_op jit(solution)/shard_map/ppermute | solution.py:27
  59.2 5.9 %collective-permute-start.19 = (f32[8,128]{1,0:T(8,128)S(1)}, f32[8,128]{1,0:T(8,128)S(1)}, u32[]{:S(2)}, u32[]{:S(2)}) collective-permute-start(f32[8,128]{1,0:T(8,128)S(1)} %image.3.own.third), channel_id=1, source_target_pairs={{0,28},{4,0},{8,4},{12,8},{16,12},{20,16},{24,20},{28,24},{1,29},{... | collective-permute-start | bytes 12296 | tf_op jit(solution)/shard_map/ppermute | solution.py:27
  66.2 1.5 %collective-permute-start.20 = (f32[24,128]{1,0:T(8,128)S(1)}, f32[24,128]{1,0:T(8,128)S(1)}, u32[]{:S(2)}, u32[]{:S(2)}) collective-permute-start(f32[24,128]{1,0:T(8,128)S(1)} %pad_maximum_fusion.1), channel_id=1, source_target_pairs={{0,32},{32,64},{64,96},{96,128},{128,160},{160,192},{192,224},{224... | collective-permute-start | bytes 36872 | tf_op jit(solution)/shard_map/ppermute | solution.py:27
  68.9 1.1 %collective-permute-done.20.below = f32[24,128]{1,0:T(8,128)S(1)} collective-permute-done((f32[24,128]{1,0:T(8,128)S(1)}, f32[24,128]{1,0:T(8,128)S(1)}, u32[]{:S(2)}, u32[]{:S(2)}) %collective-permute-start.20) | collective-permute-done | bytes 12320 | tf_op jit(solution)/shard_map/ppermute | solution.py:27
  70.0 1.6 %spread.5 = (f32[528,256]{1,0:T(8,128)S(1)}, f32[16,256]{1,0:T(8,128)S(1)}, f32[16,256]{1,0:T(8,128)S(1)}) custom-call(f32[528,256]{1,0:T(8,128)S(1)} %own_spread.5.moved, f32[24,128]{1,0:T(8,128)S(1)} %collective-permute-done.20.below, f32[24,128]{1,0:T(8,128)S(1)} %collective-permute-done.21.above, f32[32,2304]{1,0:T(8,128)S(1)} %get-tuple-element.42.plane_weights, ...), custom_call_target="tpu_custom_call" | custom-call | tf_op jit(solution)/shard_map/spread/pallas_call | solution.py:417
  71.7 1.5 %collective-permute-start.23 = (f32[16,256]{1,0:T(8,128)S(1)}, f32[16,256]{1,0:T(8,128)S(1)}, u32[]{:S(2)}, u32[]{:S(2)}) collective-permute-start(f32[16,256]{1,0:T(8,128)S(1)} %get-tuple-element.56), channel_id=1, source_target_pairs={{0,1},{1,2},{2,3},{3,0},{4,5},{5,6},{6,7},{7,4},{8,9},{9,10},{10,1... | collective-permute-start | bytes 49160 | tf_op jit(solution)/shard_map/ppermute | solution.py:27
  73.2 1.1 %collective-permute-done.22.low = f32[16,256]{1,0:T(8,128)S(1)} collective-permute-done((f32[16,256]{1,0:T(8,128)S(1)}, f32[16,256]{1,0:T(8,128)S(1)}, u32[]{:S(2)}, u32[]{:S(2)}) %collective-permute-start.22) | collective-permute-done | bytes 16416 | tf_op jit(solution)/shard_map/ppermute | solution.py:27
  74.3 1.3 %collective-permute-done.23.high = f32[16,256]{1,0:T(8,128)S(1)} collective-permute-done((f32[16,256]{1,0:T(8,128)S(1)}, f32[16,256]{1,0:T(8,128)S(1)}, u32[]{:S(2)}, u32[]{:S(2)}) %collective-permute-start.23) | collective-permute-done | bytes 16416 | tf_op jit(solution)/shard_map/ppermute | solution.py:27
  75.6 1.2 %last.1 = f32[256,128]{1,0:T(8,128)S(1)} custom-call(f32[528,256]{1,0:T(8,128)S(1)} %get-tuple-element.54.velocity, f32[16,256]{1,0:T(8,128)S(1)} %collective-permute-done.22.low, f32[16,256]{1,0:T(8,128)S(1)} %collective-permute-done.23.high, f32[32,2304]{1,0:T(8,128)S(1)} %get-tuple-element.42.plane_weights, ...), custom_call_target="tpu_custom_call" | custom-call | tf_op jit(solution)/shard_map/last/pallas_call | solution.py:417
  76.8 23.4 %all_to_all.11 = f32[256,1,128]{2,1,0:T(1,128)S(1)} all-to-all(f32[256,1,128]{2,1,0:T(1,128)S(1)} %bitcast.5), channel_id=1, replica_groups=mesh['gx'=8,'gy_0'=4,'gy_1'=2,'gz'=4] {'gx','gy_0','gy_1','gz'}, dimensions={0} | all-to-all | bytes 262144 | tf_op jit(solution)/shard_map/all_to_all | solution.py:487
  100.2 1.3 %finish.1 = f32[3,256]{1,0:T(4,128)} custom-call(f32[256,128]{1,0:T(8,128)S(1)} %bitcast.6, f32[8,128]{1,0:T(8,128)S(1)} %get-tuple-element.46.own.vector.first, f32[8,128]{1,0:T(8,128)S(1)} %image.2.own.vector.second, f32[8,128]{1,0:T(8,128)S(1)} %image.3.own.third), custom_call_target="tpu_custom_call" | custom-call | tf_op jit(solution)/shard_map/finish/pallas_call | solution.py:417
  (37 shorter events, 10.7 us)
Async XLA Ops:
  1.7 4.7 %collective-permute-start.1 = (f32[112,128]{1,0:T(8,128)S(1)}, f32[112,128]{1,0:T(8,128)S(1)}, u32[]{:S(2)}, u32[]{:S(2)}) collective-permute-start(f32[112,128]{1,0:T(8,128)S(1)} %get-tuple-element.34), channel_id=1, source_target_pairs={{0,28},{4,0},{8,4},{12,8},{16,12},{20,16},{24,20},{28,24},{1,29},{... | collective-permute-start | bytes 172040 | tf_op jit(solution)/shard_map/ppermute | solution.py:27
  4.9 1.5 %collective-permute-start = (f32[80,128]{1,0:T(8,128)S(1)}, f32[80,128]{1,0:T(8,128)S(1)}, u32[]{:S(2)}, u32[]{:S(2)}) collective-permute-start(f32[80,128]{1,0:T(8,128)S(1)} %get-tuple-element.33), channel_id=1, source_target_pairs={{0,4},{4,8},{8,12},{12,16},{16,20},{20,24},{24,28},{28,0},{1,5},{5... | collective-permute-start | bytes 122888 | tf_op jit(solution)/shard_map/ppermute | solution.py:27
  6.4 10.2 %collective-permute-start.3 = (f32[240,128]{1,0:T(8,128)S(1)}, f32[240,128]{1,0:T(8,128)S(1)}, u32[]{:S(2)}, u32[]{:S(2)}) collective-permute-start(f32[240,128]{1,0:T(8,128)S(1)} %get-tuple-element.37), channel_id=1, source_target_pairs={{0,224},{32,0},{64,32},{96,64},{128,96},{160,128},{192,160},{224,1... | collective-permute-start | bytes 368648 | tf_op jit(solution)/shard_map/ppermute | solution.py:27
  12.1 4.6 %collective-permute-start.2 = (f32[176,128]{1,0:T(8,128)S(1)}, f32[176,128]{1,0:T(8,128)S(1)}, u32[]{:S(2)}, u32[]{:S(2)}) collective-permute-start(f32[176,128]{1,0:T(8,128)S(1)} %get-tuple-element.36), channel_id=1, source_target_pairs={{0,32},{32,64},{64,96},{96,128},{128,160},{160,192},{192,224},{224... | collective-permute-start | bytes 270344 | tf_op jit(solution)/shard_map/ppermute | solution.py:27
  16.8 4.9 %collective-permute-start.4 = (f32[8,896]{1,0:T(8,128)S(1)}, f32[8,896]{1,0:T(8,128)S(1)}, u32[]{:S(2)}, u32[]{:S(2)}) collective-permute-start(f32[8,896]{1,0:T(8,128)S(1)} %get-tuple-element.39), channel_id=1, source_target_pairs={{0,3},{1,0},{2,1},{3,2},{4,7},{5,4},{6,5},{7,6},{8,11},{9,8},{10,9... | collective-permute-start | bytes 86024 | tf_op jit(solution)/shard_map/ppermute | solution.py:27
  19.4 3.9 %collective-permute-start.5 = (f32[8,896]{1,0:T(8,128)S(1)}, f32[8,896]{1,0:T(8,128)S(1)}, u32[]{:S(2)}, u32[]{:S(2)}) collective-permute-start(f32[8,896]{1,0:T(8,128)S(1)} %get-tuple-element.40), channel_id=1, source_target_pairs={{0,1},{1,2},{2,3},{3,0},{4,5},{5,6},{6,7},{7,4},{8,9},{9,10},{10,1... | collective-permute-start | bytes 86024 | tf_op jit(solution)/shard_map/ppermute | solution.py:27
  23.9 7.5 %collective-permute-start.6 = (f32[8,128]{1,0:T(8,128)S(1)}, f32[8,128]{1,0:T(8,128)S(1)}, u32[]{:S(2)}, u32[]{:S(2)}) collective-permute-start(f32[8,128]{1,0:T(8,128)S(1)} %get-tuple-element.46.own.vector.first), channel_id=1, source_target_pairs={{0,4},{4,8},{8,12},{12,16},{16,20},{20,24},{24,28},{28,0},{1,5},{5... | collective-permute-start | bytes 12296 | tf_op jit(solution)/shard_map/ppermute | solution.py:27
  28.2 3.3 %collective-permute-start.7 = (f32[8,128]{1,0:T(8,128)S(1)}, f32[8,128]{1,0:T(8,128)S(1)}, u32[]{:S(2)}, u32[]{:S(2)}) collective-permute-start(f32[8,128]{1,0:T(8,128)S(1)} %get-tuple-element.46.own.vector.first), channel_id=1, source_target_pairs={{0,28},{4,0},{8,4},{12,8},{16,12},{20,16},{24,20},{28,24},{1,29},{... | collective-permute-start | bytes 12296 | tf_op jit(solution)/shard_map/ppermute | solution.py:27
  31.5 2.8 %collective-permute-start.9 = (f32[24,128]{1,0:T(8,128)S(1)}, f32[24,128]{1,0:T(8,128)S(1)}, u32[]{:S(2)}, u32[]{:S(2)}) collective-permute-start(f32[24,128]{1,0:T(8,128)S(1)} %constant_dynamic-update-slice_fusion), channel_id=1, source_target_pairs={{0,224},{32,0},{64,32},{96,64},{128,96},{160,128},{192,160},{224,1... | collective-permute-start | bytes 36872 | tf_op jit(solution)/shard_map/ppermute | solution.py:27
  31.8 3.8 %collective-permute-start.8 = (f32[24,128]{1,0:T(8,128)S(1)}, f32[24,128]{1,0:T(8,128)S(1)}, u32[]{:S(2)}, u32[]{:S(2)}) collective-permute-start(f32[24,128]{1,0:T(8,128)S(1)} %constant_dynamic-update-slice_fusion), channel_id=1, source_target_pairs={{0,32},{32,64},{64,96},{96,128},{128,160},{160,192},{192,224},{224... | collective-permute-start | bytes 36872 | tf_op jit(solution)/shard_map/ppermute | solution.py:27
  37.2 2.7 %collective-permute-start.10 = (f32[16,256]{1,0:T(8,128)S(1)}, f32[16,256]{1,0:T(8,128)S(1)}, u32[]{:S(2)}, u32[]{:S(2)}) collective-permute-start(f32[16,256]{1,0:T(8,128)S(1)} %get-tuple-element.49), channel_id=1, source_target_pairs={{0,3},{1,0},{2,1},{3,2},{4,7},{5,4},{6,5},{7,6},{8,11},{9,8},{10,9... | collective-permute-start | bytes 49160 | tf_op jit(solution)/shard_map/ppermute | solution.py:27
  37.4 3.8 %collective-permute-start.11 = (f32[16,256]{1,0:T(8,128)S(1)}, f32[16,256]{1,0:T(8,128)S(1)}, u32[]{:S(2)}, u32[]{:S(2)}) collective-permute-start(f32[16,256]{1,0:T(8,128)S(1)} %get-tuple-element.50), channel_id=1, source_target_pairs={{0,1},{1,2},{2,3},{3,0},{4,5},{5,6},{6,7},{7,4},{8,9},{9,10},{10,1... | collective-permute-start | bytes 49160 | tf_op jit(solution)/shard_map/ppermute | solution.py:27
  41.9 7.0 %collective-permute-start.13 = (f32[8,128]{1,0:T(8,128)S(1)}, f32[8,128]{1,0:T(8,128)S(1)}, u32[]{:S(2)}, u32[]{:S(2)}) collective-permute-start(f32[8,128]{1,0:T(8,128)S(1)} %image.2.own.vector.second), channel_id=1, source_target_pairs={{0,28},{4,0},{8,4},{12,8},{16,12},{20,16},{24,20},{28,24},{1,29},{... | collective-permute-start | bytes 12296 | tf_op jit(solution)/shard_map/ppermute | solution.py:27
  48.1 1.2 %collective-permute-start.12 = (f32[8,128]{1,0:T(8,128)S(1)}, f32[8,128]{1,0:T(8,128)S(1)}, u32[]{:S(2)}, u32[]{:S(2)}) collective-permute-start(f32[8,128]{1,0:T(8,128)S(1)} %image.2.own.vector.second), channel_id=1, source_target_pairs={{0,4},{4,8},{8,12},{12,16},{16,20},{20,24},{24,28},{28,0},{1,5},{5... | collective-permute-start | bytes 12296 | tf_op jit(solution)/shard_map/ppermute | solution.py:27
  49.2 2.7 %collective-permute-start.15 = (f32[24,128]{1,0:T(8,128)S(1)}, f32[24,128]{1,0:T(8,128)S(1)}, u32[]{:S(2)}, u32[]{:S(2)}) collective-permute-start(f32[24,128]{1,0:T(8,128)S(1)} %pad_maximum_fusion), channel_id=1, source_target_pairs={{0,224},{32,0},{64,32},{96,64},{128,96},{160,128},{192,160},{224,1... | collective-permute-start | bytes 36872 | tf_op jit(solution)/shard_map/ppermute | solution.py:27
  49.2 3.8 %collective-permute-start.14 = (f32[24,128]{1,0:T(8,128)S(1)}, f32[24,128]{1,0:T(8,128)S(1)}, u32[]{:S(2)}, u32[]{:S(2)}) collective-permute-start(f32[24,128]{1,0:T(8,128)S(1)} %pad_maximum_fusion), channel_id=1, source_target_pairs={{0,32},{32,64},{64,96},{96,128},{128,160},{160,192},{192,224},{224... | collective-permute-start | bytes 36872 | tf_op jit(solution)/shard_map/ppermute | solution.py:27
  54.6 2.6 %collective-permute-start.16 = (f32[16,256]{1,0:T(8,128)S(1)}, f32[16,256]{1,0:T(8,128)S(1)}, u32[]{:S(2)}, u32[]{:S(2)}) collective-permute-start(f32[16,256]{1,0:T(8,128)S(1)} %get-tuple-element.52), channel_id=1, source_target_pairs={{0,3},{1,0},{2,1},{3,2},{4,7},{5,4},{6,5},{7,6},{8,11},{9,8},{10,9... | collective-permute-start | bytes 49160 | tf_op jit(solution)/shard_map/ppermute | solution.py:27
  54.7 3.9 %collective-permute-start.17 = (f32[16,256]{1,0:T(8,128)S(1)}, f32[16,256]{1,0:T(8,128)S(1)}, u32[]{:S(2)}, u32[]{:S(2)}) collective-permute-start(f32[16,256]{1,0:T(8,128)S(1)} %get-tuple-element.53), channel_id=1, source_target_pairs={{0,1},{1,2},{2,3},{3,0},{4,5},{5,6},{6,7},{7,4},{8,9},{9,10},{10,1... | collective-permute-start | bytes 49160 | tf_op jit(solution)/shard_map/ppermute | solution.py:27
  59.2 6.7 %collective-permute-start.19 = (f32[8,128]{1,0:T(8,128)S(1)}, f32[8,128]{1,0:T(8,128)S(1)}, u32[]{:S(2)}, u32[]{:S(2)}) collective-permute-start(f32[8,128]{1,0:T(8,128)S(1)} %image.3.own.third), channel_id=1, source_target_pairs={{0,28},{4,0},{8,4},{12,8},{16,12},{20,16},{24,20},{28,24},{1,29},{... | collective-permute-start | bytes 12296 | tf_op jit(solution)/shard_map/ppermute | solution.py:27
  65.1 1.2 %collective-permute-start.18 = (f32[8,128]{1,0:T(8,128)S(1)}, f32[8,128]{1,0:T(8,128)S(1)}, u32[]{:S(2)}, u32[]{:S(2)}) collective-permute-start(f32[8,128]{1,0:T(8,128)S(1)} %image.3.own.third), channel_id=1, source_target_pairs={{0,4},{4,8},{8,12},{12,16},{16,20},{20,24},{24,28},{28,0},{1,5},{5... | collective-permute-start | bytes 12296 | tf_op jit(solution)/shard_map/ppermute | solution.py:27
  66.2 2.7 %collective-permute-start.21 = (f32[24,128]{1,0:T(8,128)S(1)}, f32[24,128]{1,0:T(8,128)S(1)}, u32[]{:S(2)}, u32[]{:S(2)}) collective-permute-start(f32[24,128]{1,0:T(8,128)S(1)} %pad_maximum_fusion.1), channel_id=1, source_target_pairs={{0,224},{32,0},{64,32},{96,64},{128,96},{160,128},{192,160},{224,1... | collective-permute-start | bytes 36872 | tf_op jit(solution)/shard_map/ppermute | solution.py:27
  66.2 3.8 %collective-permute-start.20 = (f32[24,128]{1,0:T(8,128)S(1)}, f32[24,128]{1,0:T(8,128)S(1)}, u32[]{:S(2)}, u32[]{:S(2)}) collective-permute-start(f32[24,128]{1,0:T(8,128)S(1)} %pad_maximum_fusion.1), channel_id=1, source_target_pairs={{0,32},{32,64},{64,96},{96,128},{128,160},{160,192},{192,224},{224... | collective-permute-start | bytes 36872 | tf_op jit(solution)/shard_map/ppermute | solution.py:27
  71.6 2.6 %collective-permute-start.22 = (f32[16,256]{1,0:T(8,128)S(1)}, f32[16,256]{1,0:T(8,128)S(1)}, u32[]{:S(2)}, u32[]{:S(2)}) collective-permute-start(f32[16,256]{1,0:T(8,128)S(1)} %get-tuple-element.55), channel_id=1, source_target_pairs={{0,3},{1,0},{2,1},{3,2},{4,7},{5,4},{6,5},{7,6},{8,11},{9,8},{10,9... | collective-permute-start | bytes 49160 | tf_op jit(solution)/shard_map/ppermute | solution.py:27
  71.7 3.9 %collective-permute-start.23 = (f32[16,256]{1,0:T(8,128)S(1)}, f32[16,256]{1,0:T(8,128)S(1)}, u32[]{:S(2)}, u32[]{:S(2)}) collective-permute-start(f32[16,256]{1,0:T(8,128)S(1)} %get-tuple-element.56), channel_id=1, source_target_pairs={{0,1},{1,2},{2,3},{3,0},{4,5},{5,6},{6,7},{7,4},{8,9},{9,10},{10,1... | collective-permute-start | bytes 49160 | tf_op jit(solution)/shard_map/ppermute | solution.py:27

commit v3 on v2

v3 whole, which is shorter than its diff:
```python
import jax
import jax.numpy as jnp
from jax import lax
from jax.experimental import pallas as pl
from jax.experimental.pallas import tpu as pltpu
from jax.sharding import Mesh
from jax.sharding import PartitionSpec as P

GY = ("gy_0", "gy_1")
GX_GY_GZ = ("gx", "gy_0", "gy_1", "gz")

PLANES = 13
YPAD = 16
ROWS = PLANES * YPAD
INNER = 11 * YPAD
LANES = 256
DEEP = 16
REACH = 12
MARKERS = 256
FIRST = 3 * MARKERS
STATIC = FIRST + 3 * 128
COLS = STATIC + 3 * 384
F32 = jnp.float32
BF16 = jnp.bfloat16
PARAMS = pltpu.CompilerParams(vmem_limit_bytes=12 * 1024 * 1024)


def shifted(shard, axis, by):
    length = lax.axis_size(axis)
    return lax.ppermute(shard, axis, [(i, (i + by) % length) for i in range(length)])


def halves(value):
    high = value.astype(BF16)
    return high, (value - high.astype(F32)).astype(BF16)


def transposed_dot(left, right):
    return lax.dot_general(left, right, (((1,), (1,)), ((), ())), preferred_element_type=F32)


def plain_dot(left, right):
    return lax.dot_general(left, right, (((1,), (0,)), ((), ())), preferred_element_type=F32)


def delta_rows(extent, cell, fraction):
    step = lax.broadcasted_iota(jnp.int32, (extent, cell.shape[1]), 0).astype(F32) - cell
    radius = jnp.abs(step - fraction)
    near = (step == 0.0) | (step == 1.0)
    far = (step == -1.0) | (step == 2.0)
    inner = (3.0 - 2.0 * radius + jnp.sqrt(jnp.maximum(1.0 + 4.0 * radius - 4.0 * radius * radius, 0.0))) / 8.0
    outer = (5.0 - 2.0 * radius - jnp.sqrt(jnp.maximum(-7.0 + 12.0 * radius - 4.0 * radius * radius, 0.0))) / 8.0
    return jnp.where(near, inner, jnp.where(far, outer, 0.0))


def pack_kernel(
    density_in, base_in, cells_in, offsets_in, target_in, stiffness_in, counts, fields, own, to_above, to_below,
    density, base, cells, offsets, target, stiffness, arrived,
):
    sources = (density_in, base_in, cells_in, offsets_in, target_in, stiffness_in)
    places = (density, base, cells, offsets, target, stiffness)
    copies = [pltpu.make_async_copy(a, b, arrived.at[i]) for i, (a, b) in enumerate(zip(sources, places))]
    for copy in copies:
        copy.start()
    for copy in copies:
        copy.wait()
    for plane in range(8):
        for field in range(4):
            piece = density[plane] if field == 3 else base[field, plane]
            fields[(field * 8 + plane) * 8 : (field * 8 + plane) * 8 + 8, :] = piece
    for block in range(2):
        turned = fields[block * 128 : block * 128 + 128, :].T
        to_below[block * 16 : block * 16 + 16, :] = turned[0:DEEP]
        to_above[block * 16 : block * 16 + 16, :] = turned[128 - DEEP : 128]
    lane = lax.broadcasted_iota(jnp.int32, (1, MARKERS), 1)
    live = jnp.where(lane < counts[0], 1.0, 0.0).astype(F32)
    inside = [(cells[k : k + 1, :] & (7, 7, 127)[k]).astype(F32) for k in range(3)]
    data = inside + [offsets[k : k + 1, :] for k in range(3)] + [live, stiffness[0:1, :]]
    data += [target[k : k + 1, :] for k in range(3)]
    for k, row in enumerate(data):
        own[2 * k : 2 * k + 1, :] = row[:, 0:128]
        own[2 * k + 1 : 2 * k + 2, :] = row[:, 128:256]
    own[22:24, :] = jnp.zeros((2, 128), F32)
    table = jnp.concatenate(data + [jnp.zeros((5, MARKERS), F32)], axis=0)
    table_high = table.astype(BF16)
    rest = table - table_high.astype(F32)
    table_mid = rest.astype(BF16)
    table_low = (rest - table_mid.astype(F32)).astype(BF16)
    upper = jnp.where(inside[2] >= 128.0 - REACH, live, 0.0)
    lower = jnp.where(inside[2] < 1.0 * REACH, live, 0.0)
    flags = jnp.concatenate([upper, lower, jnp.zeros((14, MARKERS), F32)], axis=0).astype(BF16)
    earlier = lax.broadcasted_iota(jnp.int32, (MARKERS, MARKERS), 0) < lax.broadcasted_iota(
        jnp.int32, (MARKERS, MARKERS), 1
    )
    ranks = plain_dot(flags, jnp.where(earlier, 1.0, 0.0).astype(BF16)).astype(jnp.int32)
    slot = lax.broadcasted_iota(jnp.int32, (512, MARKERS), 0)
    lane = lax.broadcasted_iota(jnp.int32, (1, 128), 1)
    for at, (flag, out, shift) in enumerate(((upper, to_above, -128.0), (lower, to_below, 128.0))):
        rank = ranks[at : at + 1, :]
        goal = ((rank >> 6) << 7) + (rank & 63) + 64 * at
        chosen = jnp.where((slot == goal) & (flag > 0.0), 1.0, 0.0).astype(BF16)
        moved = transposed_dot(table_high, chosen) + transposed_dot(table_mid, chosen)
        moved = moved + transposed_dot(table_low, chosen)
        number = jnp.broadcast_to(jnp.sum(flag, axis=1, keepdims=True), (1, 128))
        number = jnp.where((lane < 64) == (at == 0), number, 0.0)
        for block in range(4):
            columns = slice(block * 128, block * 128 + 128)
            for k in range(11):
                row = moved[k : k + 1, columns]
                if k == 2:
                    row = row + shift * moved[6:7, columns]
                out[32 + 4 * k + block : 33 + 4 * k + block, :] = row
            out[76 + block : 77 + block, :] = number


def deepen_z_kernel(fields, own, below, above, wide, marks, aux, upward, downward):
    lane = lax.broadcasted_iota(jnp.int32, (128, 128), 1)
    packed = jnp.zeros((64, 128), F32)
    lane64 = lax.broadcasted_iota(jnp.int32, (64, 128), 1)
    for block in range(2):
        edge = jnp.concatenate(
            [below[block * 16 : block * 16 + 16, :], above[block * 16 : block * 16 + 16, :], jnp.zeros((96, 128), F32)],
            axis=0,
        ).T
        turned = pltpu.roll(fields[block * 128 : block * 128 + 128, :], DEEP, 1)
        wide[block * 128 : block * 128 + 128, :] = jnp.where(lane < DEEP, edge, turned)
        beyond = jnp.where(lane < DEEP, turned, edge)
        for half in range(2):
            field = 2 * block + half
            piece = beyond[half * 64 : half * 64 + 64]
            piece = pltpu.roll(piece, 32 * field, 1) if field else piece
            packed = jnp.where((lane64 >= 32 * field) & (lane64 < 32 * field + 32), piece, packed)
    wide[256:320, :] = packed
    for at in range(40):
        upward[at * 2 : at * 2 + 2, :] = wide[at * 8 + 6 : at * 8 + 8, :]
        downward[at * 3 : at * 3 + 3, :] = wide[at * 8 : at * 8 + 3, :]
    halo = below[32:80, :] + above[32:80, :]
    marks[0:16, :] = own[0:16, :]
    marks[16:40, :] = halo[0:24]
    marks[40:48, :] = jnp.broadcast_to(halo[44:45], (8, 128))
    upward[80:128, :] = marks[...]
    downward[120:168, :] = marks[...]
    aux[...] = jnp.zeros((72, 128), F32)
    for kind in range(3):
        for c in range(3):
            k = 6 + kind if kind < 2 else 8 + c
            aux[24 * kind + 2 * c : 24 * kind + 2 * c + 2, :] = own[2 * k : 2 * k + 2, :]
            for block in range(4):
                row = 24 * kind + 8 + 3 * block + c
                aux[row : row + 1, :] = halo[4 * k + block : 4 * k + block + 1]


def deepen_y_kernel(wide, marks, below, above, deep, three, upward, downward):
    for at in range(40):
        row = at * YPAD
        deep[row : row + 2, :] = below[at * 2 : at * 2 + 2, :]
        deep[row + 2 : row + 10, :] = wide[at * 8 : at * 8 + 8, :]
        deep[row + 10 : row + 13, :] = above[at * 3 : at * 3 + 3, :]
        deep[row + 13 : row + 16, :] = jnp.ones((3, 128), F32)
    for c in range(3):
        upward[c * 16 : c * 16 + 16, :] = deep[c * 128 + 112 : c * 128 + 128, :]
        downward[c * 32 : c * 32 + 32, :] = deep[c * 128 : c * 128 + 32, :]
    for at in range(2):
        row = (3 + at) * 128
        upward[48 + at * 32 : 80 + at * 32, :] = deep[row + 96 : row + 128, :]
        downward[96 + at * 48 : 144 + at * 48, :] = deep[row : row + 48, :]
    three[0:48, :] = marks[...]
    three[48:96, :] = below[80:128, :]
    three[96:144, :] = above[120:168, :]
    upward[112:256, :] = three[...]
    downward[192:336, :] = three[...]


def blocks_used(refs):
    most = jnp.max(jnp.concatenate([ref[first + 40 + 48 * part : first + 41 + 48 * part, :] for ref, first in refs for part in range(3)], axis=0))
    return (most.astype(jnp.int32) + 63) >> 6


def trips(used):
    return jnp.max(used[0:1, :])


def fill_tables(ref, first, along_x, used, plane_weights, z_high, z_low):
    def fill(read, along_y, place):
        plane_weights[0:16, place] = delta_rows(16, read(0) + (along_x + 2.0), read(3))
        plane_weights[16:32, place] = delta_rows(16, read(1) + (along_y + 2.0), read(4))
        high, rest = halves(delta_rows(160, read(2) + 16.0, read(5)))
        z_high[0:160, place] = high
        z_low[0:160, place] = rest

    for part, along_y in enumerate((0.0, -8.0, 8.0)):
        top = first + 48 * part
        for half in range(2):
            column = part * 256 + half * 128
            fill(lambda k: ref[top + 2 * k + half : top + 2 * k + half + 1, :], along_y, slice(column, column + 128))
        column = FIRST + part * 128
        fill(lambda k: ref[top + 16 + 4 * k : top + 17 + 4 * k, :], along_y, slice(column, column + 128))

    def further(block, carry):
        for part, along_y in enumerate((0.0, -8.0, 8.0)):
            top = first + 48 * part + 16 + block
            column = pl.multiple_of(STATIC + (block - 1) * 384 + part * 128, 128)
            fill(lambda k: ref[pl.ds(top + 4 * k, 1), :], along_y, pl.ds(column, 128))
        return carry

    lax.fori_loop(1, used, further, 0)
    z_high[160:256, :] = jnp.zeros((96, COLS), BF16)
    z_low[160:256, :] = jnp.zeros((96, COLS), BF16)


def own_tables_kernel(three, plane_weights, z_high, z_low, used):
    count = blocks_used([(three, 0)])
    used[...] = jnp.full((8, 128), count, jnp.int32)
    fill_tables(three, 0, 0.0, count, plane_weights, z_high, z_low)


def side_tables_kernel(below, above, b_weights, b_high, b_low, a_weights, a_high, a_low, used):
    count = blocks_used([(below, 112), (above, 192)])
    used[...] = jnp.full((8, 128), count, jnp.int32)
    fill_tables(below, 112, -8.0, count, b_weights, b_high, b_low)
    fill_tables(above, 192, 8.0, count, a_weights, a_high, a_low)


def interpolate(velocity_high, velocity_low, plane_weights, z_high, z_low, used, image):
    def lines(place):
        partial = plain_dot(velocity_high[...], z_high[:, place]) + plain_dot(velocity_low[...], z_high[:, place])
        partial = partial + plain_dot(velocity_high[...], z_low[:, place])
        result = []
        for c in range(3):
            total = partial[c * INNER : c * INNER + YPAD] * plane_weights[1:2, place]
            for plane in range(1, 11):
                row = c * INNER + plane * YPAD
                total = total + partial[row : row + YPAD] * plane_weights[plane + 1 : plane + 2, place]
            result.append(jnp.sum(total * plane_weights[16:32, place], axis=0, keepdims=True))
        return result

    image[...] = jnp.zeros((24, 128), F32)
    for c, line in enumerate(lines(slice(0, MARKERS))):
        image[2 * c : 2 * c + 1, :] = line[:, 0:128]
        image[2 * c + 1 : 2 * c + 2, :] = line[:, 128:256]
    for c, line in enumerate(lines(slice(FIRST, FIRST + 128))):
        image[8 + c : 9 + c, :] = line

    def further(block, carry):
        for c, line in enumerate(lines(pl.ds(pl.multiple_of(STATIC + (block - 1) * 384, 128), 128))):
            image[pl.ds(8 + 3 * block + c, 1), :] = line
        return carry

    lax.fori_loop(1, used, further, 0)


def setup_kernel(deep, below, above, plane_weights, z_high, z_low, aux, used, scale, start, velocity_high, velocity_low, image):
    lane = lax.broadcasted_iota(jnp.int32, (YPAD, 128), 1)
    for plane in range(PLANES):
        at = plane * YPAD

        def piece(field):
            if plane < 2:
                row = field * 16 if field < 3 else 48 + (field - 3) * 32 + plane * 16
                return below[row : row + 16, :]
            if plane < 10:
                row = field * 128 + (plane - 2) * 16
                return deep[row : row + 16, :]
            row = field * 32 if field < 3 else 96 + (field - 3) * 48
            row += (plane - 10) * 16
            return above[row : row + 16, :]

        packed = piece(4)
        scale[at : at + YPAD, 0:128] = lax.rsqrt(piece(3))
        scale[at : at + YPAD, 128:256] = lax.rsqrt(jnp.where(lane < 32, pltpu.roll(packed, 32, 1), 1.0))
        if 1 <= plane <= 11:
            for c in range(3):
                row = c * INNER + at - YPAD
                top, rest = halves(piece(c))
                velocity_high[row : row + YPAD, 0:128] = top
                velocity_low[row : row + YPAD, 0:128] = rest
                beyond = pltpu.roll(packed, 128 - 32 * c, 1) if c else packed
                top, rest = halves(jnp.where(lane < 32, beyond, 0.0))
                velocity_high[row : row + YPAD, 128:256] = top
                velocity_low[row : row + YPAD, 128:256] = rest
    interpolate(velocity_high, velocity_low, plane_weights, z_high, z_low, trips(used), image)
    start[...] = aux[0:24, :] * (aux[48:72, :] - image[...])


def fill_tile(rows, planes, plane_weights, weight, left_high, left_low, place):
    along_y = plane_weights[16:32, weight]
    vector = [row * along_y for row in rows]
    for at, plane in enumerate(planes):
        along_x = plane_weights[plane : plane + 1, weight]
        for c in range(3):
            top, rest = halves(vector[c] * along_x)
            row = (c * len(planes) + at) * YPAD
            left_high[row : row + YPAD, place] = top
            left_low[row : row + YPAD, place] = rest


def spread_columns(left_high, left_low, z_high, z_low, left, right):
    total = transposed_dot(left_high[:, left], z_high[:, right]) + transposed_dot(left_low[:, left], z_high[:, right])
    return total + transposed_dot(left_high[:, left], z_low[:, right])


def spread_group(refs, planes, plane_weights, z_high, z_low, used, left_high, left_low, total):
    for part, (ref, first) in enumerate(refs):
        for half in range(2):
            place = slice(part * 256 + half * 128, part * 256 + half * 128 + 128)
            rows = [ref[first + 2 * c + half : first + 2 * c + half + 1, :] for c in range(3)]
            fill_tile(rows, planes, plane_weights, place, left_high, left_low, place)
        place = slice(FIRST + part * 128, FIRST + part * 128 + 128)
        rows = [ref[first + 8 + c : first + 9 + c, :] for c in range(3)]
        fill_tile(rows, planes, plane_weights, place, left_high, left_low, place)
    whole = slice(0, STATIC)
    total[...] = spread_columns(left_high, left_low, z_high, z_low, whole, whole)

    def further(block, carry):
        for part, (ref, first) in enumerate(refs):
            column = pl.multiple_of(STATIC + (block - 1) * 384 + part * 128, 128)
            rows = [ref[pl.ds(first + 8 + 3 * block + c, 1), :] for c in range(3)]
            place = slice(part * 128, part * 128 + 128)
            fill_tile(rows, planes, plane_weights, pl.ds(column, 128), left_high, left_low, place)
        right = pl.ds(pl.multiple_of(STATIC + (block - 1) * 384, 128), 384)
        total[...] += spread_columns(left_high, left_low, z_high, z_low, slice(0, 384), right)
        return carry

    lax.fori_loop(1, used, further, 0)


def own_spread_kernel(own, below, above, plane_weights, z_high, z_low, used, moved, left_high, left_low):
    refs = [(own, 0), (below, 0), (above, 0)]
    spread_group(refs, range(1, 12), plane_weights, z_high, z_low, trips(used), left_high, left_low, moved)


def apply_image(
    moved, below, above, own_tables, own_used, side_tables, side_used, scale, aux, vector,
    left_high, left_low, first, final, field, velocity_high, velocity_low, image,
):
    refs = [[(ref, 24 * part) for part in range(3)] for ref in (below, above)]
    spread_group(refs[0], range(0, 4), *side_tables[0:3], trips(side_used), left_high.at[0], left_low.at[0], first)
    spread_group(refs[1], range(9, 13), *side_tables[3:6], trips(side_used), left_high.at[1], left_low.at[1], final)
    for c in range(3):
        for plane in range(PLANES):
            parts = []
            if 1 <= plane <= 11:
                row = c * INNER + (plane - 1) * YPAD
                parts.append(moved[row : row + YPAD, :])
            if plane < 4:
                row = c * 64 + plane * YPAD
                parts.append(first[row : row + YPAD, :])
            if plane >= 9:
                row = c * 64 + (plane - 9) * YPAD
                parts.append(final[row : row + YPAD, :])
            total = parts[0] if len(parts) == 1 else parts[0] + parts[1]
            row = c * ROWS + plane * YPAD
            field[row : row + YPAD, :] = total * scale[plane * YPAD : plane * YPAD + YPAD, :]
    axial, diagonal = 1.0 / 6.0, 1.0 / 12.0
    up_y = lambda a: pltpu.roll(a, 1, 0)
    down_y = lambda a: pltpu.roll(a, YPAD - 1, 0)
    up_z = lambda a: pltpu.roll(a, 1, 1)
    down_z = lambda a: pltpu.roll(a, LANES - 1, 1)
    onward = [None] * PLANES
    back = [None] * PLANES
    still = [None] * PLANES
    for plane in range(PLANES):
        gx, gy, gz = (field[c * ROWS + plane * YPAD : c * ROWS + plane * YPAD + YPAD, :] for c in range(3))
        hx, hy, hz = gx * diagonal, gy * diagonal, gz * diagonal
        sum_xy, dif_xy = hx + hy, hx - hy
        zx_up, zy_up, zz_up = up_z(hx), up_z(hy), up_z(hz)
        zx_dn, zy_dn, zz_dn = down_z(hx), down_z(hy), down_z(hz)
        xz_sum_up, xz_sum_dn, xz_dif_up, xz_dif_dn = zx_up + zz_up, zx_dn + zz_dn, zx_up - zz_up, zx_dn - zz_dn
        xy_sum_up, xy_sum_dn, xy_dif_up, xy_dif_dn = up_y(sum_xy), down_y(sum_xy), up_y(dif_xy), down_y(dif_xy)
        ax = gx * axial
        onward[plane] = (
            ax + ((xy_sum_up + xy_dif_dn) + (xz_sum_up + xz_dif_dn)),
            xy_sum_up - xy_dif_dn,
            xz_sum_up - xz_dif_dn,
        )
        back[plane] = (
            ax + ((xy_sum_dn + xy_dif_up) + (xz_sum_dn + xz_dif_up)),
            xy_sum_dn - xy_dif_up,
            xz_sum_dn - xz_dif_up,
        )
        yz_same = up_y(zy_up + zz_up)
        yz_same_dn = down_y(zy_dn + zz_dn)
        yz_cross = up_y(zy_dn - zz_dn)
        yz_cross_dn = down_y(zy_up - zz_up)
        same, cross = yz_same + yz_same_dn, yz_cross + yz_cross_dn
        still[plane] = (
            gx,
            gy + ((up_y(hy) + down_y(hy)) * 2.0 + (same + cross)),
            gz + ((zz_up + zz_dn) * 2.0 + (same - cross)),
        )
        if plane >= 2:
            out = plane - 1
            factor = scale[out * YPAD : out * YPAD + YPAD, :] * 0.5
            first = (out - 1) * YPAD
            for c in range(3):
                value = (still[out][c] + (onward[out - 1][c] + back[out + 1][c])) * factor
                top, rest = halves(value)
                row = c * INNER + first
                velocity_high[row : row + YPAD, :] = top
                velocity_low[row : row + YPAD, :] = rest
    interpolate(velocity_high, velocity_low, *own_tables, trips(own_used), image)
    return aux[0:24, :] * (image[...] + aux[24:48, :] * vector[...])


def image_kernel(
    moved, below, above, w, h, l, own_used, bw, bh, bl, aw, ah, al, side_used, scale, aux, vector, result, *scratch
):
    result[...] = apply_image(
        moved, below, above, (w, h, l), own_used, (bw, bh, bl, aw, ah, al), side_used, scale, aux, vector, *scratch
    )


def two_sum(a, b):
    total = a + b
    part = total - a
    return total, (a - (total - part)) + (b - part)


def fast_two_sum(a, b):
    total = a + b
    return total, b - (total - a)


def split(a):
    scaled = a * 4097.0
    high = scaled - (scaled - a)
    return high, a - high


def two_product(a, b):
    product = a * b
    a_high, a_low = split(a)
    b_high, b_low = split(b)
    return product, ((a_high * b_high - product) + a_high * b_low + a_low * b_high) + a_low * b_low


def pair_add(a, b):
    head, tail = two_sum(a[0], b[0])
    return fast_two_sum(head, tail + (a[1] + b[1]))


def pair_negative(a):
    return (-a[0], -a[1])


def pair_multiply(a, b):
    head, tail = two_product(a[0], b[0])
    return fast_two_sum(head, tail + (a[0] * b[1] + a[1] * b[0]))


def pair_divide(a, b):
    first = a[0] / b[0]
    rest = pair_add(a, pair_negative(pair_multiply((first, jnp.zeros_like(first)), b)))
    return fast_two_sum(first, rest[0] / b[0])


ENTRIES = ((0, 0), (0, 1), (0, 2), (0, 3), (1, 1), (1, 2), (1, 3), (2, 2), (2, 3))


def last_kernel(
    moved, below, above, w, h, l, own_used, bw, bh, bl, aw, ah, al, side_used, scale, aux, third, first, second, sums,
    *scratch
):
    fourth = apply_image(
        moved, below, above, (w, h, l), own_used, (bw, bh, bl, aw, ah, al), side_used, scale, aux, third, *scratch
    )
    vectors = [first[0:8, :], second[0:8, :], third[0:8, :], fourth[0:8]]
    lane = lax.broadcasted_iota(jnp.int32, (8, 128), 1)
    packed = jnp.zeros((8, 128), F32)
    for at, (i, j) in enumerate(ENTRIES):
        value = two_product(vectors[i], vectors[j])
        for axis, steps in ((0, (4, 2, 1)), (1, (64, 32, 16, 8, 4, 2, 1))):
            for step in steps:
                value = pair_add(value, (pltpu.roll(value[0], step, axis), pltpu.roll(value[1], step, axis)))
        packed = jnp.where(lane == at, value[0], jnp.where(lane == 16 + at, value[1], packed))
    for block in range(sums.shape[0] // 8):
        sums[block * 8 : block * 8 + 8, :] = packed


def finish_kernel(gathered, first, second, third, forces):
    a = gathered[...]
    count = a.shape[0]
    value = (a, pltpu.roll(a, 112, 1))
    while count > 8:
        count //= 2
        value = pair_add(
            (value[0][0:count], value[1][0:count]), (value[0][count : 2 * count], value[1][count : 2 * count])
        )
    for step in (4, 2, 1):
        value = pair_add(value, (pltpu.roll(value[0], step, 0), pltpu.roll(value[1], step, 0)))
    lane = lax.broadcasted_iota(jnp.int32, (8, 128), 1)
    gram = {}
    for at, (i, j) in enumerate(ENTRIES):
        entry = tuple(
            jnp.broadcast_to(jnp.sum(jnp.where(lane == at, v, 0.0), axis=1, keepdims=True), (8, 128)) for v in value
        )
        gram[i, j] = entry
        gram[j, i] = entry
    add, times = pair_add, pair_multiply
    minus = lambda a, b: pair_add(a, pair_negative(b))

    def form(left, right, shift):
        total = None
        for i, a in enumerate(left):
            for j, b in enumerate(right):
                term = times(times(a, b), gram[i, j + shift])
                total = term if total is None else add(total, term)
        return total

    one = (jnp.ones((8, 128), F32), jnp.zeros((8, 128), F32))
    alpha0 = pair_divide(gram[0, 0], gram[0, 1])
    residual = [one, pair_negative(alpha0)]
    norm1 = form(residual, residual, 0)
    beta0 = pair_divide(norm1, gram[0, 0])
    along1 = [add(one, beta0), pair_negative(alpha0)]
    alpha1 = pair_divide(norm1, form(along1, along1, 1))
    residual = [one, minus(residual[1], times(alpha1, along1[0])), pair_negative(times(alpha1, along1[1]))]
    norm2 = form(residual, residual, 0)
    beta1 = pair_divide(norm2, norm1)
    along2 = [add(one, times(beta1, along1[0])), add(residual[1], times(beta1, along1[1])), residual[2]]
    alpha2 = pair_divide(norm2, form(along2, along2, 1))
    weight0 = add(alpha0, add(times(alpha1, along1[0]), times(alpha2, along2[0])))
    weight1 = add(times(alpha1, along1[1]), times(alpha2, along2[1]))
    weight2 = times(alpha2, along2[2])
    total = weight0[0] * first[0:8, :] + (weight1[0] * second[0:8, :] + weight2[0] * third[0:8, :])
    for c in range(3):
        forces[c : c + 1, 0:128] = total[2 * c : 2 * c + 1, :]
        forces[c : c + 1, 128:256] = total[2 * c + 1 : 2 * c + 2, :]


def call(kernel, name, outs, *operands, memory=None, scratch=()):
    spec = lambda space: pl.BlockSpec(memory_space=space)
    memory = memory or [pltpu.VMEM] * len(operands)
    return pl.pallas_call(
        kernel,
        name=name,
        out_shape=[jax.ShapeDtypeStruct(shape, kind) for shape, kind in outs],
        in_specs=[spec(space) for space in memory],
        out_specs=[spec(pltpu.VMEM)] * len(outs),
        scratch_shapes=list(scratch),
        compiler_params=PARAMS,
    )(*operands)


def body(density, base_velocity, cells, offsets, target, stiffness, counts):
    rows = lambda n: ((n, 128), F32)
    vmem, smem, hbm = pltpu.VMEM, pltpu.SMEM, pltpu.HBM
    table_shapes = [((32, COLS), F32), ((256, COLS), BF16), ((256, COLS), BF16)]
    used_shape = [((8, 128), jnp.int32)]
    arguments = (density, base_velocity, cells, offsets, target, stiffness.reshape(1, MARKERS))
    fields, own, to_above, to_below = call(
        pack_kernel, "pack", [rows(256), rows(24), rows(80), rows(80)],
        *(pltpu.with_memory_space_constraint(a, hbm) for a in arguments), counts,
        memory=[hbm] * 6 + [smem],
        scratch=[
            vmem((8, 8, 128), F32), vmem((3, 8, 8, 128), F32), vmem((3, MARKERS), jnp.int32),
            vmem((3, MARKERS), F32), vmem((3, MARKERS), F32), vmem((1, MARKERS), F32),
            pltpu.SemaphoreType.DMA((6,)),
        ],
    )
    below, above = shifted(to_above, "gz", 1), shifted(to_below, "gz", -1)
    wide, marks, aux, upward, downward = call(
        deepen_z_kernel, "deepen_z", [rows(320), rows(48), rows(72), rows(128), rows(168)], fields, own, below, above
    )
    below, above = shifted(upward, GY, 1), shifted(downward, GY, -1)
    deep, three, upward, downward = call(
        deepen_y_kernel, "deepen_y", [rows(640), rows(144), rows(256), rows(336)], wide, marks, below, above
    )
    below, above = shifted(upward, "gx", 1), shifted(downward, "gx", -1)
    own_tables = call(
        own_tables_kernel, "own_tables", table_shapes + used_shape, three
    )
    side_tables = call(
        side_tables_kernel, "side_tables", table_shapes * 2 + used_shape, below, above
    )
    velocity_scratch = [vmem((3 * INNER, LANES), BF16)] * 2 + [vmem((24, 128), F32)]
    scale, start = call(
        setup_kernel, "setup", [((ROWS, LANES), F32), rows(24)], deep, below, above, *own_tables[0:3], aux, own_tables[3],
        scratch=velocity_scratch,
    )

    def image_of(kernel, name, outs, vector, *others):
        below, above = shifted(vector, GY, 1), shifted(vector, GY, -1)
        three = jnp.concatenate([vector, below, above], axis=0)
        below_three, above_three = shifted(three, "gx", 1), shifted(three, "gx", -1)
        (moved,) = call(
            own_spread_kernel, "own_spread", [((3 * INNER, LANES), F32)], vector, below, above, *own_tables,
            scratch=[vmem((3 * INNER, STATIC), BF16)] * 2,
        )
        (result,) = call(
            kernel, name, outs, moved, below_three, above_three, *own_tables, *side_tables, scale, aux, vector, *others,
            scratch=[vmem((2, 192, STATIC), BF16)] * 2 + [vmem((192, LANES), F32)] * 2
            + [vmem((3 * ROWS, LANES), F32)] + velocity_scratch,
        )
        return result

    second = image_of(image_kernel, "image", [rows(24)], start)
    third = image_of(image_kernel, "image", [rows(24)], second)
    sums = image_of(last_kernel, "last", [rows(256)], third, start, second)
    gathered = lax.all_to_all(sums, GX_GY_GZ, 0, 0, tiled=True)
    (forces,) = call(finish_kernel, "finish", [((3, MARKERS), F32)], gathered, start, second, third)
    return forces


def solution(mesh):
    finer = Mesh(
        mesh.devices.reshape(mesh.shape["gx"], 4, 2, mesh.shape["gz"]), ("gx", "gy_0", "gy_1", "gz")
    )
    return jax.shard_map(
        body,
        mesh=finer,
        in_specs=(
            P("gx", GY, "gz"),
            P(None, "gx", GY, "gz"),
            P(None, GX_GY_GZ),
            P(None, GX_GY_GZ),
            P(None, GX_GY_GZ),
            P(GX_GY_GZ),
            P(GX_GY_GZ),
        ),
        out_specs=P(None, GX_GY_GZ),
        check_vma=False,
    )
```

time: 102 us -> 91.3 us (0.90)
  waiting for transfers between devices: 22.6 us -> 11.3 us
  starting transfers between devices: 39.2 us -> 32.3 us
  Pallas kernels: 15.4 us -> 21 us
  blocking collectives: 23.4 us -> 25.8 us
    ppermute x24 -> x18, waiting for transfers between devices: 22.6 us -> 11.3 us  [shifted(): lax.ppermute(shard, axis, [(i, (i + by) % length) for i in range(length)])]
    ppermute x24 -> x18, starting transfers between devices: 39.2 us -> 32.3 us  [shifted(): lax.ppermute(shard, axis, [(i, (i + by) % length) for i in range(length)])]
    pallas_call x15 -> x13, Pallas kernels: 15.4 us -> 21 us  [call(): pl.pallas_call(kernel, name=name, out_shape=[jax.ShapeDtypeStruct(shape,...]
    all_to_all x1, blocking collectives: 23.4 us -> 25.8 us  [body(): gathered = lax.all_to_all(sums, GX_GY_GZ, 0, 0, tiled=True)]
  transfers between devices with their start and end apart: 24 -> 18, of which waited for: 21 -> 11; matrix products, arithmetic and copies ran while one was open for 0% -> 0% of each run, Pallas kernels for 5% -> 9%
where the time goes in v3:
time: 91.3 us; the launch traced here: 91.2 us
  starting transfers between devices  32.3 us (35%)
  blocking collectives  25.8 us (28%)
  Pallas kernels  21 us (23%)
  waiting for transfers between devices  11.3 us (12%)
    ppermute x18, starting transfers between devices, shifted(): lax.ppermute(shard, axis, [(i, (i + by) % length) for i in range(length)])  32.3 us
    all_to_all x1, blocking collectives, body(): gathered = lax.all_to_all(sums, GX_GY_GZ, 0, 0, tiled=True)  25.8 us
    pallas_call x13, Pallas kernels, call(): pl.pallas_call(kernel, name=name, out_shape=[jax.ShapeDtypeStruct(shape,...  21 us
    ppermute x18, waiting for transfers between devices, shifted(): lax.ppermute(shard, axis, [(i, (i + by) % length) for i in range(length)])  11.3 us
  transfers between devices with their start and end apart: 18, of which 11 were waited for; matrix products, arithmetic and copies ran while one was open for 0% of the time, Pallas kernels for 9%

profile of v3, /device:TPU:1, one launch (start us, length us, event | category | flops | bytes accessed | tf_op | source)
XLA Modules:
  0.0 91.2 jit_solution(285997516616149755)
XLA Ops:
  0.7 1.7 %pack.1 = (f32[256,128]{1,0:T(8,128)S(1)}, f32[24,128]{1,0:T(8,128)S(1)}, f32[80,128]{1,0:T(8,128)S(1)}, f32[80,128]{1,0:T(8,128)S(1)}) custom-call(f32[8,8,128]{2,1,0:T(8,128)} %density_in.1, f32[3,8,8,128]{3,2,1,0:T(8,128)} %base_in.1, s32[3,256]{1,0:T(4,128)} %cells_in.1, f32[3,256]{1,0:T(4,128)} %offsets_in.1, f32[3,256]{1,0:T(4,128)} %target_in.1, ...), custom_call_target="tpu_custom_call" | custom-call | tf_op jit(solution)/shard_map/pack/pallas_call | solution.py:534
  2.3 2.1 %collective-permute-start = (f32[80,128]{1,0:T(8,128)S(1)}, f32[80,128]{1,0:T(8,128)S(1)}, u32[]{:S(2)}, u32[]{:S(2)}) collective-permute-start(f32[80,128]{1,0:T(8,128)S(1)} %get-tuple-element.33), channel_id=1, source_target_pairs={{0,1},{1,2},{2,3},{3,0},{4,5},{5,6},{6,7},{7,4},{8,9},{9,10},{10,1... | collective-permute-start | bytes 122888 | tf_op jit(solution)/shard_map/ppermute | solution.py:30
  4.4 1.4 %collective-permute-start.1 = (f32[80,128]{1,0:T(8,128)S(1)}, f32[80,128]{1,0:T(8,128)S(1)}, u32[]{:S(2)}, u32[]{:S(2)}) collective-permute-start(f32[80,128]{1,0:T(8,128)S(1)} %get-tuple-element.34), channel_id=1, source_target_pairs={{0,3},{1,0},{2,1},{3,2},{4,7},{5,4},{6,5},{7,6},{8,11},{9,8},{10,9... | collective-permute-start | bytes 122888 | tf_op jit(solution)/shard_map/ppermute | solution.py:30
  5.8 1.3 %collective-permute-done.below = f32[80,128]{1,0:T(8,128)S(1)} collective-permute-done((f32[80,128]{1,0:T(8,128)S(1)}, f32[80,128]{1,0:T(8,128)S(1)}, u32[]{:S(2)}, u32[]{:S(2)}) %collective-permute-start) | collective-permute-done | bytes 40992 | tf_op jit(solution)/shard_map/ppermute | solution.py:30
  7.6 3.5 %collective-permute-start.3 = (f32[168,128]{1,0:T(8,128)S(1)}, f32[168,128]{1,0:T(8,128)S(1)}, u32[]{:S(2)}, u32[]{:S(2)}) collective-permute-start(f32[168,128]{1,0:T(8,128)S(1)} %get-tuple-element.38), channel_id=1, source_target_pairs={{0,28},{4,0},{8,4},{12,8},{16,12},{20,16},{24,20},{28,24},{1,29},{... | collective-permute-start | bytes 258056 | tf_op jit(solution)/shard_map/ppermute | solution.py:30
  11.2 1.3 %collective-permute-done.2.below = f32[128,128]{1,0:T(8,128)S(1)} collective-permute-done((f32[128,128]{1,0:T(8,128)S(1)}, f32[128,128]{1,0:T(8,128)S(1)}, u32[]{:S(2)}, u32[]{:S(2)}) %collective-permute-start.2) | collective-permute-done | bytes 65568 | tf_op jit(solution)/shard_map/ppermute | solution.py:30
  13.2 5.7 %collective-permute-start.5 = (f32[336,128]{1,0:T(8,128)S(1)}, f32[336,128]{1,0:T(8,128)S(1)}, u32[]{:S(2)}, u32[]{:S(2)}) collective-permute-start(f32[336,128]{1,0:T(8,128)S(1)} %get-tuple-element.41), channel_id=1, source_target_pairs={{0,224},{32,0},{64,32},{96,64},{128,96},{160,128},{192,160},{224,1... | collective-permute-start | bytes 516104 | tf_op jit(solution)/shard_map/ppermute | solution.py:30
  18.8 1.5 %own_tables.1 = (f32[32,2304]{1,0:T(8,128)S(1)}, bf16[256,2304]{1,0:T(8,128)(2,1)S(1)}, bf16[256,2304]{1,0:T(8,128)(2,1)S(1)}, s32[8,128]{1,0:T(8,128)S(1)}) custom-call(f32[144,128]{1,0:T(8,128)S(1)} %get-tuple-element.42.three), custom_call_target="tpu_custom_call" | custom-call | tf_op jit(solution)/shard_map/own_tables/pallas_call | solution.py:534
  20.3 3.5 %collective-permute-done.4.below = f32[256,128]{1,0:T(8,128)S(1)} collective-permute-done((f32[256,128]{1,0:T(8,128)S(1)}, f32[256,128]{1,0:T(8,128)S(1)}, u32[]{:S(2)}, u32[]{:S(2)}) %collective-permute-start.4) | collective-permute-done | bytes 131104 | tf_op jit(solution)/shard_map/ppermute | solution.py:30
  23.8 0.6 setup.1
  24.5 3.3 %collective-permute-start.6 = (f32[24,128]{1,0:T(8,128)S(1)}, f32[24,128]{1,0:T(8,128)S(1)}, u32[]{:S(2)}, u32[]{:S(2)}) collective-permute-start(f32[24,128]{1,0:T(8,128)S(1)} %get-tuple-element.48.own.vector.first), channel_id=1, source_target_pairs={{0,4},{4,8},{8,12},{12,16},{16,20},{20,24},{24,28},{28,0},{1,5},{5... | collective-permute-start | bytes 36872 | tf_op jit(solution)/shard_map/ppermute | solution.py:30
  27.8 0.8 collective-permute-start.7
  28.5 0.6 collective-permute-done.6.below
  29.2 1.7 %collective-permute-done.7.above = f32[24,128]{1,0:T(8,128)S(1)} collective-permute-done((f32[24,128]{1,0:T(8,128)S(1)}, f32[24,128]{1,0:T(8,128)S(1)}, u32[]{:S(2)}, u32[]{:S(2)}) %collective-permute-start.7) | collective-permute-done | bytes 12320 | tf_op jit(solution)/shard_map/ppermute | solution.py:30
  30.9 2.7 %collective-permute-start.9 = (f32[72,128]{1,0:T(8,128)S(1)}, f32[72,128]{1,0:T(8,128)S(1)}, u32[]{:S(2)}, u32[]{:S(2)}) collective-permute-start(f32[72,128]{1,0:T(8,128)S(1)} %constant_dynamic-update-slice_fusion), channel_id=1, source_target_pairs={{0,224},{32,0},{64,32},{96,64},{128,96},{160,128},{192,160},{224,1... | collective-permute-start | bytes 110600 | tf_op jit(solution)/shard_map/ppermute | solution.py:30
  33.6 2.9 %side_tables.1 = (f32[32,2304]{1,0:T(8,128)S(1)}, bf16[256,2304]{1,0:T(8,128)(2,1)S(1)}, bf16[256,2304]{1,0:T(8,128)(2,1)S(1)}, f32[32,2304]{1,0:T(8,128)S(1)}, ...) custom-call(f32[256,128]{1,0:T(8,128)S(1)} %collective-permute-done.4.below, ...), custom_call_target="tpu_custom_call" | custom-call | tf_op jit(solution)/shard_map/side_tables/pallas_call | solution.py:534
  36.5 1.4 %own_spread.3.moved = f32[528,256]{1,0:T(8,128)S(1)} custom-call(f32[24,128]{1,0:T(8,128)S(1)} %get-tuple-element.48.own.vector.first, f32[24,128]{1,0:T(8,128)S(1)} %collective-permute-done.6.below, f32[24,128]{1,0:T(8,128)S(1)} %collective-permute-done.7.above, f32[32,2304]{1,0:T(8,128)S(1)} %get-tuple-element.43.plane_weights.w, ...), custom_call_target="tpu_custom_call" | custom-call | tf_op jit(solution)/shard_map/own_spread/pallas_call | solution.py:534
  37.9 2.7 %image.2.own.vector.second = f32[24,128]{1,0:T(8,128)S(1)} custom-call(f32[528,256]{1,0:T(8,128)S(1)} %own_spread.3.moved, f32[72,128]{1,0:T(8,128)S(1)} %collective-permute-done.8.below, f32[72,128]{1,0:T(8,128)S(1)} %collective-permute-done.9.above, f32[32,2304]{1,0:T(8,128)S(1)} %get-tuple-element.43.plane_weights.w, ...), custom_call_target="tpu_custom_call" | custom-call | tf_op jit(solution)/shard_map/image/pallas_call | solution.py:534
  40.6 0.6 collective-permute-start.10
  41.2 2.0 %collective-permute-start.11 = (f32[24,128]{1,0:T(8,128)S(1)}, f32[24,128]{1,0:T(8,128)S(1)}, u32[]{:S(2)}, u32[]{:S(2)}) collective-permute-start(f32[24,128]{1,0:T(8,128)S(1)} %image.2.own.vector.second), channel_id=1, source_target_pairs={{0,28},{4,0},{8,4},{12,8},{16,12},{20,16},{24,20},{28,24},{1,29},{... | collective-permute-start | bytes 36872 | tf_op jit(solution)/shard_map/ppermute | solution.py:30
  43.2 0.6 collective-permute-done.10.below
  44.3 2.7 %collective-permute-start.13 = (f32[72,128]{1,0:T(8,128)S(1)}, f32[72,128]{1,0:T(8,128)S(1)}, u32[]{:S(2)}, u32[]{:S(2)}) collective-permute-start(f32[72,128]{1,0:T(8,128)S(1)} %pad_maximum_fusion), channel_id=1, source_target_pairs={{0,224},{32,0},{64,32},{96,64},{128,96},{160,128},{192,160},{224,1... | collective-permute-start | bytes 110600 | tf_op jit(solution)/shard_map/ppermute | solution.py:30
  47.0 1.3 %own_spread.4.moved = f32[528,256]{1,0:T(8,128)S(1)} custom-call(f32[24,128]{1,0:T(8,128)S(1)} %image.2.own.vector.second, f32[24,128]{1,0:T(8,128)S(1)} %collective-permute-done.10.below, f32[24,128]{1,0:T(8,128)S(1)} %collective-permute-done.11.above, f32[32,2304]{1,0:T(8,128)S(1)} %get-tuple-element.43.plane_weights.w, ...), custom_call_target="tpu_custom_call" | custom-call | tf_op jit(solution)/shard_map/own_spread/pallas_call | solution.py:534
  48.4 2.7 %image.3.own.third = f32[24,128]{1,0:T(8,128)S(1)} custom-call(f32[528,256]{1,0:T(8,128)S(1)} %own_spread.4.moved, f32[72,128]{1,0:T(8,128)S(1)} %collective-permute-done.12.below, f32[72,128]{1,0:T(8,128)S(1)} %collective-permute-done.13.above, f32[32,2304]{1,0:T(8,128)S(1)} %get-tuple-element.43.plane_weights.w, ...), custom_call_target="tpu_custom_call" | custom-call | tf_op jit(solution)/shard_map/image/pallas_call | solution.py:534
  51.1 1.2 %collective-permute-start.14 = (f32[24,128]{1,0:T(8,128)S(1)}, f32[24,128]{1,0:T(8,128)S(1)}, u32[]{:S(2)}, u32[]{:S(2)}) collective-permute-start(f32[24,128]{1,0:T(8,128)S(1)} %image.3.own.third), channel_id=1, source_target_pairs={{0,4},{4,8},{8,12},{12,16},{16,20},{20,24},{24,28},{28,0},{1,5},{5... | collective-permute-start | bytes 36872 | tf_op jit(solution)/shard_map/ppermute | solution.py:30
  52.3 3.2 %collective-permute-start.15 = (f32[24,128]{1,0:T(8,128)S(1)}, f32[24,128]{1,0:T(8,128)S(1)}, u32[]{:S(2)}, u32[]{:S(2)}) collective-permute-start(f32[24,128]{1,0:T(8,128)S(1)} %image.3.own.third), channel_id=1, source_target_pairs={{0,28},{4,0},{8,4},{12,8},{16,12},{20,16},{24,20},{28,24},{1,29},{... | collective-permute-start | bytes 36872 | tf_op jit(solution)/shard_map/ppermute | solution.py:30
  55.4 0.6 collective-permute-done.14.below
  56.3 3.2 %collective-permute-start.17 = (f32[72,128]{1,0:T(8,128)S(1)}, f32[72,128]{1,0:T(8,128)S(1)}, u32[]{:S(2)}, u32[]{:S(2)}) collective-permute-start(f32[72,128]{1,0:T(8,128)S(1)} %pad_maximum_fusion.1), channel_id=1, source_target_pairs={{0,224},{32,0},{64,32},{96,64},{128,96},{160,128},{192,160},{224,1... | collective-permute-start | bytes 110600 | tf_op jit(solution)/shard_map/ppermute | solution.py:30
  59.5 1.4 %own_spread.5.moved = f32[528,256]{1,0:T(8,128)S(1)} custom-call(f32[24,128]{1,0:T(8,128)S(1)} %image.3.own.third, f32[24,128]{1,0:T(8,128)S(1)} %collective-permute-done.14.below, f32[24,128]{1,0:T(8,128)S(1)} %collective-permute-done.15.above, f32[32,2304]{1,0:T(8,128)S(1)} %get-tuple-element.43.plane_weights.w, ...), custom_call_target="tpu_custom_call" | custom-call | tf_op jit(solution)/shard_map/own_spread/pallas_call | solution.py:534
  60.9 3.2 %last.1 = f32[256,128]{1,0:T(8,128)S(1)} custom-call(f32[528,256]{1,0:T(8,128)S(1)} %own_spread.5.moved, f32[72,128]{1,0:T(8,128)S(1)} %collective-permute-done.16.below, f32[72,128]{1,0:T(8,128)S(1)} %collective-permute-done.17.above, f32[32,2304]{1,0:T(8,128)S(1)} %get-tuple-element.43.plane_weights.w, bf16[256,2304]{1,0:T(8,128)(2,1)S(1)} %get-tuple-element.44.z_high.h, ...), custom_call_target="tpu_custom_call" | custom-call | tf_op jit(solution)/shard_map/last/pallas_call | solution.py:534
  64.1 25.8 %all_to_all.11 = f32[256,1,128]{2,1,0:T(1,128)S(1)} all-to-all(f32[256,1,128]{2,1,0:T(1,128)S(1)} %bitcast.5), channel_id=1, replica_groups=mesh['gx'=8,'gy_0'=4,'gy_1'=2,'gz'=4] {'gx','gy_0','gy_1','gz'}, dimensions={0} | all-to-all | bytes 262144 | tf_op jit(solution)/shard_map/all_to_all | solution.py:600
  89.9 1.3 %finish.1 = f32[3,256]{1,0:T(4,128)} custom-call(f32[256,128]{1,0:T(8,128)S(1)} %bitcast.6, f32[24,128]{1,0:T(8,128)S(1)} %get-tuple-element.48.own.vector.first, f32[24,128]{1,0:T(8,128)S(1)} %image.2.own.vector.second, f32[24,128]{1,0:T(8,128)S(1)} %image.3.own.third), custom_call_target="tpu_custom_call" | custom-call | tf_op jit(solution)/shard_map/finish/pallas_call | solution.py:534
  (23 shorter events, 1.9 us)
Async XLA Ops:
  2.3 4.8 %collective-permute-start = (f32[80,128]{1,0:T(8,128)S(1)}, f32[80,128]{1,0:T(8,128)S(1)}, u32[]{:S(2)}, u32[]{:S(2)}) collective-permute-start(f32[80,128]{1,0:T(8,128)S(1)} %get-tuple-element.33), channel_id=1, source_target_pairs={{0,1},{1,2},{2,3},{3,0},{4,5},{5,6},{6,7},{7,4},{8,9},{9,10},{10,1... | collective-permute-start | bytes 122888 | tf_op jit(solution)/shard_map/ppermute | solution.py:30
  4.4 2.9 %collective-permute-start.1 = (f32[80,128]{1,0:T(8,128)S(1)}, f32[80,128]{1,0:T(8,128)S(1)}, u32[]{:S(2)}, u32[]{:S(2)}) collective-permute-start(f32[80,128]{1,0:T(8,128)S(1)} %get-tuple-element.34), channel_id=1, source_target_pairs={{0,3},{1,0},{2,1},{3,2},{4,7},{5,4},{6,5},{7,6},{8,11},{9,8},{10,9... | collective-permute-start | bytes 122888 | tf_op jit(solution)/shard_map/ppermute | solution.py:30
  7.6 5.5 %collective-permute-start.3 = (f32[168,128]{1,0:T(8,128)S(1)}, f32[168,128]{1,0:T(8,128)S(1)}, u32[]{:S(2)}, u32[]{:S(2)}) collective-permute-start(f32[168,128]{1,0:T(8,128)S(1)} %get-tuple-element.38), channel_id=1, source_target_pairs={{0,28},{4,0},{8,4},{12,8},{16,12},{20,16},{24,20},{28,24},{1,29},{... | collective-permute-start | bytes 258056 | tf_op jit(solution)/shard_map/ppermute | solution.py:30
  11.2 1.3 %collective-permute-start.2 = (f32[128,128]{1,0:T(8,128)S(1)}, f32[128,128]{1,0:T(8,128)S(1)}, u32[]{:S(2)}, u32[]{:S(2)}) collective-permute-start(f32[128,128]{1,0:T(8,128)S(1)} %get-tuple-element.37), channel_id=1, source_target_pairs={{0,4},{4,8},{8,12},{12,16},{16,20},{20,24},{24,28},{28,0},{1,5},{5... | collective-permute-start | bytes 196616 | tf_op jit(solution)/shard_map/ppermute | solution.py:30
  13.2 10.7 %collective-permute-start.5 = (f32[336,128]{1,0:T(8,128)S(1)}, f32[336,128]{1,0:T(8,128)S(1)}, u32[]{:S(2)}, u32[]{:S(2)}) collective-permute-start(f32[336,128]{1,0:T(8,128)S(1)} %get-tuple-element.41), channel_id=1, source_target_pairs={{0,224},{32,0},{64,32},{96,64},{128,96},{160,128},{192,160},{224,1... | collective-permute-start | bytes 516104 | tf_op jit(solution)/shard_map/ppermute | solution.py:30
  18.8 5.0 %collective-permute-start.4 = (f32[256,128]{1,0:T(8,128)S(1)}, f32[256,128]{1,0:T(8,128)S(1)}, u32[]{:S(2)}, u32[]{:S(2)}) collective-permute-start(f32[256,128]{1,0:T(8,128)S(1)} %get-tuple-element.40), channel_id=1, source_target_pairs={{0,32},{32,64},{64,96},{96,128},{128,160},{160,192},{192,224},{224... | collective-permute-start | bytes 393224 | tf_op jit(solution)/shard_map/ppermute | solution.py:30
  24.5 4.7 %collective-permute-start.6 = (f32[24,128]{1,0:T(8,128)S(1)}, f32[24,128]{1,0:T(8,128)S(1)}, u32[]{:S(2)}, u32[]{:S(2)}) collective-permute-start(f32[24,128]{1,0:T(8,128)S(1)} %get-tuple-element.48.own.vector.first), channel_id=1, source_target_pairs={{0,4},{4,8},{8,12},{12,16},{16,20},{20,24},{24,28},{28,0},{1,5},{5... | collective-permute-start | bytes 36872 | tf_op jit(solution)/shard_map/ppermute | solution.py:30
  27.8 3.1 %collective-permute-start.7 = (f32[24,128]{1,0:T(8,128)S(1)}, f32[24,128]{1,0:T(8,128)S(1)}, u32[]{:S(2)}, u32[]{:S(2)}) collective-permute-start(f32[24,128]{1,0:T(8,128)S(1)} %get-tuple-element.48.own.vector.first), channel_id=1, source_target_pairs={{0,28},{4,0},{8,4},{12,8},{16,12},{20,16},{24,20},{28,24},{1,29},{... | collective-permute-start | bytes 36872 | tf_op jit(solution)/shard_map/ppermute | solution.py:30
  30.9 7.0 %collective-permute-start.8 = (f32[72,128]{1,0:T(8,128)S(1)}, f32[72,128]{1,0:T(8,128)S(1)}, u32[]{:S(2)}, u32[]{:S(2)}) collective-permute-start(f32[72,128]{1,0:T(8,128)S(1)} %constant_dynamic-update-slice_fusion), channel_id=1, source_target_pairs={{0,32},{32,64},{64,96},{96,128},{128,160},{160,192},{192,224},{224... | collective-permute-start | bytes 110600 | tf_op jit(solution)/shard_map/ppermute | solution.py:30
  30.9 7.0 %collective-permute-start.9 = (f32[72,128]{1,0:T(8,128)S(1)}, f32[72,128]{1,0:T(8,128)S(1)}, u32[]{:S(2)}, u32[]{:S(2)}) collective-permute-start(f32[72,128]{1,0:T(8,128)S(1)} %constant_dynamic-update-slice_fusion), channel_id=1, source_target_pairs={{0,224},{32,0},{64,32},{96,64},{128,96},{160,128},{192,160},{224,1... | collective-permute-start | bytes 110600 | tf_op jit(solution)/shard_map/ppermute | solution.py:30
  40.6 3.3 %collective-permute-start.10 = (f32[24,128]{1,0:T(8,128)S(1)}, f32[24,128]{1,0:T(8,128)S(1)}, u32[]{:S(2)}, u32[]{:S(2)}) collective-permute-start(f32[24,128]{1,0:T(8,128)S(1)} %image.2.own.vector.second), channel_id=1, source_target_pairs={{0,4},{4,8},{8,12},{12,16},{16,20},{20,24},{24,28},{28,0},{1,5},{5... | collective-permute-start | bytes 36872 | tf_op jit(solution)/shard_map/ppermute | solution.py:30
  41.2 3.1 %collective-permute-start.11 = (f32[24,128]{1,0:T(8,128)S(1)}, f32[24,128]{1,0:T(8,128)S(1)}, u32[]{:S(2)}, u32[]{:S(2)}) collective-permute-start(f32[24,128]{1,0:T(8,128)S(1)} %image.2.own.vector.second), channel_id=1, source_target_pairs={{0,28},{4,0},{8,4},{12,8},{16,12},{20,16},{24,20},{28,24},{1,29},{... | collective-permute-start | bytes 36872 | tf_op jit(solution)/shard_map/ppermute | solution.py:30
  44.3 4.0 %collective-permute-start.12 = (f32[72,128]{1,0:T(8,128)S(1)}, f32[72,128]{1,0:T(8,128)S(1)}, u32[]{:S(2)}, u32[]{:S(2)}) collective-permute-start(f32[72,128]{1,0:T(8,128)S(1)} %pad_maximum_fusion), channel_id=1, source_target_pairs={{0,32},{32,64},{64,96},{96,128},{128,160},{160,192},{192,224},{224... | collective-permute-start | bytes 110600 | tf_op jit(solution)/shard_map/ppermute | solution.py:30
  44.3 4.0 %collective-permute-start.13 = (f32[72,128]{1,0:T(8,128)S(1)}, f32[72,128]{1,0:T(8,128)S(1)}, u32[]{:S(2)}, u32[]{:S(2)}) collective-permute-start(f32[72,128]{1,0:T(8,128)S(1)} %pad_maximum_fusion), channel_id=1, source_target_pairs={{0,224},{32,0},{64,32},{96,64},{128,96},{160,128},{192,160},{224,1... | collective-permute-start | bytes 110600 | tf_op jit(solution)/shard_map/ppermute | solution.py:30
  51.1 5.0 %collective-permute-start.14 = (f32[24,128]{1,0:T(8,128)S(1)}, f32[24,128]{1,0:T(8,128)S(1)}, u32[]{:S(2)}, u32[]{:S(2)}) collective-permute-start(f32[24,128]{1,0:T(8,128)S(1)} %image.3.own.third), channel_id=1, source_target_pairs={{0,4},{4,8},{8,12},{12,16},{16,20},{20,24},{24,28},{28,0},{1,5},{5... | collective-permute-start | bytes 36872 | tf_op jit(solution)/shard_map/ppermute | solution.py:30
  52.3 4.0 %collective-permute-start.15 = (f32[24,128]{1,0:T(8,128)S(1)}, f32[24,128]{1,0:T(8,128)S(1)}, u32[]{:S(2)}, u32[]{:S(2)}) collective-permute-start(f32[24,128]{1,0:T(8,128)S(1)} %image.3.own.third), channel_id=1, source_target_pairs={{0,28},{4,0},{8,4},{12,8},{16,12},{20,16},{24,20},{28,24},{1,29},{... | collective-permute-start | bytes 36872 | tf_op jit(solution)/shard_map/ppermute | solution.py:30
  56.3 4.6 %collective-permute-start.16 = (f32[72,128]{1,0:T(8,128)S(1)}, f32[72,128]{1,0:T(8,128)S(1)}, u32[]{:S(2)}, u32[]{:S(2)}) collective-permute-start(f32[72,128]{1,0:T(8,128)S(1)} %pad_maximum_fusion.1), channel_id=1, source_target_pairs={{0,32},{32,64},{64,96},{96,128},{128,160},{160,192},{192,224},{224... | collective-permute-start | bytes 110600 | tf_op jit(solution)/shard_map/ppermute | solution.py:30
  56.3 4.6 %collective-permute-start.17 = (f32[72,128]{1,0:T(8,128)S(1)}, f32[72,128]{1,0:T(8,128)S(1)}, u32[]{:S(2)}, u32[]{:S(2)}) collective-permute-start(f32[72,128]{1,0:T(8,128)S(1)} %pad_maximum_fusion.1), channel_id=1, source_target_pairs={{0,224},{32,0},{64,32},{96,64},{128,96},{160,128},{192,160},{224,1... | collective-permute-start | bytes 110600 | tf_op jit(solution)/shard_map/ppermute | solution.py:30

commit v4 on v3

--- a/solution.py
+++ b/solution.py
@@ -43,14 +43,22 @@
     return lax.dot_general(left, right, (((1,), (0,)), ((), ())), preferred_element_type=F32)
 
 
-def delta_rows(extent, cell, fraction):
+def delta_weights(fraction):
+    def inner(radius):
+        return (3.0 - 2.0 * radius + jnp.sqrt(jnp.maximum(1.0 + 4.0 * radius - 4.0 * radius * radius, 0.0))) / 8.0
+
+    def outer(radius):
+        return (5.0 - 2.0 * radius - jnp.sqrt(jnp.maximum(-7.0 + 12.0 * radius - 4.0 * radius * radius, 0.0))) / 8.0
+
+    return [outer(1.0 + fraction), inner(fraction), inner(1.0 - fraction), outer(2.0 - fraction)]
+
+
+def delta_rows(extent, cell, weights, at):
     step = lax.broadcasted_iota(jnp.int32, (extent, cell.shape[1]), 0).astype(F32) - cell
-    radius = jnp.abs(step - fraction)
-    near = (step == 0.0) | (step == 1.0)
-    far = (step == -1.0) | (step == 2.0)
-    inner = (3.0 - 2.0 * radius + jnp.sqrt(jnp.maximum(1.0 + 4.0 * radius - 4.0 * radius * radius, 0.0))) / 8.0
-    outer = (5.0 - 2.0 * radius - jnp.sqrt(jnp.maximum(-7.0 + 12.0 * radius - 4.0 * radius * radius, 0.0))) / 8.0
-    return jnp.where(near, inner, jnp.where(far, outer, 0.0))
+    value = jnp.zeros_like(step)
+    for place, weight in zip((-1.0, 0.0, 1.0, 2.0), weights):
+        value = jnp.where(step == place, weight[at : at + 1], value)
+    return value
 
 
 def pack_kernel(
@@ -131,15 +139,19 @@
             piece = pltpu.roll(piece, 32 * field, 1) if field else piece
             packed = jnp.where((lane64 >= 32 * field) & (lane64 < 32 * field + 32), piece, packed)
     wide[256:320, :] = packed
-    for at in range(40):
-        upward[at * 2 : at * 2 + 2, :] = wide[at * 8 + 6 : at * 8 + 8, :]
-        downward[at * 3 : at * 3 + 3, :] = wide[at * 8 : at * 8 + 3, :]
+    for at in range(24):
+        upward[at : at + 1, :] = wide[at * 8 + 7 : at * 8 + 8, :]
+        downward[at * 2 : at * 2 + 2, :] = wide[at * 8 : at * 8 + 2, :]
+    for at in range(16):
+        row = 192 + at * 8
+        upward[24 + at * 2 : 26 + at * 2, :] = wide[row + 6 : row + 8, :]
+        downward[48 + at * 3 : 51 + at * 3, :] = wide[row : row + 3, :]
     halo = below[32:80, :] + above[32:80, :]
-    marks[0:16, :] = own[0:16, :]
-    marks[16:40, :] = halo[0:24]
-    marks[40:48, :] = jnp.broadcast_to(halo[44:45], (8, 128))
-    upward[80:128, :] = marks[...]
-    downward[120:168, :] = marks[...]
+    marks[0:12, :] = own[0:12, :]
+    marks[12:36, :] = halo[0:24]
+    marks[36:40, :] = jnp.broadcast_to(halo[44:45], (4, 128))
+    upward[56:96, :] = marks[...]
+    downward[96:136, :] = marks[...]
     aux[...] = jnp.zeros((72, 128), F32)
     for kind in range(3):
         for c in range(3):
@@ -153,26 +165,37 @@
 def deepen_y_kernel(wide, marks, below, above, deep, three, upward, downward):
     for at in range(40):
         row = at * YPAD
-        deep[row : row + 2, :] = below[at * 2 : at * 2 + 2, :]
         deep[row + 2 : row + 10, :] = wide[at * 8 : at * 8 + 8, :]
-        deep[row + 10 : row + 13, :] = above[at * 3 : at * 3 + 3, :]
-        deep[row + 13 : row + 16, :] = jnp.ones((3, 128), F32)
+        if at < 24:
+            deep[row : row + 1, :] = jnp.ones((1, 128), F32)
+            deep[row + 1 : row + 2, :] = below[at : at + 1, :]
+            deep[row + 10 : row + 12, :] = above[at * 2 : at * 2 + 2, :]
+            deep[row + 12 : row + 16, :] = jnp.ones((4, 128), F32)
+        else:
+            near, far = 24 + (at - 24) * 2, 48 + (at - 24) * 3
+            deep[row : row + 2, :] = below[near : near + 2, :]
+            deep[row + 10 : row + 13, :] = above[far : far + 3, :]
+            deep[row + 13 : row + 16, :] = jnp.ones((3, 128), F32)
     for c in range(3):
-        upward[c * 16 : c * 16 + 16, :] = deep[c * 128 + 112 : c * 128 + 128, :]
-        downward[c * 32 : c * 32 + 32, :] = deep[c * 128 : c * 128 + 32, :]
+        upward[c * 13 : c * 13 + 13, :] = deep[c * 128 + 112 : c * 128 + 125, :]
+        for k in range(2):
+            row = c * 128 + k * YPAD
+            downward[c * 26 + k * 13 : c * 26 + k * 13 + 13, :] = deep[row : row + 13, :]
     for at in range(2):
         row = (3 + at) * 128
-        upward[48 + at * 32 : 80 + at * 32, :] = deep[row + 96 : row + 128, :]
-        downward[96 + at * 48 : 144 + at * 48, :] = deep[row : row + 48, :]
-    three[0:48, :] = marks[...]
-    three[48:96, :] = below[80:128, :]
-    three[96:144, :] = above[120:168, :]
-    upward[112:256, :] = three[...]
-    downward[192:336, :] = three[...]
+        for k in range(3):
+            if k < 2:
+                upward[39 + at * 26 + k * 13 : 52 + at * 26 + k * 13, :] = deep[row + 96 + k * 16 : row + 109 + k * 16, :]
+            downward[78 + at * 39 + k * 13 : 91 + at * 39 + k * 13, :] = deep[row + k * 16 : row + k * 16 + 13, :]
+    three[0:40, :] = marks[...]
+    three[40:80, :] = below[56:96, :]
+    three[80:120, :] = above[96:136, :]
+    upward[96:216, :] = three[...]
+    downward[160:280, :] = three[...]
 
 
 def blocks_used(refs):
-    most = jnp.max(jnp.concatenate([ref[first + 40 + 48 * part : first + 41 + 48 * part, :] for ref, first in refs for part in range(3)], axis=0))
+    most = jnp.max(jnp.concatenate([ref[first + 36 + 40 * part : first + 37 + 40 * part, :] for ref, first in refs for part in range(3)], axis=0))
     return (most.astype(jnp.int32) + 63) >> 6
 
 
@@ -182,23 +205,25 @@
 
 def fill_tables(ref, first, along_x, used, plane_weights, z_high, z_low):
     def fill(read, along_y, place):
-        plane_weights[0:16, place] = delta_rows(16, read(0) + (along_x + 2.0), read(3))
-        plane_weights[16:32, place] = delta_rows(16, read(1) + (along_y + 2.0), read(4))
-        high, rest = halves(delta_rows(160, read(2) + 16.0, read(5)))
+        fractions = jnp.concatenate([read(3), read(4), read(5), jnp.zeros((5, 128), F32)], axis=0)
+        weights = delta_weights(fractions)
+        plane_weights[0:16, place] = delta_rows(16, read(0) + (along_x + 2.0), weights, 0)
+        plane_weights[16:32, place] = delta_rows(16, read(1) + (along_y + 2.0), weights, 1)
+        high, rest = halves(delta_rows(160, read(2) + 16.0, weights, 2))
         z_high[0:160, place] = high
         z_low[0:160, place] = rest
 
     for part, along_y in enumerate((0.0, -8.0, 8.0)):
-        top = first + 48 * part
+        top = first + 40 * part
         for half in range(2):
             column = part * 256 + half * 128
             fill(lambda k: ref[top + 2 * k + half : top + 2 * k + half + 1, :], along_y, slice(column, column + 128))
         column = FIRST + part * 128
-        fill(lambda k: ref[top + 16 + 4 * k : top + 17 + 4 * k, :], along_y, slice(column, column + 128))
+        fill(lambda k: ref[top + 12 + 4 * k : top + 13 + 4 * k, :], along_y, slice(column, column + 128))
 
     def further(block, carry):
         for part, along_y in enumerate((0.0, -8.0, 8.0)):
-            top = first + 48 * part + 16 + block
+            top = first + 40 * part + 12 + block
             column = pl.multiple_of(STATIC + (block - 1) * 384 + part * 128, 128)
             fill(lambda k: ref[pl.ds(top + 4 * k, 1), :], along_y, pl.ds(column, 128))
         return carry
@@ -215,22 +240,23 @@
 
 
 def side_tables_kernel(below, above, b_weights, b_high, b_low, a_weights, a_high, a_low, used):
-    count = blocks_used([(below, 112), (above, 192)])
+    count = blocks_used([(below, 96), (above, 160)])
     used[...] = jnp.full((8, 128), count, jnp.int32)
-    fill_tables(below, 112, -8.0, count, b_weights, b_high, b_low)
-    fill_tables(above, 192, 8.0, count, a_weights, a_high, a_low)
-
-
-def interpolate(velocity_high, velocity_low, plane_weights, z_high, z_low, used, image):
+    fill_tables(below, 96, -8.0, count, b_weights, b_high, b_low)
+    fill_tables(above, 160, 8.0, count, a_weights, a_high, a_low)
+
+
+def interpolate(velocity_high, velocity_low, planes, plane_weights, z_high, z_low, used, image):
     def lines(place):
         partial = plain_dot(velocity_high[...], z_high[:, place]) + plain_dot(velocity_low[...], z_high[:, place])
         partial = partial + plain_dot(velocity_high[...], z_low[:, place])
         result = []
         for c in range(3):
-            total = partial[c * INNER : c * INNER + YPAD] * plane_weights[1:2, place]
-            for plane in range(1, 11):
-                row = c * INNER + plane * YPAD
-                total = total + partial[row : row + YPAD] * plane_weights[plane + 1 : plane + 2, place]
+            total = None
+            for at, plane in enumerate(planes):
+                row = (c * len(planes) + at) * YPAD
+                term = partial[row : row + YPAD] * plane_weights[plane : plane + 1, place]
+                total = term if total is None else total + term
             result.append(jnp.sum(total * plane_weights[16:32, place], axis=0, keepdims=True))
         return result
 
@@ -251,19 +277,20 @@
 
 def setup_kernel(deep, below, above, plane_weights, z_high, z_low, aux, used, scale, start, velocity_high, velocity_low, image):
     lane = lax.broadcasted_iota(jnp.int32, (YPAD, 128), 1)
+    used_rows = lax.broadcasted_iota(jnp.int32, (YPAD, 128), 0) < 13
     for plane in range(PLANES):
         at = plane * YPAD
 
         def piece(field):
             if plane < 2:
-                row = field * 16 if field < 3 else 48 + (field - 3) * 32 + plane * 16
-                return below[row : row + 16, :]
+                row = field * 13 if field < 3 else 39 + (field - 3) * 26 + plane * 13
+                return jnp.where(used_rows, below[row : row + 16, :], 1.0)
             if plane < 10:
                 row = field * 128 + (plane - 2) * 16
                 return deep[row : row + 16, :]
-            row = field * 32 if field < 3 else 96 + (field - 3) * 48
-            row += (plane - 10) * 16
-            return above[row : row + 16, :]
+            row = field * 26 if field < 3 else 78 + (field - 3) * 39
+            row += (plane - 10) * 13
+            return jnp.where(used_rows, above[row : row + 16, :], 1.0)
 
         packed = piece(4)
         scale[at : at + YPAD, 0:128] = lax.rsqrt(piece(3))
@@ -278,7 +305,7 @@
                 top, rest = halves(jnp.where(lane < 32, beyond, 0.0))
                 velocity_high[row : row + YPAD, 128:256] = top
                 velocity_low[row : row + YPAD, 128:256] = rest
-    interpolate(velocity_high, velocity_low, plane_weights, z_high, z_low, trips(used), image)
+    interpolate(velocity_high, velocity_low, range(1, 12), plane_weights, z_high, z_low, trips(used), image)
     start[...] = aux[0:24, :] * (aux[48:72, :] - image[...])
 
 
@@ -299,68 +326,52 @@
     return total + transposed_dot(left_high[:, left], z_low[:, right])
 
 
-def spread_group(refs, planes, plane_weights, z_high, z_low, used, left_high, left_low, total):
-    for part, (ref, first) in enumerate(refs):
+def spread_group(refs, planes, plane_weights, z_high, z_low, used, left_high, left_low, total, begun=None, part0=0):
+    count = len(refs)
+    for at, (ref, first) in enumerate(refs):
+        part = part0 + at
         for half in range(2):
-            place = slice(part * 256 + half * 128, part * 256 + half * 128 + 128)
+            place = slice(at * 256 + half * 128, at * 256 + half * 128 + 128)
+            weight = slice(part * 256 + half * 128, part * 256 + half * 128 + 128)
             rows = [ref[first + 2 * c + half : first + 2 * c + half + 1, :] for c in range(3)]
-            fill_tile(rows, planes, plane_weights, place, left_high, left_low, place)
-        place = slice(FIRST + part * 128, FIRST + part * 128 + 128)
+            fill_tile(rows, planes, plane_weights, weight, left_high, left_low, place)
+        place = slice(count * 256 + at * 128, count * 256 + at * 128 + 128)
+        weight = slice(FIRST + part * 128, FIRST + part * 128 + 128)
         rows = [ref[first + 8 + c : first + 9 + c, :] for c in range(3)]
-        fill_tile(rows, planes, plane_weights, place, left_high, left_low, place)
-    whole = slice(0, STATIC)
-    total[...] = spread_columns(left_high, left_low, z_high, z_low, whole, whole)
+        fill_tile(rows, planes, plane_weights, weight, left_high, left_low, place)
+    value = spread_columns(
+        left_high, left_low, z_high, z_low, slice(0, count * 256), slice(part0 * 256, (part0 + count) * 256)
+    )
+    value = value + spread_columns(
+        left_high, left_low, z_high, z_low, slice(count * 256, count * 384),
+        slice(FIRST + part0 * 128, FIRST + (part0 + count) * 128),
+    )
+    total[...] = value if begun is None else value + begun[...]
 
     def further(block, carry):
-        for part, (ref, first) in enumerate(refs):
-            column = pl.multiple_of(STATIC + (block - 1) * 384 + part * 128, 128)
+        for at, (ref, first) in enumerate(refs):
+            column = pl.multiple_of(STATIC + (block - 1) * 384 + (part0 + at) * 128, 128)
             rows = [ref[pl.ds(first + 8 + 3 * block + c, 1), :] for c in range(3)]
-            place = slice(part * 128, part * 128 + 128)
+            place = slice(at * 128, at * 128 + 128)
             fill_tile(rows, planes, plane_weights, pl.ds(column, 128), left_high, left_low, place)
-        right = pl.ds(pl.multiple_of(STATIC + (block - 1) * 384, 128), 384)
-        total[...] += spread_columns(left_high, left_low, z_high, z_low, slice(0, 384), right)
+        right = pl.ds(pl.multiple_of(STATIC + (block - 1) * 384 + part0 * 128, 128), count * 128)
+        total[...] += spread_columns(left_high, left_low, z_high, z_low, slice(0, count * 128), right)
         return carry
 
     lax.fori_loop(1, used, further, 0)
 
 
-def own_spread_kernel(own, below, above, plane_weights, z_high, z_low, used, moved, left_high, left_low):
-    refs = [(own, 0), (below, 0), (above, 0)]
-    spread_group(refs, range(1, 12), plane_weights, z_high, z_low, trips(used), left_high, left_low, moved)
-
-
-def apply_image(
-    moved, below, above, own_tables, own_used, side_tables, side_used, scale, aux, vector,
-    left_high, left_low, first, final, field, velocity_high, velocity_low, image,
-):
-    refs = [[(ref, 24 * part) for part in range(3)] for ref in (below, above)]
-    spread_group(refs[0], range(0, 4), *side_tables[0:3], trips(side_used), left_high.at[0], left_low.at[0], first)
-    spread_group(refs[1], range(9, 13), *side_tables[3:6], trips(side_used), left_high.at[1], left_low.at[1], final)
-    for c in range(3):
-        for plane in range(PLANES):
-            parts = []
-            if 1 <= plane <= 11:
-                row = c * INNER + (plane - 1) * YPAD
-                parts.append(moved[row : row + YPAD, :])
-            if plane < 4:
-                row = c * 64 + plane * YPAD
-                parts.append(first[row : row + YPAD, :])
-            if plane >= 9:
-                row = c * 64 + (plane - 9) * YPAD
-                parts.append(final[row : row + YPAD, :])
-            total = parts[0] if len(parts) == 1 else parts[0] + parts[1]
-            row = c * ROWS + plane * YPAD
-            field[row : row + YPAD, :] = total * scale[plane * YPAD : plane * YPAD + YPAD, :]
+def respond(moved, planes, outs, scale, velocity_high, velocity_low):
     axial, diagonal = 1.0 / 6.0, 1.0 / 12.0
     up_y = lambda a: pltpu.roll(a, 1, 0)
     down_y = lambda a: pltpu.roll(a, YPAD - 1, 0)
     up_z = lambda a: pltpu.roll(a, 1, 1)
     down_z = lambda a: pltpu.roll(a, LANES - 1, 1)
-    onward = [None] * PLANES
-    back = [None] * PLANES
-    still = [None] * PLANES
-    for plane in range(PLANES):
-        gx, gy, gz = (field[c * ROWS + plane * YPAD : c * ROWS + plane * YPAD + YPAD, :] for c in range(3))
+    onward, back, still = {}, {}, {}
+    for at, plane in enumerate(planes):
+        factor = scale[plane * YPAD : plane * YPAD + YPAD, :]
+        rows = [(c * len(planes) + at) * YPAD for c in range(3)]
+        gx, gy, gz = (moved[row : row + YPAD, :] * factor for row in rows)
         hx, hy, hz = gx * diagonal, gy * diagonal, gz * diagonal
         sum_xy, dif_xy = hx + hy, hx - hy
         zx_up, zy_up, zz_up = up_z(hx), up_z(hy), up_z(hz)
@@ -388,26 +399,60 @@
             gy + ((up_y(hy) + down_y(hy)) * 2.0 + (same + cross)),
             gz + ((zz_up + zz_dn) * 2.0 + (same - cross)),
         )
-        if plane >= 2:
-            out = plane - 1
+        for place, out in enumerate(outs):
+            if min(out + 1, planes[-1]) != plane:
+                continue
             factor = scale[out * YPAD : out * YPAD + YPAD, :] * 0.5
-            first = (out - 1) * YPAD
             for c in range(3):
-                value = (still[out][c] + (onward[out - 1][c] + back[out + 1][c])) * factor
-                top, rest = halves(value)
-                row = c * INNER + first
+                parts = [group[at][c] for group, at in ((onward, out - 1), (still, out), (back, out + 1)) if at in group]
+                total = parts[0]
+                for part in parts[1:]:
+                    total = total + part
+                top, rest = halves(total * factor)
+                row = (c * len(outs) + place) * YPAD
                 velocity_high[row : row + YPAD, :] = top
                 velocity_low[row : row + YPAD, :] = rest
-    interpolate(velocity_high, velocity_low, *own_tables, trips(own_used), image)
-    return aux[0:24, :] * (image[...] + aux[24:48, :] * vector[...])
-
-
-def image_kernel(
-    moved, below, above, w, h, l, own_used, bw, bh, bl, aw, ah, al, side_used, scale, aux, vector, result, *scratch
+
+
+def own_spread(own, plane_weights, z_high, z_low, used, total, left_high, left_low):
+    spread_group([(own, 0)], range(1, 12), plane_weights, z_high, z_low, trips(used), left_high, left_low, total)
+
+
+def own_image(
+    begun, below, above, plane_weights, z_high, z_low, used, scale, result, left_high, left_low, moved, velocity_high,
+    velocity_low,
 ):
-    result[...] = apply_image(
-        moved, below, above, (w, h, l), own_used, (bw, bh, bl, aw, ah, al), side_used, scale, aux, vector, *scratch
-    )
+    refs = [(below, 0), (above, 0)]
+    planes = range(1, 12)
+    count = trips(used)
+    spread_group(refs, planes, plane_weights, z_high, z_low, count, left_high, left_low, moved, begun, 1)
+    respond(moved, planes, planes, scale, velocity_high, velocity_low)
+    interpolate(velocity_high, velocity_low, planes, plane_weights, z_high, z_low, count, result)
+
+
+def side_image(
+    below, begun, three, own_tables, own_used, side_tables, used, scale, left_high, left_low, moved, velocity_high,
+    velocity_low, image,
+):
+    planes, outs = (range(0, 4), range(1, 5)) if below else (range(9, 13), range(8, 12))
+    refs = [(three, 24 * part) for part in range(3)]
+    spread_group(refs, planes, *side_tables, trips(used), left_high, left_low, moved)
+    respond(moved, planes, outs, scale, velocity_high, velocity_low)
+    interpolate(velocity_high, velocity_low, outs, *own_tables, trips(own_used), image)
+    return begun[...] + image[...]
+
+
+def below_kernel(begun, three, w, h, l, own_used, sw, sh, sl, used, scale, result, *scratch):
+    result[...] = side_image(True, begun, three, (w, h, l), own_used, (sw, sh, sl), used, scale, *scratch)
+
+
+def above_image(begun, three, w, h, l, own_used, sw, sh, sl, used, scale, aux, vector, *scratch):
+    image = side_image(False, begun, three, (w, h, l), own_used, (sw, sh, sl), used, scale, *scratch)
+    return aux[0:24, :] * (image + aux[24:48, :] * vector[...])
+
+
+def above_kernel(begun, three, w, h, l, own_used, sw, sh, sl, used, scale, aux, vector, result, *scratch):
+    result[...] = above_image(begun, three, w, h, l, own_used, sw, sh, sl, used, scale, aux, vector, *scratch)
 
 
 def two_sum(a, b):
@@ -457,22 +502,34 @@
 ENTRIES = ((0, 0), (0, 1), (0, 2), (0, 3), (1, 1), (1, 2), (1, 3), (2, 2), (2, 3))
 
 
-def last_kernel(
-    moved, below, above, w, h, l, own_used, bw, bh, bl, aw, ah, al, side_used, scale, aux, third, first, second, sums,
-    *scratch
-):
-    fourth = apply_image(
-        moved, below, above, (w, h, l), own_used, (bw, bh, bl, aw, ah, al), side_used, scale, aux, third, *scratch
-    )
-    vectors = [first[0:8, :], second[0:8, :], third[0:8, :], fourth[0:8]]
+def gram_lanes(vectors, entries, packed):
     lane = lax.broadcasted_iota(jnp.int32, (8, 128), 1)
-    packed = jnp.zeros((8, 128), F32)
     for at, (i, j) in enumerate(ENTRIES):
+        if (i, j) not in entries:
+            continue
         value = two_product(vectors[i], vectors[j])
         for axis, steps in ((0, (4, 2, 1)), (1, (64, 32, 16, 8, 4, 2, 1))):
             for step in steps:
                 value = pair_add(value, (pltpu.roll(value[0], step, axis), pltpu.roll(value[1], step, axis)))
         packed = jnp.where(lane == at, value[0], jnp.where(lane == 16 + at, value[1], packed))
+    return packed
+
+
+EARLY = tuple(entry for entry in ENTRIES if entry[1] < 3)
+LATE = tuple(entry for entry in ENTRIES if entry[1] == 3)
+
+
+def own_spread_last(own, w, h, l, used, first, second, total, early, *scratch):
+    own_spread(own, w, h, l, used, total, *scratch)
+    early[...] = gram_lanes([first[0:8, :], second[0:8, :], own[0:8, :]], EARLY, jnp.zeros((8, 128), F32))
+
+
+def last_kernel(
+    begun, three, w, h, l, own_used, sw, sh, sl, used, scale, aux, third, first, second, early, sums, *scratch
+):
+    fourth = above_image(begun, three, w, h, l, own_used, sw, sh, sl, used, scale, aux, third, *scratch)
+    vectors = [first[0:8, :], second[0:8, :], third[0:8, :], fourth[0:8]]
+    packed = gram_lanes(vectors, LATE, early[...])
     for block in range(sums.shape[0] // 8):
         sums[block * 8 : block * 8 + 8, :] = packed
 
@@ -560,11 +617,11 @@
     )
     below, above = shifted(to_above, "gz", 1), shifted(to_below, "gz", -1)
     wide, marks, aux, upward, downward = call(
-        deepen_z_kernel, "deepen_z", [rows(320), rows(48), rows(72), rows(128), rows(168)], fields, own, below, above
+        deepen_z_kernel, "deepen_z", [rows(320), rows(40), rows(72), rows(96), rows(136)], fields, own, below, above
     )
     below, above = shifted(upward, GY, 1), shifted(downward, GY, -1)
     deep, three, upward, downward = call(
-        deepen_y_kernel, "deepen_y", [rows(640), rows(144), rows(256), rows(336)], wide, marks, below, above
+        deepen_y_kernel, "deepen_y", [rows(640), rows(120), rows(216), rows(280)], wide, marks, below, above
     )
     below, above = shifted(upward, "gx", 1), shifted(downward, "gx", -1)
     own_tables = call(
@@ -573,30 +630,43 @@
     side_tables = call(
         side_tables_kernel, "side_tables", table_shapes * 2 + used_shape, below, above
     )
-    velocity_scratch = [vmem((3 * INNER, LANES), BF16)] * 2 + [vmem((24, 128), F32)]
+    velocity_scratch = [vmem((3 * INNER, LANES), BF16)] * 2
+    image_scratch = vmem((24, 128), F32)
     scale, start = call(
         setup_kernel, "setup", [((ROWS, LANES), F32), rows(24)], deep, below, above, *own_tables[0:3], aux, own_tables[3],
-        scratch=velocity_scratch,
-    )
-
-    def image_of(kernel, name, outs, vector, *others):
+        scratch=velocity_scratch + [image_scratch],
+    )
+
+    def image_of(last, vector, *others):
         below, above = shifted(vector, GY, 1), shifted(vector, GY, -1)
-        three = jnp.concatenate([vector, below, above], axis=0)
+        begun = call(
+            own_spread_last if last else own_spread, "own_spread",
+            [((3 * INNER, LANES), F32)] + ([rows(8)] if last else []), vector, *own_tables, *others,
+            scratch=[vmem((3 * INNER, 384), BF16)] * 2,
+        )
+        held = list(begun) + (list(side_tables) if vector is start else [])
+        three = lax.optimization_barrier((jnp.concatenate([vector, below, above], axis=0), *held))[0]
         below_three, above_three = shifted(three, "gx", 1), shifted(three, "gx", -1)
-        (moved,) = call(
-            own_spread_kernel, "own_spread", [((3 * INNER, LANES), F32)], vector, below, above, *own_tables,
-            scratch=[vmem((3 * INNER, STATIC), BF16)] * 2,
+        (own_part,) = call(
+            own_image, "own_image", [rows(24)], begun[0], below, above, *own_tables, scale,
+            scratch=[vmem((3 * INNER, 768), BF16)] * 2 + [vmem((3 * INNER, LANES), F32)] + velocity_scratch,
+        )
+        side_scratch = [vmem((192, STATIC), BF16)] * 2 + [vmem((192, LANES), F32)]
+        side_scratch += [vmem((192, LANES), BF16)] * 2 + [image_scratch]
+        (part,) = call(
+            below_kernel, "below", [rows(24)], own_part, below_three, *own_tables, *side_tables[0:3], side_tables[6], scale,
+            scratch=side_scratch,
         )
         (result,) = call(
-            kernel, name, outs, moved, below_three, above_three, *own_tables, *side_tables, scale, aux, vector, *others,
-            scratch=[vmem((2, 192, STATIC), BF16)] * 2 + [vmem((192, LANES), F32)] * 2
-            + [vmem((3 * ROWS, LANES), F32)] + velocity_scratch,
+            last_kernel if last else above_kernel, "above", [rows(256 if last else 24)],
+            part, above_three, *own_tables, *side_tables[3:7], scale, aux, vector, *others, *begun[1:],
+            scratch=side_scratch,
         )
         return result
 
-    second = image_of(image_kernel, "image", [rows(24)], start)
-    third = image_of(image_kernel, "image", [rows(24)], second)
-    sums = image_of(last_kernel, "last", [rows(256)], third, start, second)
+    second = image_of(False, start)
+    third = image_of(False, second)
+    sums = image_of(True, third, start, second)
     gathered = lax.all_to_all(sums, GX_GY_GZ, 0, 0, tiled=True)
     (forces,) = call(finish_kernel, "finish", [((3, MARKERS), F32)], gathered, start, second, third)
     return forces

time: 91.3 us -> 87.7 us (0.961)
  waiting for transfers between devices: 11.3 us -> 8.1 us
  blocking collectives: 25.8 us -> 23.7 us
  Pallas kernels: 21 us -> 22.7 us
    ppermute x18, waiting for transfers between devices: 11.3 us -> 8.1 us  [shifted(): lax.ppermute(shard, axis, [(i, (i + by) % length) for i in range(length)])]
    all_to_all x1, blocking collectives: 25.8 us -> 23.7 us  [body(): gathered = lax.all_to_all(sums, GX_GY_GZ, 0, 0, tiled=True)]
    pallas_call x13 -> x19, Pallas kernels: 21 us -> 22.7 us  [call(): pl.pallas_call(kernel, name=name, out_shape=[jax.ShapeDtypeStruct(shape,...]
  transfers between devices with their start and end apart: 18 -> 18, of which waited for: 11 -> 7; matrix products, arithmetic and copies ran while one was open for 0% -> 0% of each run, Pallas kernels for 9% -> 16%
where the time goes in v4:
time: 87.7 us; the launch traced here: 87.5 us
  starting transfers between devices  32.1 us (37%)
  blocking collectives  23.7 us (27%)
  Pallas kernels  22.7 us (26%)
  waiting for transfers between devices  8.1 us (9%)
    ppermute x18, starting transfers between devices, shifted(): lax.ppermute(shard, axis, [(i, (i + by) % length) for i in range(length)])  32.1 us
    all_to_all x1, blocking collectives, body(): gathered = lax.all_to_all(sums, GX_GY_GZ, 0, 0, tiled=True)  23.7 us
    pallas_call x19, Pallas kernels, call(): pl.pallas_call(kernel, name=name, out_shape=[jax.ShapeDtypeStruct(shape,...  22.7 us
    ppermute x18, waiting for transfers between devices, shifted(): lax.ppermute(shard, axis, [(i, (i + by) % length) for i in range(length)])  8.1 us
  transfers between devices with their start and end apart: 18, of which 7 were waited for; matrix products, arithmetic and copies ran while one was open for 0% of the time, Pallas kernels for 16%

profile of v4, /device:TPU:1, one launch (start us, length us, event | category | flops | bytes accessed | tf_op | source)
XLA Modules:
  0.0 87.5 jit_solution(17503291184092217675)
XLA Ops:
  0.7 1.7 %pack.1 = (f32[256,128]{1,0:T(8,128)S(1)}, f32[24,128]{1,0:T(8,128)S(1)}, f32[80,128]{1,0:T(8,128)S(1)}, f32[80,128]{1,0:T(8,128)S(1)}) custom-call(f32[8,8,128]{2,1,0:T(8,128)} %density_in.1, f32[3,8,8,128]{3,2,1,0:T(8,128)} %base_in.1, s32[3,256]{1,0:T(4,128)} %cells_in.1, f32[3,256]{1,0:T(4,128)} %offsets_in.1, f32[3,256]{1,0:T(4,128)} %target_in.1, ...), custom_call_target="tpu_custom_call" | custom-call | tf_op jit(solution)/shard_map/pack/pallas_call | solution.py:591
  2.3 2.1 %collective-permute-start = (f32[80,128]{1,0:T(8,128)S(1)}, f32[80,128]{1,0:T(8,128)S(1)}, u32[]{:S(2)}, u32[]{:S(2)}) collective-permute-start(f32[80,128]{1,0:T(8,128)S(1)} %get-tuple-element.38), channel_id=1, source_target_pairs={{0,1},{1,2},{2,3},{3,0},{4,5},{5,6},{6,7},{7,4},{8,9},{9,10},{10,1... | collective-permute-start | bytes 122888 | tf_op jit(solution)/shard_map/ppermute | solution.py:30
  4.4 1.4 %collective-permute-start.1 = (f32[80,128]{1,0:T(8,128)S(1)}, f32[80,128]{1,0:T(8,128)S(1)}, u32[]{:S(2)}, u32[]{:S(2)}) collective-permute-start(f32[80,128]{1,0:T(8,128)S(1)} %get-tuple-element.39), channel_id=1, source_target_pairs={{0,3},{1,0},{2,1},{3,2},{4,7},{5,4},{6,5},{7,6},{8,11},{9,8},{10,9... | collective-permute-start | bytes 122888 | tf_op jit(solution)/shard_map/ppermute | solution.py:30
  5.8 1.3 %collective-permute-done.below = f32[80,128]{1,0:T(8,128)S(1)} collective-permute-done((f32[80,128]{1,0:T(8,128)S(1)}, f32[80,128]{1,0:T(8,128)S(1)}, u32[]{:S(2)}, u32[]{:S(2)}) %collective-permute-start) | collective-permute-done | bytes 40992 | tf_op jit(solution)/shard_map/ppermute | solution.py:30
  7.6 3.5 %collective-permute-start.3 = (f32[136,128]{1,0:T(8,128)S(1)}, f32[136,128]{1,0:T(8,128)S(1)}, u32[]{:S(2)}, u32[]{:S(2)}) collective-permute-start(f32[136,128]{1,0:T(8,128)S(1)} %get-tuple-element.43), channel_id=1, source_target_pairs={{0,28},{4,0},{8,4},{12,8},{16,12},{20,16},{24,20},{28,24},{1,29},{... | collective-permute-start | bytes 208904 | tf_op jit(solution)/shard_map/ppermute | solution.py:30
  11.2 1.2 %collective-permute-done.2.below = f32[96,128]{1,0:T(8,128)S(1)} collective-permute-done((f32[96,128]{1,0:T(8,128)S(1)}, f32[96,128]{1,0:T(8,128)S(1)}, u32[]{:S(2)}, u32[]{:S(2)}) %collective-permute-start.2) | collective-permute-done | bytes 49184 | tf_op jit(solution)/shard_map/ppermute | solution.py:30
  13.0 5.7 %collective-permute-start.5 = (f32[280,128]{1,0:T(8,128)S(1)}, f32[280,128]{1,0:T(8,128)S(1)}, u32[]{:S(2)}, u32[]{:S(2)}) collective-permute-start(f32[280,128]{1,0:T(8,128)S(1)} %get-tuple-element.46), channel_id=1, source_target_pairs={{0,224},{32,0},{64,32},{96,64},{128,96},{160,128},{192,160},{224,1... | collective-permute-start | bytes 430088 | tf_op jit(solution)/shard_map/ppermute | solution.py:30
  19.3 4.2 %collective-permute-done.4.below = f32[216,128]{1,0:T(8,128)S(1)} collective-permute-done((f32[216,128]{1,0:T(8,128)S(1)}, f32[216,128]{1,0:T(8,128)S(1)}, u32[]{:S(2)}, u32[]{:S(2)}) %collective-permute-start.4) | collective-permute-done | bytes 110624 | tf_op jit(solution)/shard_map/ppermute | solution.py:30
  23.5 0.6 setup.1
  24.1 3.1 %collective-permute-start.6 = (f32[24,128]{1,0:T(8,128)S(1)}, f32[24,128]{1,0:T(8,128)S(1)}, u32[]{:S(2)}, u32[]{:S(2)}) collective-permute-start(f32[24,128]{1,0:T(8,128)S(1)} %get-tuple-element.53.own.vector.first), channel_id=1, source_target_pairs={{0,4},{4,8},{8,12},{12,16},{16,20},{20,24},{24,28},{28,0},{1,5},{5... | collective-permute-start | bytes 36872 | tf_op jit(solution)/shard_map/ppermute | solution.py:30
  27.2 1.0 %collective-permute-start.7 = (f32[24,128]{1,0:T(8,128)S(1)}, f32[24,128]{1,0:T(8,128)S(1)}, u32[]{:S(2)}, u32[]{:S(2)}) collective-permute-start(f32[24,128]{1,0:T(8,128)S(1)} %get-tuple-element.53.own.vector.first), channel_id=1, source_target_pairs={{0,28},{4,0},{8,4},{12,8},{16,12},{20,16},{24,20},{28,24},{1,29},{... | collective-permute-start | bytes 36872 | tf_op jit(solution)/shard_map/ppermute | solution.py:30
  28.1 0.6 own_spread.3.begun
  28.8 1.1 %side_tables.1 = (f32[32,2304]{1,0:T(8,128)S(1)}, bf16[256,2304]{1,0:T(8,128)(2,1)S(1)}, bf16[256,2304]{1,0:T(8,128)(2,1)S(1)}, f32[32,2304]{1,0:T(8,128)S(1)}, ...) custom-call(f32[216,128]{1,0:T(8,128)S(1)} %collective-permute-done.4.below, ...), custom_call_target="tpu_custom_call" | custom-call | tf_op jit(solution)/shard_map/side_tables/pallas_call | solution.py:591
  30.3 2.7 %collective-permute-start.9 = (f32[72,128]{1,0:T(8,128)S(1)}, f32[72,128]{1,0:T(8,128)S(1)}, u32[]{:S(2)}, u32[]{:S(2)}) collective-permute-start(f32[72,128]{1,0:T(8,128)S(1)} %pad_maximum_fusion), channel_id=1, source_target_pairs={{0,224},{32,0},{64,32},{96,64},{128,96},{160,128},{192,160},{224,1... | collective-permute-start | bytes 110600 | tf_op jit(solution)/shard_map/ppermute | solution.py:30
  33.0 2.2 %own_image.3.begun = f32[24,128]{1,0:T(8,128)S(1)} custom-call(f32[528,256]{1,0:T(8,128)S(1)} %own_spread.3.begun, f32[24,128]{1,0:T(8,128)S(1)} %collective-permute-done.6.below, f32[24,128]{1,0:T(8,128)S(1)} %collective-permute-done.7.above, f32[32,2304]{1,0:T(8,128)S(1)} %get-tuple-element.48.plane_weights.w, ...), custom_call_target="tpu_custom_call" | custom-call | tf_op jit(solution)/shard_map/own_image/pallas_call | solution.py:591
  35.2 1.3 %below.3.begun = f32[24,128]{1,0:T(8,128)S(1)} custom-call(f32[24,128]{1,0:T(8,128)S(1)} %own_image.3.begun, f32[72,128]{1,0:T(8,128)S(1)} %collective-permute-done.8.three, f32[32,2304]{1,0:T(8,128)S(1)} %get-tuple-element.48.plane_weights.w, bf16[256,2304]{1,0:T(8,128)(2,1)S(1)} %get-tuple-element.49.z_high.h, ...), custom_call_target="tpu_custom_call" | custom-call | tf_op jit(solution)/shard_map/below/pallas_call | solution.py:591
  36.5 1.3 %above.3.own.vector.second = f32[24,128]{1,0:T(8,128)S(1)} custom-call(f32[24,128]{1,0:T(8,128)S(1)} %below.3.begun, f32[72,128]{1,0:T(8,128)S(1)} %collective-permute-done.9.three, f32[32,2304]{1,0:T(8,128)S(1)} %get-tuple-element.48.plane_weights.w, bf16[256,2304]{1,0:T(8,128)(2,1)S(1)} %get-tuple-element.49.z_high.h, ...), custom_call_target="tpu_custom_call" | custom-call | tf_op jit(solution)/shard_map/above/pallas_call | solution.py:591
  37.8 1.1 %collective-permute-start.10 = (f32[24,128]{1,0:T(8,128)S(1)}, f32[24,128]{1,0:T(8,128)S(1)}, u32[]{:S(2)}, u32[]{:S(2)}) collective-permute-start(f32[24,128]{1,0:T(8,128)S(1)} %above.3.own.vector.second), channel_id=1, source_target_pairs={{0,4},{4,8},{8,12},{12,16},{16,20},{20,24},{24,28},{28,0},{1,5},{5... | collective-permute-start | bytes 36872 | tf_op jit(solution)/shard_map/ppermute | solution.py:30
  38.8 2.2 %collective-permute-start.11 = (f32[24,128]{1,0:T(8,128)S(1)}, f32[24,128]{1,0:T(8,128)S(1)}, u32[]{:S(2)}, u32[]{:S(2)}) collective-permute-start(f32[24,128]{1,0:T(8,128)S(1)} %above.3.own.vector.second), channel_id=1, source_target_pairs={{0,28},{4,0},{8,4},{12,8},{16,12},{20,16},{24,20},{28,24},{1,29},{... | collective-permute-start | bytes 36872 | tf_op jit(solution)/shard_map/ppermute | solution.py:30
  42.0 2.7 %collective-permute-start.13 = (f32[72,128]{1,0:T(8,128)S(1)}, f32[72,128]{1,0:T(8,128)S(1)}, u32[]{:S(2)}, u32[]{:S(2)}) collective-permute-start(f32[72,128]{1,0:T(8,128)S(1)} %pad_maximum_fusion.1), channel_id=1, source_target_pairs={{0,224},{32,0},{64,32},{96,64},{128,96},{160,128},{192,160},{224,1... | collective-permute-start | bytes 110600 | tf_op jit(solution)/shard_map/ppermute | solution.py:30
  44.6 2.0 %own_image.4.begun = f32[24,128]{1,0:T(8,128)S(1)} custom-call(f32[528,256]{1,0:T(8,128)S(1)} %own_spread.4.begun, f32[24,128]{1,0:T(8,128)S(1)} %collective-permute-done.10.below, f32[24,128]{1,0:T(8,128)S(1)} %collective-permute-done.11.above, f32[32,2304]{1,0:T(8,128)S(1)} %get-tuple-element.48.plane_weights.w, ...), custom_call_target="tpu_custom_call" | custom-call | tf_op jit(solution)/shard_map/own_image/pallas_call | solution.py:591
  46.7 1.3 %below.4.begun = f32[24,128]{1,0:T(8,128)S(1)} custom-call(f32[24,128]{1,0:T(8,128)S(1)} %own_image.4.begun, f32[72,128]{1,0:T(8,128)S(1)} %collective-permute-done.12.three, f32[32,2304]{1,0:T(8,128)S(1)} %get-tuple-element.48.plane_weights.w, bf16[256,2304]{1,0:T(8,128)(2,1)S(1)} %get-tuple-element.49.z_high.h, ...), custom_call_target="tpu_custom_call" | custom-call | tf_op jit(solution)/shard_map/below/pallas_call | solution.py:591
  48.0 1.3 %above.4.own.third = f32[24,128]{1,0:T(8,128)S(1)} custom-call(f32[24,128]{1,0:T(8,128)S(1)} %below.4.begun, f32[72,128]{1,0:T(8,128)S(1)} %collective-permute-done.13.three, f32[32,2304]{1,0:T(8,128)S(1)} %get-tuple-element.48.plane_weights.w, bf16[256,2304]{1,0:T(8,128)(2,1)S(1)} %get-tuple-element.49.z_high.h, ...), custom_call_target="tpu_custom_call" | custom-call | tf_op jit(solution)/shard_map/above/pallas_call | solution.py:591
  49.3 0.6 collective-permute-start.14
  49.9 3.4 %collective-permute-start.15 = (f32[24,128]{1,0:T(8,128)S(1)}, f32[24,128]{1,0:T(8,128)S(1)}, u32[]{:S(2)}, u32[]{:S(2)}) collective-permute-start(f32[24,128]{1,0:T(8,128)S(1)} %above.4.own.third), channel_id=1, source_target_pairs={{0,28},{4,0},{8,4},{12,8},{16,12},{20,16},{24,20},{28,24},{1,29},{... | collective-permute-start | bytes 36872 | tf_op jit(solution)/shard_map/ppermute | solution.py:30
  53.3 1.2 %own_spread.5 = (f32[528,256]{1,0:T(8,128)S(1)}, f32[8,128]{1,0:T(8,128)S(1)}) custom-call(f32[24,128]{1,0:T(8,128)S(1)} %above.4.own.third, f32[32,2304]{1,0:T(8,128)S(1)} %get-tuple-element.48.plane_weights.w, bf16[256,2304]{1,0:T(8,128)(2,1)S(1)} %get-tuple-element.49.z_high.h, bf16[256,2304]{1,0:T(8,128)(2,1)S(1)} %get-tuple-element.50.z_low.l, ...), custom_call_target="tpu_custom_call" | custom-call | tf_op jit(solution)/shard_map/own_spread/pallas_call | solution.py:591
  54.7 2.7 %collective-permute-start.17 = (f32[72,128]{1,0:T(8,128)S(1)}, f32[72,128]{1,0:T(8,128)S(1)}, u32[]{:S(2)}, u32[]{:S(2)}) collective-permute-start(f32[72,128]{1,0:T(8,128)S(1)} %pad_maximum_fusion.2), channel_id=1, source_target_pairs={{0,224},{32,0},{64,32},{96,64},{128,96},{160,128},{192,160},{224,1... | collective-permute-start | bytes 110600 | tf_op jit(solution)/shard_map/ppermute | solution.py:30
  57.3 2.0 %own_image.5.begun = f32[24,128]{1,0:T(8,128)S(1)} custom-call(f32[528,256]{1,0:T(8,128)S(1)} %get-tuple-element.64.begun, f32[24,128]{1,0:T(8,128)S(1)} %collective-permute-done.14.below, f32[24,128]{1,0:T(8,128)S(1)} %collective-permute-done.15.above, f32[32,2304]{1,0:T(8,128)S(1)} %get-tuple-element.48.plane_weights.w, ...), custom_call_target="tpu_custom_call" | custom-call | tf_op jit(solution)/shard_map/own_image/pallas_call | solution.py:591
  59.4 1.3 %below.5.begun = f32[24,128]{1,0:T(8,128)S(1)} custom-call(f32[24,128]{1,0:T(8,128)S(1)} %own_image.5.begun, f32[72,128]{1,0:T(8,128)S(1)} %collective-permute-done.16.three, f32[32,2304]{1,0:T(8,128)S(1)} %get-tuple-element.48.plane_weights.w, bf16[256,2304]{1,0:T(8,128)(2,1)S(1)} %get-tuple-element.49.z_high.h, ...), custom_call_target="tpu_custom_call" | custom-call | tf_op jit(solution)/shard_map/below/pallas_call | solution.py:591
  60.7 1.9 %above.5 = f32[256,128]{1,0:T(8,128)S(1)} custom-call(f32[24,128]{1,0:T(8,128)S(1)} %below.5.begun, f32[72,128]{1,0:T(8,128)S(1)} %collective-permute-done.17.three, f32[32,2304]{1,0:T(8,128)S(1)} %get-tuple-element.48.plane_weights.w, bf16[256,2304]{1,0:T(8,128)(2,1)S(1)} %get-tuple-element.49.z_high.h, bf16[256,2304]{1,0:T(8,128)(2,1)S(1)} %get-tuple-element.50.z_low.l, ...), custom_call_target="tpu_custom_call" | custom-call | tf_op jit(solution)/shard_map/above/pallas_call | solution.py:591
  62.5 23.7 %all_to_all.11 = f32[256,1,128]{2,1,0:T(1,128)S(1)} all-to-all(f32[256,1,128]{2,1,0:T(1,128)S(1)} %bitcast.5), channel_id=1, replica_groups=mesh['gx'=8,'gy_0'=4,'gy_1'=2,'gz'=4] {'gx','gy_0','gy_1','gz'}, dimensions={0} | all-to-all | bytes 262144 | tf_op jit(solution)/shard_map/all_to_all | solution.py:670
  86.3 1.3 %finish.1 = f32[3,256]{1,0:T(4,128)} custom-call(f32[256,128]{1,0:T(8,128)S(1)} %bitcast.6, f32[24,128]{1,0:T(8,128)S(1)} %get-tuple-element.53.own.vector.first, f32[24,128]{1,0:T(8,128)S(1)} %above.3.own.vector.second, f32[24,128]{1,0:T(8,128)S(1)} %above.4.own.third), custom_call_target="tpu_custom_call" | custom-call | tf_op jit(solution)/shard_map/finish/pallas_call | solution.py:591
  (27 shorter events, 3.1 us)
Async XLA Ops:
  2.3 4.8 %collective-permute-start = (f32[80,128]{1,0:T(8,128)S(1)}, f32[80,128]{1,0:T(8,128)S(1)}, u32[]{:S(2)}, u32[]{:S(2)}) collective-permute-start(f32[80,128]{1,0:T(8,128)S(1)} %get-tuple-element.38), channel_id=1, source_target_pairs={{0,1},{1,2},{2,3},{3,0},{4,5},{5,6},{6,7},{7,4},{8,9},{9,10},{10,1... | collective-permute-start | bytes 122888 | tf_op jit(solution)/shard_map/ppermute | solution.py:30
  4.4 2.9 %collective-permute-start.1 = (f32[80,128]{1,0:T(8,128)S(1)}, f32[80,128]{1,0:T(8,128)S(1)}, u32[]{:S(2)}, u32[]{:S(2)}) collective-permute-start(f32[80,128]{1,0:T(8,128)S(1)} %get-tuple-element.39), channel_id=1, source_target_pairs={{0,3},{1,0},{2,1},{3,2},{4,7},{5,4},{6,5},{7,6},{8,11},{9,8},{10,9... | collective-permute-start | bytes 122888 | tf_op jit(solution)/shard_map/ppermute | solution.py:30
  7.6 5.3 %collective-permute-start.3 = (f32[136,128]{1,0:T(8,128)S(1)}, f32[136,128]{1,0:T(8,128)S(1)}, u32[]{:S(2)}, u32[]{:S(2)}) collective-permute-start(f32[136,128]{1,0:T(8,128)S(1)} %get-tuple-element.43), channel_id=1, source_target_pairs={{0,28},{4,0},{8,4},{12,8},{16,12},{20,16},{24,20},{28,24},{1,29},{... | collective-permute-start | bytes 208904 | tf_op jit(solution)/shard_map/ppermute | solution.py:30
  11.2 1.2 %collective-permute-start.2 = (f32[96,128]{1,0:T(8,128)S(1)}, f32[96,128]{1,0:T(8,128)S(1)}, u32[]{:S(2)}, u32[]{:S(2)}) collective-permute-start(f32[96,128]{1,0:T(8,128)S(1)} %get-tuple-element.42), channel_id=1, source_target_pairs={{0,4},{4,8},{8,12},{12,16},{16,20},{20,24},{24,28},{28,0},{1,5},{5... | collective-permute-start | bytes 147464 | tf_op jit(solution)/shard_map/ppermute | solution.py:30
  13.0 10.5 %collective-permute-start.5 = (f32[280,128]{1,0:T(8,128)S(1)}, f32[280,128]{1,0:T(8,128)S(1)}, u32[]{:S(2)}, u32[]{:S(2)}) collective-permute-start(f32[280,128]{1,0:T(8,128)S(1)} %get-tuple-element.46), channel_id=1, source_target_pairs={{0,224},{32,0},{64,32},{96,64},{128,96},{160,128},{192,160},{224,1... | collective-permute-start | bytes 430088 | tf_op jit(solution)/shard_map/ppermute | solution.py:30
  18.6 4.8 %collective-permute-start.4 = (f32[216,128]{1,0:T(8,128)S(1)}, f32[216,128]{1,0:T(8,128)S(1)}, u32[]{:S(2)}, u32[]{:S(2)}) collective-permute-start(f32[216,128]{1,0:T(8,128)S(1)} %get-tuple-element.45), channel_id=1, source_target_pairs={{0,32},{32,64},{64,96},{96,128},{128,160},{160,192},{192,224},{224... | collective-permute-start | bytes 331784 | tf_op jit(solution)/shard_map/ppermute | solution.py:30
  24.1 5.8 %collective-permute-start.6 = (f32[24,128]{1,0:T(8,128)S(1)}, f32[24,128]{1,0:T(8,128)S(1)}, u32[]{:S(2)}, u32[]{:S(2)}) collective-permute-start(f32[24,128]{1,0:T(8,128)S(1)} %get-tuple-element.53.own.vector.first), channel_id=1, source_target_pairs={{0,4},{4,8},{8,12},{12,16},{16,20},{20,24},{24,28},{28,0},{1,5},{5... | collective-permute-start | bytes 36872 | tf_op jit(solution)/shard_map/ppermute | solution.py:30
  27.2 3.1 %collective-permute-start.7 = (f32[24,128]{1,0:T(8,128)S(1)}, f32[24,128]{1,0:T(8,128)S(1)}, u32[]{:S(2)}, u32[]{:S(2)}) collective-permute-start(f32[24,128]{1,0:T(8,128)S(1)} %get-tuple-element.53.own.vector.first), channel_id=1, source_target_pairs={{0,28},{4,0},{8,4},{12,8},{16,12},{20,16},{24,20},{28,24},{1,29},{... | collective-permute-start | bytes 36872 | tf_op jit(solution)/shard_map/ppermute | solution.py:30
  30.3 4.9 %collective-permute-start.8 = (f32[72,128]{1,0:T(8,128)S(1)}, f32[72,128]{1,0:T(8,128)S(1)}, u32[]{:S(2)}, u32[]{:S(2)}) collective-permute-start(f32[72,128]{1,0:T(8,128)S(1)} %pad_maximum_fusion), channel_id=1, source_target_pairs={{0,32},{32,64},{64,96},{96,128},{128,160},{160,192},{192,224},{224... | collective-permute-start | bytes 110600 | tf_op jit(solution)/shard_map/ppermute | solution.py:30
  30.3 6.2 %collective-permute-start.9 = (f32[72,128]{1,0:T(8,128)S(1)}, f32[72,128]{1,0:T(8,128)S(1)}, u32[]{:S(2)}, u32[]{:S(2)}) collective-permute-start(f32[72,128]{1,0:T(8,128)S(1)} %pad_maximum_fusion), channel_id=1, source_target_pairs={{0,224},{32,0},{64,32},{96,64},{128,96},{160,128},{192,160},{224,1... | collective-permute-start | bytes 110600 | tf_op jit(solution)/shard_map/ppermute | solution.py:30
  37.8 3.9 %collective-permute-start.10 = (f32[24,128]{1,0:T(8,128)S(1)}, f32[24,128]{1,0:T(8,128)S(1)}, u32[]{:S(2)}, u32[]{:S(2)}) collective-permute-start(f32[24,128]{1,0:T(8,128)S(1)} %above.3.own.vector.second), channel_id=1, source_target_pairs={{0,4},{4,8},{8,12},{12,16},{16,20},{20,24},{24,28},{28,0},{1,5},{5... | collective-permute-start | bytes 36872 | tf_op jit(solution)/shard_map/ppermute | solution.py:30
  38.8 3.1 %collective-permute-start.11 = (f32[24,128]{1,0:T(8,128)S(1)}, f32[24,128]{1,0:T(8,128)S(1)}, u32[]{:S(2)}, u32[]{:S(2)}) collective-permute-start(f32[24,128]{1,0:T(8,128)S(1)} %above.3.own.vector.second), channel_id=1, source_target_pairs={{0,28},{4,0},{8,4},{12,8},{16,12},{20,16},{24,20},{28,24},{1,29},{... | collective-permute-start | bytes 36872 | tf_op jit(solution)/shard_map/ppermute | solution.py:30
  42.0 4.7 %collective-permute-start.12 = (f32[72,128]{1,0:T(8,128)S(1)}, f32[72,128]{1,0:T(8,128)S(1)}, u32[]{:S(2)}, u32[]{:S(2)}) collective-permute-start(f32[72,128]{1,0:T(8,128)S(1)} %pad_maximum_fusion.1), channel_id=1, source_target_pairs={{0,32},{32,64},{64,96},{96,128},{128,160},{160,192},{192,224},{224... | collective-permute-start | bytes 110600 | tf_op jit(solution)/shard_map/ppermute | solution.py:30
  42.0 6.0 %collective-permute-start.13 = (f32[72,128]{1,0:T(8,128)S(1)}, f32[72,128]{1,0:T(8,128)S(1)}, u32[]{:S(2)}, u32[]{:S(2)}) collective-permute-start(f32[72,128]{1,0:T(8,128)S(1)} %pad_maximum_fusion.1), channel_id=1, source_target_pairs={{0,224},{32,0},{64,32},{96,64},{128,96},{160,128},{192,160},{224,1... | collective-permute-start | bytes 110600 | tf_op jit(solution)/shard_map/ppermute | solution.py:30
  49.3 5.3 %collective-permute-start.14 = (f32[24,128]{1,0:T(8,128)S(1)}, f32[24,128]{1,0:T(8,128)S(1)}, u32[]{:S(2)}, u32[]{:S(2)}) collective-permute-start(f32[24,128]{1,0:T(8,128)S(1)} %above.4.own.third), channel_id=1, source_target_pairs={{0,4},{4,8},{8,12},{12,16},{16,20},{20,24},{24,28},{28,0},{1,5},{5... | collective-permute-start | bytes 36872 | tf_op jit(solution)/shard_map/ppermute | solution.py:30
  49.9 4.7 %collective-permute-start.15 = (f32[24,128]{1,0:T(8,128)S(1)}, f32[24,128]{1,0:T(8,128)S(1)}, u32[]{:S(2)}, u32[]{:S(2)}) collective-permute-start(f32[24,128]{1,0:T(8,128)S(1)} %above.4.own.third), channel_id=1, source_target_pairs={{0,28},{4,0},{8,4},{12,8},{16,12},{20,16},{24,20},{28,24},{1,29},{... | collective-permute-start | bytes 36872 | tf_op jit(solution)/shard_map/ppermute | solution.py:30
  54.6 4.8 %collective-permute-start.16 = (f32[72,128]{1,0:T(8,128)S(1)}, f32[72,128]{1,0:T(8,128)S(1)}, u32[]{:S(2)}, u32[]{:S(2)}) collective-permute-start(f32[72,128]{1,0:T(8,128)S(1)} %pad_maximum_fusion.2), channel_id=1, source_target_pairs={{0,32},{32,64},{64,96},{96,128},{128,160},{160,192},{192,224},{224... | collective-permute-start | bytes 110600 | tf_op jit(solution)/shard_map/ppermute | solution.py:30
  54.7 6.0 %collective-permute-start.17 = (f32[72,128]{1,0:T(8,128)S(1)}, f32[72,128]{1,0:T(8,128)S(1)}, u32[]{:S(2)}, u32[]{:S(2)}) collective-permute-start(f32[72,128]{1,0:T(8,128)S(1)} %pad_maximum_fusion.2), channel_id=1, source_target_pairs={{0,224},{32,0},{64,32},{96,64},{128,96},{160,128},{192,160},{224,1... | collective-permute-start | bytes 110600 | tf_op jit(solution)/shard_map/ppermute | solution.py:30

commit v5 on v4

--- a/solution.py
+++ b/solution.py
@@ -28,6 +28,16 @@
 def shifted(shard, axis, by):
     length = lax.axis_size(axis)
     return lax.ppermute(shard, axis, [(i, (i + by) % length) for i in range(length)])
+
+
+def swapped_y(to_apart, to_near):
+    length = lax.axis_size(GY)
+    apart = lax.ppermute(to_apart, GY, [(i, (i + 1 if i % 2 else i - 1) % length) for i in range(length)])
+    return apart, lax.ppermute(to_near, GY, [(i, i ^ 1) for i in range(length)])
+
+
+def apart_is_below():
+    return lax.axis_index("gy_1") == 0
 
 
 def halves(value):
@@ -121,7 +131,7 @@
             out[76 + block : 77 + block, :] = number
 
 
-def deepen_z_kernel(fields, own, below, above, wide, marks, aux, upward, downward):
+def deepen_z_kernel(fields, own, below, above, wide, marks, aux, to_apart, to_near, upward, downward):
     lane = lax.broadcasted_iota(jnp.int32, (128, 128), 1)
     packed = jnp.zeros((64, 128), F32)
     lane64 = lax.broadcasted_iota(jnp.int32, (64, 128), 1)
@@ -152,6 +162,10 @@
     marks[36:40, :] = jnp.broadcast_to(halo[44:45], (4, 128))
     upward[56:96, :] = marks[...]
     downward[96:136, :] = marks[...]
+    upward[96:136, :] = jnp.zeros((40, 128), F32)
+    order = apart_is_below()
+    to_apart[...] = jnp.where(order, downward[...], upward[...])
+    to_near[...] = jnp.where(order, upward[...], downward[...])
     aux[...] = jnp.zeros((72, 128), F32)
     for kind in range(3):
         for c in range(3):
@@ -162,7 +176,10 @@
                 aux[row : row + 1, :] = halo[4 * k + block : 4 * k + block + 1]
 
 
-def deepen_y_kernel(wide, marks, below, above, deep, three, upward, downward):
+def deepen_y_kernel(wide, marks, apart, near, deep, three, upward, downward, below, above):
+    order = apart_is_below()
+    below[...] = jnp.where(order, apart[...], near[...])
+    above[...] = jnp.where(order, near[...], apart[...])
     for at in range(40):
         row = at * YPAD
         deep[row + 2 : row + 10, :] = wide[at * 8 : at * 8 + 8, :]
@@ -188,8 +205,8 @@
                 upward[39 + at * 26 + k * 13 : 52 + at * 26 + k * 13, :] = deep[row + 96 + k * 16 : row + 109 + k * 16, :]
             downward[78 + at * 39 + k * 13 : 91 + at * 39 + k * 13, :] = deep[row + k * 16 : row + k * 16 + 13, :]
     three[0:40, :] = marks[...]
-    three[40:80, :] = below[56:96, :]
-    three[80:120, :] = above[96:136, :]
+    three[40:80, :] = jnp.where(order, below[56:96, :], above[96:136, :])
+    three[80:120, :] = jnp.where(order, above[96:136, :], below[56:96, :])
     upward[96:216, :] = three[...]
     downward[160:280, :] = three[...]
 
@@ -204,6 +221,8 @@
 
 
 def fill_tables(ref, first, along_x, used, plane_weights, z_high, z_low):
+    apart = jnp.where(apart_is_below(), -8.0, 8.0).astype(F32)
+
     def fill(read, along_y, place):
         fractions = jnp.concatenate([read(3), read(4), read(5), jnp.zeros((5, 128), F32)], axis=0)
         weights = delta_weights(fractions)
@@ -213,7 +232,7 @@
         z_high[0:160, place] = high
         z_low[0:160, place] = rest
 
-    for part, along_y in enumerate((0.0, -8.0, 8.0)):
+    for part, along_y in enumerate((0.0, apart, -apart)):
         top = first + 40 * part
         for half in range(2):
             column = part * 256 + half * 128
@@ -222,7 +241,7 @@
         fill(lambda k: ref[top + 12 + 4 * k : top + 13 + 4 * k, :], along_y, slice(column, column + 128))
 
     def further(block, carry):
-        for part, along_y in enumerate((0.0, -8.0, 8.0)):
+        for part, along_y in enumerate((0.0, apart, -apart)):
             top = first + 40 * part + 12 + block
             column = pl.multiple_of(STATIC + (block - 1) * 384 + part * 128, 128)
             fill(lambda k: ref[pl.ds(top + 4 * k, 1), :], along_y, pl.ds(column, 128))
@@ -419,10 +438,10 @@
 
 
 def own_image(
-    begun, below, above, plane_weights, z_high, z_low, used, scale, result, left_high, left_low, moved, velocity_high,
+    begun, apart, near, plane_weights, z_high, z_low, used, scale, result, left_high, left_low, moved, velocity_high,
     velocity_low,
 ):
-    refs = [(below, 0), (above, 0)]
+    refs = [(apart, 0), (near, 0)]
     planes = range(1, 12)
     count = trips(used)
     spread_group(refs, planes, plane_weights, z_high, z_low, count, left_high, left_low, moved, begun, 1)
@@ -616,12 +635,14 @@
         ],
     )
     below, above = shifted(to_above, "gz", 1), shifted(to_below, "gz", -1)
-    wide, marks, aux, upward, downward = call(
-        deepen_z_kernel, "deepen_z", [rows(320), rows(40), rows(72), rows(96), rows(136)], fields, own, below, above
-    )
-    below, above = shifted(upward, GY, 1), shifted(downward, GY, -1)
+    wide, marks, aux, to_apart, to_near = call(
+        deepen_z_kernel, "deepen_z", [rows(320), rows(40), rows(72), rows(136), rows(136)], fields, own, below, above,
+        scratch=[vmem((136, 128), F32)] * 2,
+    )
+    apart, near = swapped_y(to_apart, to_near)
     deep, three, upward, downward = call(
-        deepen_y_kernel, "deepen_y", [rows(640), rows(120), rows(216), rows(280)], wide, marks, below, above
+        deepen_y_kernel, "deepen_y", [rows(640), rows(120), rows(216), rows(280)], wide, marks, apart, near,
+        scratch=[vmem((136, 128), F32)] * 2,
     )
     below, above = shifted(upward, "gx", 1), shifted(downward, "gx", -1)
     own_tables = call(
@@ -638,17 +659,17 @@
     )
 
     def image_of(last, vector, *others):
-        below, above = shifted(vector, GY, 1), shifted(vector, GY, -1)
+        apart, near = swapped_y(vector, vector)
         begun = call(
             own_spread_last if last else own_spread, "own_spread",
             [((3 * INNER, LANES), F32)] + ([rows(8)] if last else []), vector, *own_tables, *others,
             scratch=[vmem((3 * INNER, 384), BF16)] * 2,
         )
         held = list(begun) + (list(side_tables) if vector is start else [])
-        three = lax.optimization_barrier((jnp.concatenate([vector, below, above], axis=0), *held))[0]
+        three = lax.optimization_barrier((jnp.concatenate([vector, apart, near], axis=0), *held))[0]
         below_three, above_three = shifted(three, "gx", 1), shifted(three, "gx", -1)
         (own_part,) = call(
-            own_image, "own_image", [rows(24)], begun[0], below, above, *own_tables, scale,
+            own_image, "own_image", [rows(24)], begun[0], apart, near, *own_tables, scale,
             scratch=[vmem((3 * INNER, 768), BF16)] * 2 + [vmem((3 * INNER, LANES), F32)] + velocity_scratch,
         )
         side_scratch = [vmem((192, STATIC), BF16)] * 2 + [vmem((192, LANES), F32)]

time: 87.7 us -> 85.3 us (0.973)
  blocking collectives: 23.7 us -> 22.2 us
    ppermute x18 -> x10, starting transfers between devices: 32.1 us -> 17.3 us  [shifted(): lax.ppermute(shard, axis, [(i, (i + by) % length) for i in range(length)])]
    ppermute x0 -> x8, starting transfers between devices: none -> 14.5 us  [the longest x4 10.9 us: swapped_y(): lax.ppermute(to_apart, GY, [(i, (i + 1 if i % 2 else i - 1) % length) for...]
    ppermute x18 -> x10, waiting for transfers between devices: 8.1 us -> 5.71 us  [shifted(): lax.ppermute(shard, axis, [(i, (i + by) % length) for i in range(length)])]
    ppermute x0 -> x8, waiting for transfers between devices: none -> 1.85 us  [the longest x4 1.65 us: swapped_y(): lax.ppermute(to_apart, GY, [(i, (i + 1 if i % 2 else i - 1) % length) for...]
    all_to_all x1, blocking collectives: 23.7 us -> 22.2 us  [body(): gathered = lax.all_to_all(sums, GX_GY_GZ, 0, 0, tiled=True)]
  transfers between devices with their start and end apart: 18 -> 18, of which waited for: 7 -> 5; matrix products, arithmetic and copies ran while one was open for 0% -> 0% of each run, Pallas kernels for 16% -> 17%
where the time goes in v5:
time: 85.3 us; the launch traced here: 85.2 us
  starting transfers between devices  31.8 us (37%)
  Pallas kernels  22.7 us (27%)
  blocking collectives  22.2 us (26%)
  waiting for transfers between devices  7.56 us (9%)
  between operations  0.88 us (1%)
    pallas_call x19, Pallas kernels, call(): pl.pallas_call(kernel, name=name, out_shape=[jax.ShapeDtypeStruct(shape,...  22.7 us
    all_to_all x1, blocking collectives, body(): gathered = lax.all_to_all(sums, GX_GY_GZ, 0, 0, tiled=True)  22.2 us
    ppermute x10, starting transfers between devices, shifted(): lax.ppermute(shard, axis, [(i, (i + by) % length) for i in range(length)])  17.3 us
    ppermute x4, starting transfers between devices, swapped_y(): lax.ppermute(to_apart, GY, [(i, (i + 1 if i % 2 else i - 1) % length) for...  10.9 us
    ppermute x10, waiting for transfers between devices, shifted(): lax.ppermute(shard, axis, [(i, (i + by) % length) for i in range(length)])  5.71 us
    ppermute x4, starting transfers between devices, swapped_y(): lax.ppermute(to_near, GY, [(i, i ^ 1) for i in range(length)])  3.57 us
  transfers between devices with their start and end apart: 18, of which 5 were waited for; matrix products, arithmetic and copies ran while one was open for 0% of the time, Pallas kernels for 17%

profile of v5, /device:TPU:1, one launch (start us, length us, event | category | flops | bytes accessed | tf_op | source)
XLA Modules:
  0.0 85.2 jit_solution(14867169544339256254)
XLA Ops:
  0.7 1.7 %pack.1 = (f32[256,128]{1,0:T(8,128)S(1)}, f32[24,128]{1,0:T(8,128)S(1)}, f32[80,128]{1,0:T(8,128)S(1)}, f32[80,128]{1,0:T(8,128)S(1)}) custom-call(f32[8,8,128]{2,1,0:T(8,128)} %density_in.1, f32[3,8,8,128]{3,2,1,0:T(8,128)} %base_in.1, s32[3,256]{1,0:T(4,128)} %cells_in.1, f32[3,256]{1,0:T(4,128)} %offsets_in.1, f32[3,256]{1,0:T(4,128)} %target_in.1, ...), custom_call_target="tpu_custom_call" | custom-call | tf_op jit(solution)/shard_map/pack/pallas_call | solution.py:610
  2.3 2.1 %collective-permute-start = (f32[80,128]{1,0:T(8,128)S(1)}, f32[80,128]{1,0:T(8,128)S(1)}, u32[]{:S(2)}, u32[]{:S(2)}) collective-permute-start(f32[80,128]{1,0:T(8,128)S(1)} %get-tuple-element.38), channel_id=1, source_target_pairs={{0,1},{1,2},{2,3},{3,0},{4,5},{5,6},{6,7},{7,4},{8,9},{9,10},{10,1... | collective-permute-start | bytes 122888 | tf_op jit(solution)/shard_map/ppermute | solution.py:30
  4.4 1.4 %collective-permute-start.1 = (f32[80,128]{1,0:T(8,128)S(1)}, f32[80,128]{1,0:T(8,128)S(1)}, u32[]{:S(2)}, u32[]{:S(2)}) collective-permute-start(f32[80,128]{1,0:T(8,128)S(1)} %get-tuple-element.39), channel_id=1, source_target_pairs={{0,3},{1,0},{2,1},{3,2},{4,7},{5,4},{6,5},{7,6},{8,11},{9,8},{10,9... | collective-permute-start | bytes 122888 | tf_op jit(solution)/shard_map/ppermute | solution.py:30
  5.8 1.3 %collective-permute-done.below = f32[80,128]{1,0:T(8,128)S(1)} collective-permute-done((f32[80,128]{1,0:T(8,128)S(1)}, f32[80,128]{1,0:T(8,128)S(1)}, u32[]{:S(2)}, u32[]{:S(2)}) %collective-permute-start) | collective-permute-done | bytes 40992 | tf_op jit(solution)/shard_map/ppermute | solution.py:30
  7.6 3.4 %collective-permute-start.2 = (f32[136,128]{1,0:T(8,128)S(1)}, f32[136,128]{1,0:T(8,128)S(1)}, u32[]{:S(2)}, u32[]{:S(2)}) collective-permute-start(f32[136,128]{1,0:T(8,128)S(1)} %get-tuple-element.42), channel_id=1, source_target_pairs={{0,28},{4,8},{8,4},{12,16},{16,12},{20,24},{24,20},{28,0},{1,29},{... | collective-permute-start | bytes 208904 | tf_op jit(solution)/shard_map/ppermute | solution.py:35
  11.3 1.6 %collective-permute-done.2.apart = f32[136,128]{1,0:T(8,128)S(1)} collective-permute-done((f32[136,128]{1,0:T(8,128)S(1)}, f32[136,128]{1,0:T(8,128)S(1)}, u32[]{:S(2)}, u32[]{:S(2)}) %collective-permute-start.2) | collective-permute-done | bytes 69664 | tf_op jit(solution)/shard_map/ppermute | solution.py:35
  13.0 5.7 %collective-permute-start.5 = (f32[280,128]{1,0:T(8,128)S(1)}, f32[280,128]{1,0:T(8,128)S(1)}, u32[]{:S(2)}, u32[]{:S(2)}) collective-permute-start(f32[280,128]{1,0:T(8,128)S(1)} %get-tuple-element.46), channel_id=1, source_target_pairs={{0,224},{32,0},{64,32},{96,64},{128,96},{160,128},{192,160},{224,1... | collective-permute-start | bytes 430088 | tf_op jit(solution)/shard_map/ppermute | solution.py:30
  19.3 4.2 %collective-permute-done.4.below = f32[216,128]{1,0:T(8,128)S(1)} collective-permute-done((f32[216,128]{1,0:T(8,128)S(1)}, f32[216,128]{1,0:T(8,128)S(1)}, u32[]{:S(2)}, u32[]{:S(2)}) %collective-permute-start.4) | collective-permute-done | bytes 110624 | tf_op jit(solution)/shard_map/ppermute | solution.py:30
  23.5 0.6 setup.1
  24.1 3.3 %collective-permute-start.6 = (f32[24,128]{1,0:T(8,128)S(1)}, f32[24,128]{1,0:T(8,128)S(1)}, u32[]{:S(2)}, u32[]{:S(2)}) collective-permute-start(f32[24,128]{1,0:T(8,128)S(1)} %get-tuple-element.53.own.vector.first), channel_id=1, source_target_pairs={{0,28},{4,8},{8,4},{12,16},{16,12},{20,24},{24,20},{28,0},{1,29},{... | collective-permute-start | bytes 36872 | tf_op jit(solution)/shard_map/ppermute | solution.py:35
  27.5 0.6 own_spread.3.begun
  28.2 1.1 %side_tables.1 = (f32[32,2304]{1,0:T(8,128)S(1)}, bf16[256,2304]{1,0:T(8,128)(2,1)S(1)}, bf16[256,2304]{1,0:T(8,128)(2,1)S(1)}, f32[32,2304]{1,0:T(8,128)S(1)}, ...) custom-call(f32[216,128]{1,0:T(8,128)S(1)} %collective-permute-done.4.below, ...), custom_call_target="tpu_custom_call" | custom-call | tf_op jit(solution)/shard_map/side_tables/pallas_call | solution.py:610
  29.4 2.7 %collective-permute-start.9 = (f32[72,128]{1,0:T(8,128)S(1)}, f32[72,128]{1,0:T(8,128)S(1)}, u32[]{:S(2)}, u32[]{:S(2)}) collective-permute-start(f32[72,128]{1,0:T(8,128)S(1)} %pad_maximum_fusion), channel_id=1, source_target_pairs={{0,224},{32,0},{64,32},{96,64},{128,96},{160,128},{192,160},{224,1... | collective-permute-start | bytes 110600 | tf_op jit(solution)/shard_map/ppermute | solution.py:30
  32.1 2.0 %own_image.3.begun = f32[24,128]{1,0:T(8,128)S(1)} custom-call(f32[528,256]{1,0:T(8,128)S(1)} %own_spread.3.begun, f32[24,128]{1,0:T(8,128)S(1)} %collective-permute-done.6.apart, f32[24,128]{1,0:T(8,128)S(1)} %collective-permute-done.7.near, f32[32,2304]{1,0:T(8,128)S(1)} %get-tuple-element.48.plane_weights.w, ...), custom_call_target="tpu_custom_call" | custom-call | tf_op jit(solution)/shard_map/own_image/pallas_call | solution.py:610
  34.1 1.3 %below.3.begun = f32[24,128]{1,0:T(8,128)S(1)} custom-call(f32[24,128]{1,0:T(8,128)S(1)} %own_image.3.begun, f32[72,128]{1,0:T(8,128)S(1)} %collective-permute-done.8.three, f32[32,2304]{1,0:T(8,128)S(1)} %get-tuple-element.48.plane_weights.w, bf16[256,2304]{1,0:T(8,128)(2,1)S(1)} %get-tuple-element.49.z_high.h, ...), custom_call_target="tpu_custom_call" | custom-call | tf_op jit(solution)/shard_map/below/pallas_call | solution.py:610
  35.4 1.3 %above.3.own.vector.second = f32[24,128]{1,0:T(8,128)S(1)} custom-call(f32[24,128]{1,0:T(8,128)S(1)} %below.3.begun, f32[72,128]{1,0:T(8,128)S(1)} %collective-permute-done.9.three, f32[32,2304]{1,0:T(8,128)S(1)} %get-tuple-element.48.plane_weights.w, bf16[256,2304]{1,0:T(8,128)(2,1)S(1)} %get-tuple-element.49.z_high.h, ...), custom_call_target="tpu_custom_call" | custom-call | tf_op jit(solution)/shard_map/above/pallas_call | solution.py:610
  36.7 2.2 %collective-permute-start.10 = (f32[24,128]{1,0:T(8,128)S(1)}, f32[24,128]{1,0:T(8,128)S(1)}, u32[]{:S(2)}, u32[]{:S(2)}) collective-permute-start(f32[24,128]{1,0:T(8,128)S(1)} %above.3.own.vector.second), channel_id=1, source_target_pairs={{0,28},{4,8},{8,4},{12,16},{16,12},{20,24},{24,20},{28,0},{1,29},{... | collective-permute-start | bytes 36872 | tf_op jit(solution)/shard_map/ppermute | solution.py:35
  38.9 1.0 %collective-permute-start.11 = (f32[24,128]{1,0:T(8,128)S(1)}, f32[24,128]{1,0:T(8,128)S(1)}, u32[]{:S(2)}, u32[]{:S(2)}) collective-permute-start(f32[24,128]{1,0:T(8,128)S(1)} %above.3.own.vector.second), channel_id=1, source_target_pairs={{0,4},{4,0},{8,12},{12,8},{16,20},{20,16},{24,28},{28,24},{1,5},{5... | collective-permute-start | bytes 36872 | tf_op jit(solution)/shard_map/ppermute | solution.py:36
  39.9 0.6 own_spread.4.begun
  40.7 2.7 %collective-permute-start.13 = (f32[72,128]{1,0:T(8,128)S(1)}, f32[72,128]{1,0:T(8,128)S(1)}, u32[]{:S(2)}, u32[]{:S(2)}) collective-permute-start(f32[72,128]{1,0:T(8,128)S(1)} %pad_maximum_fusion.1), channel_id=1, source_target_pairs={{0,224},{32,0},{64,32},{96,64},{128,96},{160,128},{192,160},{224,1... | collective-permute-start | bytes 110600 | tf_op jit(solution)/shard_map/ppermute | solution.py:30
  43.4 2.0 %own_image.4.begun = f32[24,128]{1,0:T(8,128)S(1)} custom-call(f32[528,256]{1,0:T(8,128)S(1)} %own_spread.4.begun, f32[24,128]{1,0:T(8,128)S(1)} %collective-permute-done.10.apart, f32[24,128]{1,0:T(8,128)S(1)} %collective-permute-done.11.near, f32[32,2304]{1,0:T(8,128)S(1)} %get-tuple-element.48.plane_weights.w, ...), custom_call_target="tpu_custom_call" | custom-call | tf_op jit(solution)/shard_map/own_image/pallas_call | solution.py:610
  45.4 1.5 %below.4.begun = f32[24,128]{1,0:T(8,128)S(1)} custom-call(f32[24,128]{1,0:T(8,128)S(1)} %own_image.4.begun, f32[72,128]{1,0:T(8,128)S(1)} %collective-permute-done.12.three, f32[32,2304]{1,0:T(8,128)S(1)} %get-tuple-element.48.plane_weights.w, bf16[256,2304]{1,0:T(8,128)(2,1)S(1)} %get-tuple-element.49.z_high.h, ...), custom_call_target="tpu_custom_call" | custom-call | tf_op jit(solution)/shard_map/below/pallas_call | solution.py:610
  47.0 1.3 %above.4.own.third = f32[24,128]{1,0:T(8,128)S(1)} custom-call(f32[24,128]{1,0:T(8,128)S(1)} %below.4.begun, f32[72,128]{1,0:T(8,128)S(1)} %collective-permute-done.13.three, f32[32,2304]{1,0:T(8,128)S(1)} %get-tuple-element.48.plane_weights.w, bf16[256,2304]{1,0:T(8,128)(2,1)S(1)} %get-tuple-element.49.z_high.h, ...), custom_call_target="tpu_custom_call" | custom-call | tf_op jit(solution)/shard_map/above/pallas_call | solution.py:610
  48.3 2.0 %collective-permute-start.14 = (f32[24,128]{1,0:T(8,128)S(1)}, f32[24,128]{1,0:T(8,128)S(1)}, u32[]{:S(2)}, u32[]{:S(2)}) collective-permute-start(f32[24,128]{1,0:T(8,128)S(1)} %above.4.own.third), channel_id=1, source_target_pairs={{0,28},{4,8},{8,4},{12,16},{16,12},{20,24},{24,20},{28,0},{1,29},{... | collective-permute-start | bytes 36872 | tf_op jit(solution)/shard_map/ppermute | solution.py:35
  50.3 2.2 %collective-permute-start.15 = (f32[24,128]{1,0:T(8,128)S(1)}, f32[24,128]{1,0:T(8,128)S(1)}, u32[]{:S(2)}, u32[]{:S(2)}) collective-permute-start(f32[24,128]{1,0:T(8,128)S(1)} %above.4.own.third), channel_id=1, source_target_pairs={{0,4},{4,0},{8,12},{12,8},{16,20},{20,16},{24,28},{28,24},{1,5},{5... | collective-permute-start | bytes 36872 | tf_op jit(solution)/shard_map/ppermute | solution.py:36
  52.5 1.2 %own_spread.5 = (f32[528,256]{1,0:T(8,128)S(1)}, f32[8,128]{1,0:T(8,128)S(1)}) custom-call(f32[24,128]{1,0:T(8,128)S(1)} %above.4.own.third, f32[32,2304]{1,0:T(8,128)S(1)} %get-tuple-element.48.plane_weights.w, bf16[256,2304]{1,0:T(8,128)(2,1)S(1)} %get-tuple-element.49.z_high.h, bf16[256,2304]{1,0:T(8,128)(2,1)S(1)} %get-tuple-element.50.z_low.l, ...), custom_call_target="tpu_custom_call" | custom-call | tf_op jit(solution)/shard_map/own_spread/pallas_call | solution.py:610
  53.8 2.7 %collective-permute-start.17 = (f32[72,128]{1,0:T(8,128)S(1)}, f32[72,128]{1,0:T(8,128)S(1)}, u32[]{:S(2)}, u32[]{:S(2)}) collective-permute-start(f32[72,128]{1,0:T(8,128)S(1)} %pad_maximum_fusion.2), channel_id=1, source_target_pairs={{0,224},{32,0},{64,32},{96,64},{128,96},{160,128},{192,160},{224,1... | collective-permute-start | bytes 110600 | tf_op jit(solution)/shard_map/ppermute | solution.py:30
  56.5 2.0 %own_image.5.begun = f32[24,128]{1,0:T(8,128)S(1)} custom-call(f32[528,256]{1,0:T(8,128)S(1)} %get-tuple-element.64.begun, f32[24,128]{1,0:T(8,128)S(1)} %collective-permute-done.14.apart, f32[24,128]{1,0:T(8,128)S(1)} %collective-permute-done.15.near, f32[32,2304]{1,0:T(8,128)S(1)} %get-tuple-element.48.plane_weights.w, ...), custom_call_target="tpu_custom_call" | custom-call | tf_op jit(solution)/shard_map/own_image/pallas_call | solution.py:610
  58.5 1.3 %below.5.begun = f32[24,128]{1,0:T(8,128)S(1)} custom-call(f32[24,128]{1,0:T(8,128)S(1)} %own_image.5.begun, f32[72,128]{1,0:T(8,128)S(1)} %collective-permute-done.16.three, f32[32,2304]{1,0:T(8,128)S(1)} %get-tuple-element.48.plane_weights.w, bf16[256,2304]{1,0:T(8,128)(2,1)S(1)} %get-tuple-element.49.z_high.h, ...), custom_call_target="tpu_custom_call" | custom-call | tf_op jit(solution)/shard_map/below/pallas_call | solution.py:610
  59.8 1.9 %above.5 = f32[256,128]{1,0:T(8,128)S(1)} custom-call(f32[24,128]{1,0:T(8,128)S(1)} %below.5.begun, f32[72,128]{1,0:T(8,128)S(1)} %collective-permute-done.17.three, f32[32,2304]{1,0:T(8,128)S(1)} %get-tuple-element.48.plane_weights.w, bf16[256,2304]{1,0:T(8,128)(2,1)S(1)} %get-tuple-element.49.z_high.h, bf16[256,2304]{1,0:T(8,128)(2,1)S(1)} %get-tuple-element.50.z_low.l, ...), custom_call_target="tpu_custom_call" | custom-call | tf_op jit(solution)/shard_map/above/pallas_call | solution.py:610
  61.7 22.2 %all_to_all.11 = f32[256,1,128]{2,1,0:T(1,128)S(1)} all-to-all(f32[256,1,128]{2,1,0:T(1,128)S(1)} %bitcast.5), channel_id=1, replica_groups=mesh['gx'=8,'gy_0'=4,'gy_1'=2,'gz'=4] {'gx','gy_0','gy_1','gz'}, dimensions={0} | all-to-all | bytes 262144 | tf_op jit(solution)/shard_map/all_to_all | solution.py:691
  83.9 1.3 %finish.1 = f32[3,256]{1,0:T(4,128)} custom-call(f32[256,128]{1,0:T(8,128)S(1)} %bitcast.6, f32[24,128]{1,0:T(8,128)S(1)} %get-tuple-element.53.own.vector.first, f32[24,128]{1,0:T(8,128)S(1)} %above.3.own.vector.second, f32[24,128]{1,0:T(8,128)S(1)} %above.4.own.third), custom_call_target="tpu_custom_call" | custom-call | tf_op jit(solution)/shard_map/finish/pallas_call | solution.py:610
  (27 shorter events, 2.0 us)
Async XLA Ops:
  2.3 4.8 %collective-permute-start = (f32[80,128]{1,0:T(8,128)S(1)}, f32[80,128]{1,0:T(8,128)S(1)}, u32[]{:S(2)}, u32[]{:S(2)}) collective-permute-start(f32[80,128]{1,0:T(8,128)S(1)} %get-tuple-element.38), channel_id=1, source_target_pairs={{0,1},{1,2},{2,3},{3,0},{4,5},{5,6},{6,7},{7,4},{8,9},{9,10},{10,1... | collective-permute-start | bytes 122888 | tf_op jit(solution)/shard_map/ppermute | solution.py:30
  4.4 2.9 %collective-permute-start.1 = (f32[80,128]{1,0:T(8,128)S(1)}, f32[80,128]{1,0:T(8,128)S(1)}, u32[]{:S(2)}, u32[]{:S(2)}) collective-permute-start(f32[80,128]{1,0:T(8,128)S(1)} %get-tuple-element.39), channel_id=1, source_target_pairs={{0,3},{1,0},{2,1},{3,2},{4,7},{5,4},{6,5},{7,6},{8,11},{9,8},{10,9... | collective-permute-start | bytes 122888 | tf_op jit(solution)/shard_map/ppermute | solution.py:30
  7.6 5.4 %collective-permute-start.2 = (f32[136,128]{1,0:T(8,128)S(1)}, f32[136,128]{1,0:T(8,128)S(1)}, u32[]{:S(2)}, u32[]{:S(2)}) collective-permute-start(f32[136,128]{1,0:T(8,128)S(1)} %get-tuple-element.42), channel_id=1, source_target_pairs={{0,28},{4,8},{8,4},{12,16},{16,12},{20,24},{24,20},{28,0},{1,29},{... | collective-permute-start | bytes 208904 | tf_op jit(solution)/shard_map/ppermute | solution.py:35
  10.9 2.0 %collective-permute-start.3 = (f32[136,128]{1,0:T(8,128)S(1)}, f32[136,128]{1,0:T(8,128)S(1)}, u32[]{:S(2)}, u32[]{:S(2)}) collective-permute-start(f32[136,128]{1,0:T(8,128)S(1)} %get-tuple-element.43), channel_id=1, source_target_pairs={{0,4},{4,0},{8,12},{12,8},{16,20},{20,16},{24,28},{28,24},{1,5},{5... | collective-permute-start | bytes 208904 | tf_op jit(solution)/shard_map/ppermute | solution.py:36
  13.0 10.5 %collective-permute-start.5 = (f32[280,128]{1,0:T(8,128)S(1)}, f32[280,128]{1,0:T(8,128)S(1)}, u32[]{:S(2)}, u32[]{:S(2)}) collective-permute-start(f32[280,128]{1,0:T(8,128)S(1)} %get-tuple-element.46), channel_id=1, source_target_pairs={{0,224},{32,0},{64,32},{96,64},{128,96},{160,128},{192,160},{224,1... | collective-permute-start | bytes 430088 | tf_op jit(solution)/shard_map/ppermute | solution.py:30
  18.7 4.8 %collective-permute-start.4 = (f32[216,128]{1,0:T(8,128)S(1)}, f32[216,128]{1,0:T(8,128)S(1)}, u32[]{:S(2)}, u32[]{:S(2)}) collective-permute-start(f32[216,128]{1,0:T(8,128)S(1)} %get-tuple-element.45), channel_id=1, source_target_pairs={{0,32},{32,64},{64,96},{96,128},{128,160},{160,192},{192,224},{224... | collective-permute-start | bytes 331784 | tf_op jit(solution)/shard_map/ppermute | solution.py:30
  24.1 5.2 %collective-permute-start.6 = (f32[24,128]{1,0:T(8,128)S(1)}, f32[24,128]{1,0:T(8,128)S(1)}, u32[]{:S(2)}, u32[]{:S(2)}) collective-permute-start(f32[24,128]{1,0:T(8,128)S(1)} %get-tuple-element.53.own.vector.first), channel_id=1, source_target_pairs={{0,28},{4,8},{8,4},{12,16},{16,12},{20,24},{24,20},{28,0},{1,29},{... | collective-permute-start | bytes 36872 | tf_op jit(solution)/shard_map/ppermute | solution.py:35
  27.4 1.9 %collective-permute-start.7 = (f32[24,128]{1,0:T(8,128)S(1)}, f32[24,128]{1,0:T(8,128)S(1)}, u32[]{:S(2)}, u32[]{:S(2)}) collective-permute-start(f32[24,128]{1,0:T(8,128)S(1)} %get-tuple-element.53.own.vector.first), channel_id=1, source_target_pairs={{0,4},{4,0},{8,12},{12,8},{16,20},{20,16},{24,28},{28,24},{1,5},{5... | collective-permute-start | bytes 36872 | tf_op jit(solution)/shard_map/ppermute | solution.py:36
  29.3 4.8 %collective-permute-start.8 = (f32[72,128]{1,0:T(8,128)S(1)}, f32[72,128]{1,0:T(8,128)S(1)}, u32[]{:S(2)}, u32[]{:S(2)}) collective-permute-start(f32[72,128]{1,0:T(8,128)S(1)} %pad_maximum_fusion), channel_id=1, source_target_pairs={{0,32},{32,64},{64,96},{96,128},{128,160},{160,192},{192,224},{224... | collective-permute-start | bytes 110600 | tf_op jit(solution)/shard_map/ppermute | solution.py:30
  29.4 6.0 %collective-permute-start.9 = (f32[72,128]{1,0:T(8,128)S(1)}, f32[72,128]{1,0:T(8,128)S(1)}, u32[]{:S(2)}, u32[]{:S(2)}) collective-permute-start(f32[72,128]{1,0:T(8,128)S(1)} %pad_maximum_fusion), channel_id=1, source_target_pairs={{0,224},{32,0},{64,32},{96,64},{128,96},{160,128},{192,160},{224,1... | collective-permute-start | bytes 110600 | tf_op jit(solution)/shard_map/ppermute | solution.py:30
  36.7 3.8 %collective-permute-start.10 = (f32[24,128]{1,0:T(8,128)S(1)}, f32[24,128]{1,0:T(8,128)S(1)}, u32[]{:S(2)}, u32[]{:S(2)}) collective-permute-start(f32[24,128]{1,0:T(8,128)S(1)} %above.3.own.vector.second), channel_id=1, source_target_pairs={{0,28},{4,8},{8,4},{12,16},{16,12},{20,24},{24,20},{28,0},{1,29},{... | collective-permute-start | bytes 36872 | tf_op jit(solution)/shard_map/ppermute | solution.py:35
  38.9 1.8 %collective-permute-start.11 = (f32[24,128]{1,0:T(8,128)S(1)}, f32[24,128]{1,0:T(8,128)S(1)}, u32[]{:S(2)}, u32[]{:S(2)}) collective-permute-start(f32[24,128]{1,0:T(8,128)S(1)} %above.3.own.vector.second), channel_id=1, source_target_pairs={{0,4},{4,0},{8,12},{12,8},{16,20},{20,16},{24,28},{28,24},{1,5},{5... | collective-permute-start | bytes 36872 | tf_op jit(solution)/shard_map/ppermute | solution.py:36
  40.7 4.7 %collective-permute-start.12 = (f32[72,128]{1,0:T(8,128)S(1)}, f32[72,128]{1,0:T(8,128)S(1)}, u32[]{:S(2)}, u32[]{:S(2)}) collective-permute-start(f32[72,128]{1,0:T(8,128)S(1)} %pad_maximum_fusion.1), channel_id=1, source_target_pairs={{0,32},{32,64},{64,96},{96,128},{128,160},{160,192},{192,224},{224... | collective-permute-start | bytes 110600 | tf_op jit(solution)/shard_map/ppermute | solution.py:30
  40.7 6.2 %collective-permute-start.13 = (f32[72,128]{1,0:T(8,128)S(1)}, f32[72,128]{1,0:T(8,128)S(1)}, u32[]{:S(2)}, u32[]{:S(2)}) collective-permute-start(f32[72,128]{1,0:T(8,128)S(1)} %pad_maximum_fusion.1), channel_id=1, source_target_pairs={{0,224},{32,0},{64,32},{96,64},{128,96},{160,128},{192,160},{224,1... | collective-permute-start | bytes 110600 | tf_op jit(solution)/shard_map/ppermute | solution.py:30
  48.3 5.4 %collective-permute-start.14 = (f32[24,128]{1,0:T(8,128)S(1)}, f32[24,128]{1,0:T(8,128)S(1)}, u32[]{:S(2)}, u32[]{:S(2)}) collective-permute-start(f32[24,128]{1,0:T(8,128)S(1)} %above.4.own.third), channel_id=1, source_target_pairs={{0,28},{4,8},{8,4},{12,16},{16,12},{20,24},{24,20},{28,0},{1,29},{... | collective-permute-start | bytes 36872 | tf_op jit(solution)/shard_map/ppermute | solution.py:35
  50.3 3.4 %collective-permute-start.15 = (f32[24,128]{1,0:T(8,128)S(1)}, f32[24,128]{1,0:T(8,128)S(1)}, u32[]{:S(2)}, u32[]{:S(2)}) collective-permute-start(f32[24,128]{1,0:T(8,128)S(1)} %above.4.own.third), channel_id=1, source_target_pairs={{0,4},{4,0},{8,12},{12,8},{16,20},{20,16},{24,28},{28,24},{1,5},{5... | collective-permute-start | bytes 36872 | tf_op jit(solution)/shard_map/ppermute | solution.py:36
  53.7 4.8 %collective-permute-start.16 = (f32[72,128]{1,0:T(8,128)S(1)}, f32[72,128]{1,0:T(8,128)S(1)}, u32[]{:S(2)}, u32[]{:S(2)}) collective-permute-start(f32[72,128]{1,0:T(8,128)S(1)} %pad_maximum_fusion.2), channel_id=1, source_target_pairs={{0,32},{32,64},{64,96},{96,128},{128,160},{160,192},{192,224},{224... | collective-permute-start | bytes 110600 | tf_op jit(solution)/shard_map/ppermute | solution.py:30
  53.8 6.0 %collective-permute-start.17 = (f32[72,128]{1,0:T(8,128)S(1)}, f32[72,128]{1,0:T(8,128)S(1)}, u32[]{:S(2)}, u32[]{:S(2)}) collective-permute-start(f32[72,128]{1,0:T(8,128)S(1)} %pad_maximum_fusion.2), channel_id=1, source_target_pairs={{0,224},{32,0},{64,32},{96,64},{128,96},{160,128},{192,160},{224,1... | collective-permute-start | bytes 110600 | tf_op jit(solution)/shard_map/ppermute | solution.py:30

commit v6 on v5

--- a/solution.py
+++ b/solution.py
@@ -36,6 +36,16 @@
     return apart, lax.ppermute(to_near, GY, [(i, i ^ 1) for i in range(length)])
 
 
+def swapped_z(to_odd, to_even):
+    length = lax.axis_size("gz")
+    odd = lax.ppermute(to_odd, "gz", [(i, (i + 1 if i % 2 else i - 1) % length) for i in range(length)])
+    return odd, lax.ppermute(to_even, "gz", [(i, i ^ 1) for i in range(length)])
+
+
+def odd_is_below():
+    return lax.rem(lax.axis_index("gz"), 2) == 0
+
+
 def apart_is_below():
     return lax.axis_index("gy_1") == 0
 
@@ -72,8 +82,8 @@
 
 
 def pack_kernel(
-    density_in, base_in, cells_in, offsets_in, target_in, stiffness_in, counts, fields, own, to_above, to_below,
-    density, base, cells, offsets, target, stiffness, arrived,
+    density_in, base_in, cells_in, offsets_in, target_in, stiffness_in, counts, fields, own, to_odd, to_even,
+    density, base, cells, offsets, target, stiffness, arrived, to_above, to_below,
 ):
     sources = (density_in, base_in, cells_in, offsets_in, target_in, stiffness_in)
     places = (density, base, cells, offsets, target, stiffness)
@@ -104,6 +114,7 @@
     rest = table - table_high.astype(F32)
     table_mid = rest.astype(BF16)
     table_low = (rest - table_mid.astype(F32)).astype(BF16)
+    split_table = jnp.concatenate([table_high, table_mid, table_low], axis=0)
     upper = jnp.where(inside[2] >= 128.0 - REACH, live, 0.0)
     lower = jnp.where(inside[2] < 1.0 * REACH, live, 0.0)
     flags = jnp.concatenate([upper, lower, jnp.zeros((14, MARKERS), F32)], axis=0).astype(BF16)
@@ -112,26 +123,30 @@
     )
     ranks = plain_dot(flags, jnp.where(earlier, 1.0, 0.0).astype(BF16)).astype(jnp.int32)
     slot = lax.broadcasted_iota(jnp.int32, (512, MARKERS), 0)
-    lane = lax.broadcasted_iota(jnp.int32, (1, 128), 1)
-    for at, (flag, out, shift) in enumerate(((upper, to_above, -128.0), (lower, to_below, 128.0))):
-        rank = ranks[at : at + 1, :]
-        goal = ((rank >> 6) << 7) + (rank & 63) + 64 * at
-        chosen = jnp.where((slot == goal) & (flag > 0.0), 1.0, 0.0).astype(BF16)
-        moved = transposed_dot(table_high, chosen) + transposed_dot(table_mid, chosen)
-        moved = moved + transposed_dot(table_low, chosen)
+    goal = jnp.where(upper > 0.0, ranks[0:1, :], jnp.where(lower > 0.0, ranks[1:2, :], 1024))
+    goal = ((goal >> 6) << 7) + (goal & 63) + jnp.where(lower > 0.0, 64, 0)
+    moved = transposed_dot(split_table, jnp.where(slot == goal, 1.0, 0.0).astype(BF16))
+    moved = (moved[0:16] + moved[16:32]) + moved[32:48]
+    first_half = lax.broadcasted_iota(jnp.int32, (1, 128), 1) < 64
+    for flag, out, shift, mine in ((upper, to_above, -128.0, first_half), (lower, to_below, 128.0, ~first_half)):
         number = jnp.broadcast_to(jnp.sum(flag, axis=1, keepdims=True), (1, 128))
-        number = jnp.where((lane < 64) == (at == 0), number, 0.0)
         for block in range(4):
             columns = slice(block * 128, block * 128 + 128)
             for k in range(11):
                 row = moved[k : k + 1, columns]
                 if k == 2:
                     row = row + shift * moved[6:7, columns]
-                out[32 + 4 * k + block : 33 + 4 * k + block, :] = row
-            out[76 + block : 77 + block, :] = number
-
-
-def deepen_z_kernel(fields, own, below, above, wide, marks, aux, to_apart, to_near, upward, downward):
+                out[32 + 4 * k + block : 33 + 4 * k + block, :] = jnp.where(mine, row, 0.0)
+            out[76 + block : 77 + block, :] = jnp.where(mine, number, 0.0)
+    order = odd_is_below()
+    to_odd[...] = jnp.where(order, to_below[...], to_above[...])
+    to_even[...] = jnp.where(order, to_above[...], to_below[...])
+
+
+def deepen_z_kernel(fields, own, odd, even, wide, marks, aux, to_apart, to_near, upward, downward, below, above):
+    order = odd_is_below()
+    below[...] = jnp.where(order, odd[...], even[...])
+    above[...] = jnp.where(order, even[...], odd[...])
     lane = lax.broadcasted_iota(jnp.int32, (128, 128), 1)
     packed = jnp.zeros((64, 128), F32)
     lane64 = lax.broadcasted_iota(jnp.int32, (64, 128), 1)
@@ -624,20 +639,20 @@
     table_shapes = [((32, COLS), F32), ((256, COLS), BF16), ((256, COLS), BF16)]
     used_shape = [((8, 128), jnp.int32)]
     arguments = (density, base_velocity, cells, offsets, target, stiffness.reshape(1, MARKERS))
-    fields, own, to_above, to_below = call(
+    fields, own, to_odd, to_even = call(
         pack_kernel, "pack", [rows(256), rows(24), rows(80), rows(80)],
         *(pltpu.with_memory_space_constraint(a, hbm) for a in arguments), counts,
         memory=[hbm] * 6 + [smem],
         scratch=[
             vmem((8, 8, 128), F32), vmem((3, 8, 8, 128), F32), vmem((3, MARKERS), jnp.int32),
             vmem((3, MARKERS), F32), vmem((3, MARKERS), F32), vmem((1, MARKERS), F32),
-            pltpu.SemaphoreType.DMA((6,)),
+            pltpu.SemaphoreType.DMA((6,)), vmem((80, 128), F32), vmem((80, 128), F32),
         ],
     )
-    below, above = shifted(to_above, "gz", 1), shifted(to_below, "gz", -1)
+    odd, even = swapped_z(to_odd, to_even)
     wide, marks, aux, to_apart, to_near = call(
-        deepen_z_kernel, "deepen_z", [rows(320), rows(40), rows(72), rows(136), rows(136)], fields, own, below, above,
-        scratch=[vmem((136, 128), F32)] * 2,
+        deepen_z_kernel, "deepen_z", [rows(320), rows(40), rows(72), rows(136), rows(136)], fields, own, odd, even,
+        scratch=[vmem((136, 128), F32)] * 2 + [vmem((80, 128), F32)] * 2,
     )
     apart, near = swapped_y(to_apart, to_near)
     deep, three, upward, downward = call(

time: 85.3 us -> 85.4 us (level)
  waiting for transfers between devices: 7.56 us -> 9.26 us
  blocking collectives: 22.2 us -> 21.2 us
    ppermute x10 -> x8, starting transfers between devices: 17.3 us -> 13.8 us  [shifted(): lax.ppermute(shard, axis, [(i, (i + by) % length) for i in range(length)])]
    ppermute x0 -> x2, starting transfers between devices: none -> 3.39 us  [the longest x1 3.38 us: swapped_z(): lax.ppermute(to_odd, 'gz', [(i, (i + 1 if i % 2 else i - 1) % length) for...]
    ppermute x0 -> x2, waiting for transfers between devices: none -> 2.85 us  [the longest x1 1.46 us: swapped_z(): lax.ppermute(to_even, 'gz', [(i, i ^ 1) for i in range(length)])]
    ppermute x10 -> x8, waiting for transfers between devices: 5.71 us -> 4.22 us  [shifted(): lax.ppermute(shard, axis, [(i, (i + by) % length) for i in range(length)])]
    all_to_all x1, blocking collectives: 22.2 us -> 21.2 us  [body(): gathered = lax.all_to_all(sums, GX_GY_GZ, 0, 0, tiled=True)]
where the time goes in v6:
time: 85.4 us; the launch traced here: 85.3 us
  starting transfers between devices  31.4 us (37%)
  Pallas kernels  22.6 us (26%)
  blocking collectives  21.2 us (25%)
  waiting for transfers between devices  9.26 us (11%)
  between operations  0.87 us (1%)
    pallas_call x19, Pallas kernels, call(): pl.pallas_call(kernel, name=name, out_shape=[jax.ShapeDtypeStruct(shape,...  22.6 us
    all_to_all x1, blocking collectives, body(): gathered = lax.all_to_all(sums, GX_GY_GZ, 0, 0, tiled=True)  21.2 us
    ppermute x8, starting transfers between devices, shifted(): lax.ppermute(shard, axis, [(i, (i + by) % length) for i in range(length)])  13.8 us
    ppermute x4, starting transfers between devices, swapped_y(): lax.ppermute(to_apart, GY, [(i, (i + 1 if i % 2 else i - 1) % length) for...  10.9 us
    ppermute x8, waiting for transfers between devices, shifted(): lax.ppermute(shard, axis, [(i, (i + by) % length) for i in range(length)])  4.22 us
    ppermute x1, starting transfers between devices, swapped_z(): lax.ppermute(to_odd, 'gz', [(i, (i + 1 if i % 2 else i - 1) % length) for...  3.38 us
    ppermute x4, starting transfers between devices, swapped_y(): lax.ppermute(to_near, GY, [(i, i ^ 1) for i in range(length)])  3.24 us
    ppermute x4, waiting for transfers between devices, swapped_y(): lax.ppermute(to_apart, GY, [(i, (i + 1 if i % 2 else i - 1) % length) for...  2 us
  transfers between devices with their start and end apart: 18, of which 5 were waited for; matrix products, arithmetic and copies ran while one was open for 0% of the time, Pallas kernels for 17%

profile of v6, /device:TPU:1, one launch (start us, length us, event | category | flops | bytes accessed | tf_op | source)
XLA Modules:
  0.0 85.3 jit_solution(10035678267679421540)
XLA Ops:
  0.7 1.4 %pack.1 = (f32[256,128]{1,0:T(8,128)S(1)}, f32[24,128]{1,0:T(8,128)S(1)}, f32[80,128]{1,0:T(8,128)S(1)}, f32[80,128]{1,0:T(8,128)S(1)}) custom-call(f32[8,8,128]{2,1,0:T(8,128)} %density_in.1, f32[3,8,8,128]{3,2,1,0:T(8,128)} %base_in.1, s32[3,256]{1,0:T(4,128)} %cells_in.1, f32[3,256]{1,0:T(4,128)} %offsets_in.1, f32[3,256]{1,0:T(4,128)} %target_in.1, ...), custom_call_target="tpu_custom_call" | custom-call | tf_op jit(solution)/shard_map/pack/pallas_call | solution.py:625
  2.0 3.4 %collective-permute-start = (f32[80,128]{1,0:T(8,128)S(1)}, f32[80,128]{1,0:T(8,128)S(1)}, u32[]{:S(2)}, u32[]{:S(2)}) collective-permute-start(f32[80,128]{1,0:T(8,128)S(1)} %get-tuple-element.38), channel_id=1, source_target_pairs={{0,3},{1,2},{2,1},{3,0},{4,7},{5,6},{6,5},{7,4},{8,11},{9,10},{10,... | collective-permute-start | bytes 122888 | tf_op jit(solution)/shard_map/ppermute | solution.py:41
  5.4 1.4 %collective-permute-done.odd = f32[80,128]{1,0:T(8,128)S(1)} collective-permute-done((f32[80,128]{1,0:T(8,128)S(1)}, f32[80,128]{1,0:T(8,128)S(1)}, u32[]{:S(2)}, u32[]{:S(2)}) %collective-permute-start) | collective-permute-done | bytes 40992 | tf_op jit(solution)/shard_map/ppermute | solution.py:41
  6.8 1.5 %collective-permute-done.1.even = f32[80,128]{1,0:T(8,128)S(1)} collective-permute-done((f32[80,128]{1,0:T(8,128)S(1)}, f32[80,128]{1,0:T(8,128)S(1)}, u32[]{:S(2)}, u32[]{:S(2)}) %collective-permute-start.1) | collective-permute-done | bytes 40992 | tf_op jit(solution)/shard_map/ppermute | solution.py:42
  8.5 3.4 %collective-permute-start.2 = (f32[136,128]{1,0:T(8,128)S(1)}, f32[136,128]{1,0:T(8,128)S(1)}, u32[]{:S(2)}, u32[]{:S(2)}) collective-permute-start(f32[136,128]{1,0:T(8,128)S(1)} %get-tuple-element.42), channel_id=1, source_target_pairs={{0,28},{4,8},{8,4},{12,16},{16,12},{20,24},{24,20},{28,0},{1,29},{... | collective-permute-start | bytes 208904 | tf_op jit(solution)/shard_map/ppermute | solution.py:35
  11.9 2.0 %collective-permute-done.2.apart = f32[136,128]{1,0:T(8,128)S(1)} collective-permute-done((f32[136,128]{1,0:T(8,128)S(1)}, f32[136,128]{1,0:T(8,128)S(1)}, u32[]{:S(2)}, u32[]{:S(2)}) %collective-permute-start.2) | collective-permute-done | bytes 69664 | tf_op jit(solution)/shard_map/ppermute | solution.py:35
  14.0 5.6 %collective-permute-start.5 = (f32[280,128]{1,0:T(8,128)S(1)}, f32[280,128]{1,0:T(8,128)S(1)}, u32[]{:S(2)}, u32[]{:S(2)}) collective-permute-start(f32[280,128]{1,0:T(8,128)S(1)} %get-tuple-element.46), channel_id=1, source_target_pairs={{0,224},{32,0},{64,32},{96,64},{128,96},{160,128},{192,160},{224,1... | collective-permute-start | bytes 430088 | tf_op jit(solution)/shard_map/ppermute | solution.py:30
  20.2 4.2 %collective-permute-done.4.below = f32[216,128]{1,0:T(8,128)S(1)} collective-permute-done((f32[216,128]{1,0:T(8,128)S(1)}, f32[216,128]{1,0:T(8,128)S(1)}, u32[]{:S(2)}, u32[]{:S(2)}) %collective-permute-start.4) | collective-permute-done | bytes 110624 | tf_op jit(solution)/shard_map/ppermute | solution.py:30
  24.5 0.6 setup.1
  25.1 3.3 %collective-permute-start.6 = (f32[24,128]{1,0:T(8,128)S(1)}, f32[24,128]{1,0:T(8,128)S(1)}, u32[]{:S(2)}, u32[]{:S(2)}) collective-permute-start(f32[24,128]{1,0:T(8,128)S(1)} %get-tuple-element.53.own.vector.first), channel_id=1, source_target_pairs={{0,28},{4,8},{8,4},{12,16},{16,12},{20,24},{24,20},{28,0},{1,29},{... | collective-permute-start | bytes 36872 | tf_op jit(solution)/shard_map/ppermute | solution.py:35
  28.5 0.6 own_spread.3.begun
  29.1 1.1 %side_tables.1 = (f32[32,2304]{1,0:T(8,128)S(1)}, bf16[256,2304]{1,0:T(8,128)(2,1)S(1)}, bf16[256,2304]{1,0:T(8,128)(2,1)S(1)}, f32[32,2304]{1,0:T(8,128)S(1)}, ...) custom-call(f32[216,128]{1,0:T(8,128)S(1)} %collective-permute-done.4.below, ...), custom_call_target="tpu_custom_call" | custom-call | tf_op jit(solution)/shard_map/side_tables/pallas_call | solution.py:625
  30.4 2.7 %collective-permute-start.9 = (f32[72,128]{1,0:T(8,128)S(1)}, f32[72,128]{1,0:T(8,128)S(1)}, u32[]{:S(2)}, u32[]{:S(2)}) collective-permute-start(f32[72,128]{1,0:T(8,128)S(1)} %pad_maximum_fusion), channel_id=1, source_target_pairs={{0,224},{32,0},{64,32},{96,64},{128,96},{160,128},{192,160},{224,1... | collective-permute-start | bytes 110600 | tf_op jit(solution)/shard_map/ppermute | solution.py:30
  33.0 2.2 %own_image.3.begun = f32[24,128]{1,0:T(8,128)S(1)} custom-call(f32[528,256]{1,0:T(8,128)S(1)} %own_spread.3.begun, f32[24,128]{1,0:T(8,128)S(1)} %collective-permute-done.6.apart, f32[24,128]{1,0:T(8,128)S(1)} %collective-permute-done.7.near, f32[32,2304]{1,0:T(8,128)S(1)} %get-tuple-element.48.plane_weights.w, ...), custom_call_target="tpu_custom_call" | custom-call | tf_op jit(solution)/shard_map/own_image/pallas_call | solution.py:625
  35.2 1.3 %below.3.begun = f32[24,128]{1,0:T(8,128)S(1)} custom-call(f32[24,128]{1,0:T(8,128)S(1)} %own_image.3.begun, f32[72,128]{1,0:T(8,128)S(1)} %collective-permute-done.8.three, f32[32,2304]{1,0:T(8,128)S(1)} %get-tuple-element.48.plane_weights.w, bf16[256,2304]{1,0:T(8,128)(2,1)S(1)} %get-tuple-element.49.z_high.h, ...), custom_call_target="tpu_custom_call" | custom-call | tf_op jit(solution)/shard_map/below/pallas_call | solution.py:625
  36.5 1.3 %above.3.own.vector.second = f32[24,128]{1,0:T(8,128)S(1)} custom-call(f32[24,128]{1,0:T(8,128)S(1)} %below.3.begun, f32[72,128]{1,0:T(8,128)S(1)} %collective-permute-done.9.three, f32[32,2304]{1,0:T(8,128)S(1)} %get-tuple-element.48.plane_weights.w, bf16[256,2304]{1,0:T(8,128)(2,1)S(1)} %get-tuple-element.49.z_high.h, ...), custom_call_target="tpu_custom_call" | custom-call | tf_op jit(solution)/shard_map/above/pallas_call | solution.py:625
  37.8 2.2 %collective-permute-start.10 = (f32[24,128]{1,0:T(8,128)S(1)}, f32[24,128]{1,0:T(8,128)S(1)}, u32[]{:S(2)}, u32[]{:S(2)}) collective-permute-start(f32[24,128]{1,0:T(8,128)S(1)} %above.3.own.vector.second), channel_id=1, source_target_pairs={{0,28},{4,8},{8,4},{12,16},{16,12},{20,24},{24,20},{28,0},{1,29},{... | collective-permute-start | bytes 36872 | tf_op jit(solution)/shard_map/ppermute | solution.py:35
  40.0 1.0 %collective-permute-start.11 = (f32[24,128]{1,0:T(8,128)S(1)}, f32[24,128]{1,0:T(8,128)S(1)}, u32[]{:S(2)}, u32[]{:S(2)}) collective-permute-start(f32[24,128]{1,0:T(8,128)S(1)} %above.3.own.vector.second), channel_id=1, source_target_pairs={{0,4},{4,0},{8,12},{12,8},{16,20},{20,16},{24,28},{28,24},{1,5},{5... | collective-permute-start | bytes 36872 | tf_op jit(solution)/shard_map/ppermute | solution.py:36
  41.0 0.6 own_spread.4.begun
  41.9 2.7 %collective-permute-start.13 = (f32[72,128]{1,0:T(8,128)S(1)}, f32[72,128]{1,0:T(8,128)S(1)}, u32[]{:S(2)}, u32[]{:S(2)}) collective-permute-start(f32[72,128]{1,0:T(8,128)S(1)} %pad_maximum_fusion.1), channel_id=1, source_target_pairs={{0,224},{32,0},{64,32},{96,64},{128,96},{160,128},{192,160},{224,1... | collective-permute-start | bytes 110600 | tf_op jit(solution)/shard_map/ppermute | solution.py:30
  44.5 2.0 %own_image.4.begun = f32[24,128]{1,0:T(8,128)S(1)} custom-call(f32[528,256]{1,0:T(8,128)S(1)} %own_spread.4.begun, f32[24,128]{1,0:T(8,128)S(1)} %collective-permute-done.10.apart, f32[24,128]{1,0:T(8,128)S(1)} %collective-permute-done.11.near, f32[32,2304]{1,0:T(8,128)S(1)} %get-tuple-element.48.plane_weights.w, ...), custom_call_target="tpu_custom_call" | custom-call | tf_op jit(solution)/shard_map/own_image/pallas_call | solution.py:625
  46.6 1.3 %below.4.begun = f32[24,128]{1,0:T(8,128)S(1)} custom-call(f32[24,128]{1,0:T(8,128)S(1)} %own_image.4.begun, f32[72,128]{1,0:T(8,128)S(1)} %collective-permute-done.12.three, f32[32,2304]{1,0:T(8,128)S(1)} %get-tuple-element.48.plane_weights.w, bf16[256,2304]{1,0:T(8,128)(2,1)S(1)} %get-tuple-element.49.z_high.h, ...), custom_call_target="tpu_custom_call" | custom-call | tf_op jit(solution)/shard_map/below/pallas_call | solution.py:625
  47.9 1.5 %above.4.own.third = f32[24,128]{1,0:T(8,128)S(1)} custom-call(f32[24,128]{1,0:T(8,128)S(1)} %below.4.begun, f32[72,128]{1,0:T(8,128)S(1)} %collective-permute-done.13.three, f32[32,2304]{1,0:T(8,128)S(1)} %get-tuple-element.48.plane_weights.w, bf16[256,2304]{1,0:T(8,128)(2,1)S(1)} %get-tuple-element.49.z_high.h, ...), custom_call_target="tpu_custom_call" | custom-call | tf_op jit(solution)/shard_map/above/pallas_call | solution.py:625
  49.4 2.0 %collective-permute-start.14 = (f32[24,128]{1,0:T(8,128)S(1)}, f32[24,128]{1,0:T(8,128)S(1)}, u32[]{:S(2)}, u32[]{:S(2)}) collective-permute-start(f32[24,128]{1,0:T(8,128)S(1)} %above.4.own.third), channel_id=1, source_target_pairs={{0,28},{4,8},{8,4},{12,16},{16,12},{20,24},{24,20},{28,0},{1,29},{... | collective-permute-start | bytes 36872 | tf_op jit(solution)/shard_map/ppermute | solution.py:35
  51.4 2.2 %collective-permute-start.15 = (f32[24,128]{1,0:T(8,128)S(1)}, f32[24,128]{1,0:T(8,128)S(1)}, u32[]{:S(2)}, u32[]{:S(2)}) collective-permute-start(f32[24,128]{1,0:T(8,128)S(1)} %above.4.own.third), channel_id=1, source_target_pairs={{0,4},{4,0},{8,12},{12,8},{16,20},{20,16},{24,28},{28,24},{1,5},{5... | collective-permute-start | bytes 36872 | tf_op jit(solution)/shard_map/ppermute | solution.py:36
  53.6 1.2 %own_spread.5 = (f32[528,256]{1,0:T(8,128)S(1)}, f32[8,128]{1,0:T(8,128)S(1)}) custom-call(f32[24,128]{1,0:T(8,128)S(1)} %above.4.own.third, f32[32,2304]{1,0:T(8,128)S(1)} %get-tuple-element.48.plane_weights.w, bf16[256,2304]{1,0:T(8,128)(2,1)S(1)} %get-tuple-element.49.z_high.h, bf16[256,2304]{1,0:T(8,128)(2,1)S(1)} %get-tuple-element.50.z_low.l, ...), custom_call_target="tpu_custom_call" | custom-call | tf_op jit(solution)/shard_map/own_spread/pallas_call | solution.py:625
  54.9 2.7 %collective-permute-start.17 = (f32[72,128]{1,0:T(8,128)S(1)}, f32[72,128]{1,0:T(8,128)S(1)}, u32[]{:S(2)}, u32[]{:S(2)}) collective-permute-start(f32[72,128]{1,0:T(8,128)S(1)} %pad_maximum_fusion.2), channel_id=1, source_target_pairs={{0,224},{32,0},{64,32},{96,64},{128,96},{160,128},{192,160},{224,1... | collective-permute-start | bytes 110600 | tf_op jit(solution)/shard_map/ppermute | solution.py:30
  57.6 2.0 %own_image.5.begun = f32[24,128]{1,0:T(8,128)S(1)} custom-call(f32[528,256]{1,0:T(8,128)S(1)} %get-tuple-element.64.begun, f32[24,128]{1,0:T(8,128)S(1)} %collective-permute-done.14.apart, f32[24,128]{1,0:T(8,128)S(1)} %collective-permute-done.15.near, f32[32,2304]{1,0:T(8,128)S(1)} %get-tuple-element.48.plane_weights.w, ...), custom_call_target="tpu_custom_call" | custom-call | tf_op jit(solution)/shard_map/own_image/pallas_call | solution.py:625
  59.6 1.3 %below.5.begun = f32[24,128]{1,0:T(8,128)S(1)} custom-call(f32[24,128]{1,0:T(8,128)S(1)} %own_image.5.begun, f32[72,128]{1,0:T(8,128)S(1)} %collective-permute-done.16.three, f32[32,2304]{1,0:T(8,128)S(1)} %get-tuple-element.48.plane_weights.w, bf16[256,2304]{1,0:T(8,128)(2,1)S(1)} %get-tuple-element.49.z_high.h, ...), custom_call_target="tpu_custom_call" | custom-call | tf_op jit(solution)/shard_map/below/pallas_call | solution.py:625
  60.9 1.9 %above.5 = f32[256,128]{1,0:T(8,128)S(1)} custom-call(f32[24,128]{1,0:T(8,128)S(1)} %below.5.begun, f32[72,128]{1,0:T(8,128)S(1)} %collective-permute-done.17.three, f32[32,2304]{1,0:T(8,128)S(1)} %get-tuple-element.48.plane_weights.w, bf16[256,2304]{1,0:T(8,128)(2,1)S(1)} %get-tuple-element.49.z_high.h, bf16[256,2304]{1,0:T(8,128)(2,1)S(1)} %get-tuple-element.50.z_low.l, ...), custom_call_target="tpu_custom_call" | custom-call | tf_op jit(solution)/shard_map/above/pallas_call | solution.py:625
  62.8 21.2 %all_to_all.11 = f32[256,1,128]{2,1,0:T(1,128)S(1)} all-to-all(f32[256,1,128]{2,1,0:T(1,128)S(1)} %bitcast.5), channel_id=1, replica_groups=mesh['gx'=8,'gy_0'=4,'gy_1'=2,'gz'=4] {'gx','gy_0','gy_1','gz'}, dimensions={0} | all-to-all | bytes 262144 | tf_op jit(solution)/shard_map/all_to_all | solution.py:706
  84.0 1.3 %finish.1 = f32[3,256]{1,0:T(4,128)} custom-call(f32[256,128]{1,0:T(8,128)S(1)} %bitcast.6, f32[24,128]{1,0:T(8,128)S(1)} %get-tuple-element.53.own.vector.first, f32[24,128]{1,0:T(8,128)S(1)} %above.3.own.vector.second, f32[24,128]{1,0:T(8,128)S(1)} %above.4.own.third), custom_call_target="tpu_custom_call" | custom-call | tf_op jit(solution)/shard_map/finish/pallas_call | solution.py:625
  (27 shorter events, 1.4 us)
Async XLA Ops:
  2.0 4.8 %collective-permute-start = (f32[80,128]{1,0:T(8,128)S(1)}, f32[80,128]{1,0:T(8,128)S(1)}, u32[]{:S(2)}, u32[]{:S(2)}) collective-permute-start(f32[80,128]{1,0:T(8,128)S(1)} %get-tuple-element.38), channel_id=1, source_target_pairs={{0,3},{1,2},{2,1},{3,0},{4,7},{5,6},{6,5},{7,4},{8,11},{9,10},{10,... | collective-permute-start | bytes 122888 | tf_op jit(solution)/shard_map/ppermute | solution.py:41
  5.4 2.9 %collective-permute-start.1 = (f32[80,128]{1,0:T(8,128)S(1)}, f32[80,128]{1,0:T(8,128)S(1)}, u32[]{:S(2)}, u32[]{:S(2)}) collective-permute-start(f32[80,128]{1,0:T(8,128)S(1)} %get-tuple-element.39), channel_id=1, source_target_pairs={{0,1},{1,0},{2,3},{3,2},{4,5},{5,4},{6,7},{7,6},{8,9},{9,8},{10,11... | collective-permute-start | bytes 122888 | tf_op jit(solution)/shard_map/ppermute | solution.py:42
  8.5 5.4 %collective-permute-start.2 = (f32[136,128]{1,0:T(8,128)S(1)}, f32[136,128]{1,0:T(8,128)S(1)}, u32[]{:S(2)}, u32[]{:S(2)}) collective-permute-start(f32[136,128]{1,0:T(8,128)S(1)} %get-tuple-element.42), channel_id=1, source_target_pairs={{0,28},{4,8},{8,4},{12,16},{16,12},{20,24},{24,20},{28,0},{1,29},{... | collective-permute-start | bytes 208904 | tf_op jit(solution)/shard_map/ppermute | solution.py:35
  11.9 2.0 %collective-permute-start.3 = (f32[136,128]{1,0:T(8,128)S(1)}, f32[136,128]{1,0:T(8,128)S(1)}, u32[]{:S(2)}, u32[]{:S(2)}) collective-permute-start(f32[136,128]{1,0:T(8,128)S(1)} %get-tuple-element.43), channel_id=1, source_target_pairs={{0,4},{4,0},{8,12},{12,8},{16,20},{20,16},{24,28},{28,24},{1,5},{5... | collective-permute-start | bytes 208904 | tf_op jit(solution)/shard_map/ppermute | solution.py:36
  14.0 10.5 %collective-permute-start.5 = (f32[280,128]{1,0:T(8,128)S(1)}, f32[280,128]{1,0:T(8,128)S(1)}, u32[]{:S(2)}, u32[]{:S(2)}) collective-permute-start(f32[280,128]{1,0:T(8,128)S(1)} %get-tuple-element.46), channel_id=1, source_target_pairs={{0,224},{32,0},{64,32},{96,64},{128,96},{160,128},{192,160},{224,1... | collective-permute-start | bytes 430088 | tf_op jit(solution)/shard_map/ppermute | solution.py:30
  19.6 4.8 %collective-permute-start.4 = (f32[216,128]{1,0:T(8,128)S(1)}, f32[216,128]{1,0:T(8,128)S(1)}, u32[]{:S(2)}, u32[]{:S(2)}) collective-permute-start(f32[216,128]{1,0:T(8,128)S(1)} %get-tuple-element.45), channel_id=1, source_target_pairs={{0,32},{32,64},{64,96},{96,128},{128,160},{160,192},{192,224},{224... | collective-permute-start | bytes 331784 | tf_op jit(solution)/shard_map/ppermute | solution.py:30
  25.1 5.2 %collective-permute-start.6 = (f32[24,128]{1,0:T(8,128)S(1)}, f32[24,128]{1,0:T(8,128)S(1)}, u32[]{:S(2)}, u32[]{:S(2)}) collective-permute-start(f32[24,128]{1,0:T(8,128)S(1)} %get-tuple-element.53.own.vector.first), channel_id=1, source_target_pairs={{0,28},{4,8},{8,4},{12,16},{16,12},{20,24},{24,20},{28,0},{1,29},{... | collective-permute-start | bytes 36872 | tf_op jit(solution)/shard_map/ppermute | solution.py:35
  28.4 1.9 %collective-permute-start.7 = (f32[24,128]{1,0:T(8,128)S(1)}, f32[24,128]{1,0:T(8,128)S(1)}, u32[]{:S(2)}, u32[]{:S(2)}) collective-permute-start(f32[24,128]{1,0:T(8,128)S(1)} %get-tuple-element.53.own.vector.first), channel_id=1, source_target_pairs={{0,4},{4,0},{8,12},{12,8},{16,20},{20,16},{24,28},{28,24},{1,5},{5... | collective-permute-start | bytes 36872 | tf_op jit(solution)/shard_map/ppermute | solution.py:36
  30.3 4.9 %collective-permute-start.8 = (f32[72,128]{1,0:T(8,128)S(1)}, f32[72,128]{1,0:T(8,128)S(1)}, u32[]{:S(2)}, u32[]{:S(2)}) collective-permute-start(f32[72,128]{1,0:T(8,128)S(1)} %pad_maximum_fusion), channel_id=1, source_target_pairs={{0,32},{32,64},{64,96},{96,128},{128,160},{160,192},{192,224},{224... | collective-permute-start | bytes 110600 | tf_op jit(solution)/shard_map/ppermute | solution.py:30
  30.4 6.2 %collective-permute-start.9 = (f32[72,128]{1,0:T(8,128)S(1)}, f32[72,128]{1,0:T(8,128)S(1)}, u32[]{:S(2)}, u32[]{:S(2)}) collective-permute-start(f32[72,128]{1,0:T(8,128)S(1)} %pad_maximum_fusion), channel_id=1, source_target_pairs={{0,224},{32,0},{64,32},{96,64},{128,96},{160,128},{192,160},{224,1... | collective-permute-start | bytes 110600 | tf_op jit(solution)/shard_map/ppermute | solution.py:30
  37.8 3.8 %collective-permute-start.10 = (f32[24,128]{1,0:T(8,128)S(1)}, f32[24,128]{1,0:T(8,128)S(1)}, u32[]{:S(2)}, u32[]{:S(2)}) collective-permute-start(f32[24,128]{1,0:T(8,128)S(1)} %above.3.own.vector.second), channel_id=1, source_target_pairs={{0,28},{4,8},{8,4},{12,16},{16,12},{20,24},{24,20},{28,0},{1,29},{... | collective-permute-start | bytes 36872 | tf_op jit(solution)/shard_map/ppermute | solution.py:35
  40.0 1.8 %collective-permute-start.11 = (f32[24,128]{1,0:T(8,128)S(1)}, f32[24,128]{1,0:T(8,128)S(1)}, u32[]{:S(2)}, u32[]{:S(2)}) collective-permute-start(f32[24,128]{1,0:T(8,128)S(1)} %above.3.own.vector.second), channel_id=1, source_target_pairs={{0,4},{4,0},{8,12},{12,8},{16,20},{20,16},{24,28},{28,24},{1,5},{5... | collective-permute-start | bytes 36872 | tf_op jit(solution)/shard_map/ppermute | solution.py:36
  41.9 4.7 %collective-permute-start.12 = (f32[72,128]{1,0:T(8,128)S(1)}, f32[72,128]{1,0:T(8,128)S(1)}, u32[]{:S(2)}, u32[]{:S(2)}) collective-permute-start(f32[72,128]{1,0:T(8,128)S(1)} %pad_maximum_fusion.1), channel_id=1, source_target_pairs={{0,32},{32,64},{64,96},{96,128},{128,160},{160,192},{192,224},{224... | collective-permute-start | bytes 110600 | tf_op jit(solution)/shard_map/ppermute | solution.py:30
  41.9 6.0 %collective-permute-start.13 = (f32[72,128]{1,0:T(8,128)S(1)}, f32[72,128]{1,0:T(8,128)S(1)}, u32[]{:S(2)}, u32[]{:S(2)}) collective-permute-start(f32[72,128]{1,0:T(8,128)S(1)} %pad_maximum_fusion.1), channel_id=1, source_target_pairs={{0,224},{32,0},{64,32},{96,64},{128,96},{160,128},{192,160},{224,1... | collective-permute-start | bytes 110600 | tf_op jit(solution)/shard_map/ppermute | solution.py:30
  49.4 5.5 %collective-permute-start.14 = (f32[24,128]{1,0:T(8,128)S(1)}, f32[24,128]{1,0:T(8,128)S(1)}, u32[]{:S(2)}, u32[]{:S(2)}) collective-permute-start(f32[24,128]{1,0:T(8,128)S(1)} %above.4.own.third), channel_id=1, source_target_pairs={{0,28},{4,8},{8,4},{12,16},{16,12},{20,24},{24,20},{28,0},{1,29},{... | collective-permute-start | bytes 36872 | tf_op jit(solution)/shard_map/ppermute | solution.py:35
  51.4 3.4 %collective-permute-start.15 = (f32[24,128]{1,0:T(8,128)S(1)}, f32[24,128]{1,0:T(8,128)S(1)}, u32[]{:S(2)}, u32[]{:S(2)}) collective-permute-start(f32[24,128]{1,0:T(8,128)S(1)} %above.4.own.third), channel_id=1, source_target_pairs={{0,4},{4,0},{8,12},{12,8},{16,20},{20,16},{24,28},{28,24},{1,5},{5... | collective-permute-start | bytes 36872 | tf_op jit(solution)/shard_map/ppermute | solution.py:36
  54.9 4.8 %collective-permute-start.16 = (f32[72,128]{1,0:T(8,128)S(1)}, f32[72,128]{1,0:T(8,128)S(1)}, u32[]{:S(2)}, u32[]{:S(2)}) collective-permute-start(f32[72,128]{1,0:T(8,128)S(1)} %pad_maximum_fusion.2), channel_id=1, source_target_pairs={{0,32},{32,64},{64,96},{96,128},{128,160},{160,192},{192,224},{224... | collective-permute-start | bytes 110600 | tf_op jit(solution)/shard_map/ppermute | solution.py:30
  54.9 6.0 %collective-permute-start.17 = (f32[72,128]{1,0:T(8,128)S(1)}, f32[72,128]{1,0:T(8,128)S(1)}, u32[]{:S(2)}, u32[]{:S(2)}) collective-permute-start(f32[72,128]{1,0:T(8,128)S(1)} %pad_maximum_fusion.2), channel_id=1, source_target_pairs={{0,224},{32,0},{64,32},{96,64},{128,96},{160,128},{192,160},{224,1... | collective-permute-start | bytes 110600 | tf_op jit(solution)/shard_map/ppermute | solution.py:30

commit v7 on v6

--- a/solution.py
+++ b/solution.py
@@ -1,3 +1,5 @@
+import functools
+
 import jax
 import jax.numpy as jnp
 from jax import lax
@@ -280,7 +282,7 @@
     fill_tables(above, 160, 8.0, count, a_weights, a_high, a_low)
 
 
-def interpolate(velocity_high, velocity_low, planes, plane_weights, z_high, z_low, used, image):
+def interpolate(velocity_high, velocity_low, planes, plane_weights, z_high, z_low, used, image, halo=True):
     def lines(place):
         partial = plain_dot(velocity_high[...], z_high[:, place]) + plain_dot(velocity_low[...], z_high[:, place])
         partial = partial + plain_dot(velocity_high[...], z_low[:, place])
@@ -298,6 +300,8 @@
     for c, line in enumerate(lines(slice(0, MARKERS))):
         image[2 * c : 2 * c + 1, :] = line[:, 0:128]
         image[2 * c + 1 : 2 * c + 2, :] = line[:, 128:256]
+    if not halo:
+        return
     for c, line in enumerate(lines(slice(FIRST, FIRST + 128))):
         image[8 + c : 9 + c, :] = line
 
@@ -454,34 +458,36 @@
 
 def own_image(
     begun, apart, near, plane_weights, z_high, z_low, used, scale, result, left_high, left_low, moved, velocity_high,
-    velocity_low,
+    velocity_low, halo=True,
 ):
     refs = [(apart, 0), (near, 0)]
     planes = range(1, 12)
     count = trips(used)
     spread_group(refs, planes, plane_weights, z_high, z_low, count, left_high, left_low, moved, begun, 1)
     respond(moved, planes, planes, scale, velocity_high, velocity_low)
-    interpolate(velocity_high, velocity_low, planes, plane_weights, z_high, z_low, count, result)
+    interpolate(velocity_high, velocity_low, planes, plane_weights, z_high, z_low, count, result, halo)
 
 
 def side_image(
     below, begun, three, own_tables, own_used, side_tables, used, scale, left_high, left_low, moved, velocity_high,
-    velocity_low, image,
+    velocity_low, image, halo=True,
 ):
     planes, outs = (range(0, 4), range(1, 5)) if below else (range(9, 13), range(8, 12))
     refs = [(three, 24 * part) for part in range(3)]
     spread_group(refs, planes, *side_tables, trips(used), left_high, left_low, moved)
     respond(moved, planes, outs, scale, velocity_high, velocity_low)
-    interpolate(velocity_high, velocity_low, outs, *own_tables, trips(own_used), image)
+    interpolate(velocity_high, velocity_low, outs, *own_tables, trips(own_used), image, halo)
     return begun[...] + image[...]
 
 
-def below_kernel(begun, three, w, h, l, own_used, sw, sh, sl, used, scale, result, *scratch):
-    result[...] = side_image(True, begun, three, (w, h, l), own_used, (sw, sh, sl), used, scale, *scratch)
-
-
-def above_image(begun, three, w, h, l, own_used, sw, sh, sl, used, scale, aux, vector, *scratch):
-    image = side_image(False, begun, three, (w, h, l), own_used, (sw, sh, sl), used, scale, *scratch)
+def below_kernel(begun, three, w, h, l, own_used, sw, sh, sl, used, scale, result, *scratch, halo=True):
+    result[...] = side_image(
+        True, begun, three, (w, h, l), own_used, (sw, sh, sl), used, scale, *scratch, halo=halo
+    )
+
+
+def above_image(begun, three, w, h, l, own_used, sw, sh, sl, used, scale, aux, vector, *scratch, halo=True):
+    image = side_image(False, begun, three, (w, h, l), own_used, (sw, sh, sl), used, scale, *scratch, halo=halo)
     return aux[0:24, :] * (image + aux[24:48, :] * vector[...])
 
 
@@ -561,7 +567,7 @@
 def last_kernel(
     begun, three, w, h, l, own_used, sw, sh, sl, used, scale, aux, third, first, second, early, sums, *scratch
 ):
-    fourth = above_image(begun, three, w, h, l, own_used, sw, sh, sl, used, scale, aux, third, *scratch)
+    fourth = above_image(begun, three, w, h, l, own_used, sw, sh, sl, used, scale, aux, third, *scratch, halo=False)
     vectors = [first[0:8, :], second[0:8, :], third[0:8, :], fourth[0:8]]
     packed = gram_lanes(vectors, LATE, early[...])
     for block in range(sums.shape[0] // 8):
@@ -684,13 +690,13 @@
         three = lax.optimization_barrier((jnp.concatenate([vector, apart, near], axis=0), *held))[0]
         below_three, above_three = shifted(three, "gx", 1), shifted(three, "gx", -1)
         (own_part,) = call(
-            own_image, "own_image", [rows(24)], begun[0], apart, near, *own_tables, scale,
+            functools.partial(own_image, halo=not last), "own_image", [rows(24)], begun[0], apart, near, *own_tables, scale,
             scratch=[vmem((3 * INNER, 768), BF16)] * 2 + [vmem((3 * INNER, LANES), F32)] + velocity_scratch,
         )
         side_scratch = [vmem((192, STATIC), BF16)] * 2 + [vmem((192, LANES), F32)]
         side_scratch += [vmem((192, LANES), BF16)] * 2 + [image_scratch]
         (part,) = call(
-            below_kernel, "below", [rows(24)], own_part, below_three, *own_tables, *side_tables[0:3], side_tables[6], scale,
+            functools.partial(below_kernel, halo=not last), "below", [rows(24)], own_part, below_three, *own_tables, *side_tables[0:3], side_tables[6], scale,
             scratch=side_scratch,
         )
         (result,) = call(

time: 85.4 us -> 85.1 us (level)
  transfers between devices with their start and end apart: 18 -> 18, of which waited for: 5 -> 5; matrix products, arithmetic and copies ran while one was open for 0% -> 0% of each run, Pallas kernels for 17% -> 16%
where the time goes in v7:
time: 85.1 us; the launch traced here: 84.9 us
  starting transfers between devices  31.4 us (37%)
  Pallas kernels  22.1 us (26%)
  blocking collectives  21.4 us (25%)
  waiting for transfers between devices  9.26 us (11%)
  between operations  0.88 us (1%)
    pallas_call x19, Pallas kernels, call(): pl.pallas_call(kernel, name=name, out_shape=[jax.ShapeDtypeStruct(shape,...  22.1 us
    all_to_all x1, blocking collectives, body(): gathered = lax.all_to_all(sums, GX_GY_GZ, 0, 0, tiled=True)  21.4 us
    ppermute x8, starting transfers between devices, shifted(): lax.ppermute(shard, axis, [(i, (i + by) % length) for i in range(length)])  13.8 us
    ppermute x4, starting transfers between devices, swapped_y(): lax.ppermute(to_apart, GY, [(i, (i + 1 if i % 2 else i - 1) % length) for...  10.9 us
    ppermute x8, waiting for transfers between devices, shifted(): lax.ppermute(shard, axis, [(i, (i + by) % length) for i in range(length)])  4.22 us
    ppermute x1, starting transfers between devices, swapped_z(): lax.ppermute(to_odd, 'gz', [(i, (i + 1 if i % 2 else i - 1) % length) for...  3.38 us
    ppermute x4, starting transfers between devices, swapped_y(): lax.ppermute(to_near, GY, [(i, i ^ 1) for i in range(length)])  3.24 us
    ppermute x4, waiting for transfers between devices, swapped_y(): lax.ppermute(to_apart, GY, [(i, (i + 1 if i % 2 else i - 1) % length) for...  2 us
  transfers between devices with their start and end apart: 18, of which 5 were waited for; matrix products, arithmetic and copies ran while one was open for 0% of the time, Pallas kernels for 16%

profile of v7, /device:TPU:1, one launch (start us, length us, event | category | flops | bytes accessed | tf_op | source)
XLA Modules:
  0.0 84.9 jit_solution(10576426438590351551)
XLA Ops:
  0.7 1.4 %pack.1 = (f32[256,128]{1,0:T(8,128)S(1)}, f32[24,128]{1,0:T(8,128)S(1)}, f32[80,128]{1,0:T(8,128)S(1)}, f32[80,128]{1,0:T(8,128)S(1)}) custom-call(f32[8,8,128]{2,1,0:T(8,128)} %density_in.1, f32[3,8,8,128]{3,2,1,0:T(8,128)} %base_in.1, s32[3,256]{1,0:T(4,128)} %cells_in.1, f32[3,256]{1,0:T(4,128)} %offsets_in.1, f32[3,256]{1,0:T(4,128)} %target_in.1, ...), custom_call_target="tpu_custom_call" | custom-call | tf_op jit(solution)/shard_map/pack/pallas_call | solution.py:631
  2.0 3.4 %collective-permute-start = (f32[80,128]{1,0:T(8,128)S(1)}, f32[80,128]{1,0:T(8,128)S(1)}, u32[]{:S(2)}, u32[]{:S(2)}) collective-permute-start(f32[80,128]{1,0:T(8,128)S(1)} %get-tuple-element.38), channel_id=1, source_target_pairs={{0,3},{1,2},{2,1},{3,0},{4,7},{5,6},{6,5},{7,4},{8,11},{9,10},{10,... | collective-permute-start | bytes 122888 | tf_op jit(solution)/shard_map/ppermute | solution.py:43
  5.4 1.4 %collective-permute-done.odd = f32[80,128]{1,0:T(8,128)S(1)} collective-permute-done((f32[80,128]{1,0:T(8,128)S(1)}, f32[80,128]{1,0:T(8,128)S(1)}, u32[]{:S(2)}, u32[]{:S(2)}) %collective-permute-start) | collective-permute-done | bytes 40992 | tf_op jit(solution)/shard_map/ppermute | solution.py:43
  6.8 1.5 %collective-permute-done.1.even = f32[80,128]{1,0:T(8,128)S(1)} collective-permute-done((f32[80,128]{1,0:T(8,128)S(1)}, f32[80,128]{1,0:T(8,128)S(1)}, u32[]{:S(2)}, u32[]{:S(2)}) %collective-permute-start.1) | collective-permute-done | bytes 40992 | tf_op jit(solution)/shard_map/ppermute | solution.py:44
  8.5 3.4 %collective-permute-start.2 = (f32[136,128]{1,0:T(8,128)S(1)}, f32[136,128]{1,0:T(8,128)S(1)}, u32[]{:S(2)}, u32[]{:S(2)}) collective-permute-start(f32[136,128]{1,0:T(8,128)S(1)} %get-tuple-element.42), channel_id=1, source_target_pairs={{0,28},{4,8},{8,4},{12,16},{16,12},{20,24},{24,20},{28,0},{1,29},{... | collective-permute-start | bytes 208904 | tf_op jit(solution)/shard_map/ppermute | solution.py:37
  11.9 2.0 %collective-permute-done.2.apart = f32[136,128]{1,0:T(8,128)S(1)} collective-permute-done((f32[136,128]{1,0:T(8,128)S(1)}, f32[136,128]{1,0:T(8,128)S(1)}, u32[]{:S(2)}, u32[]{:S(2)}) %collective-permute-start.2) | collective-permute-done | bytes 69664 | tf_op jit(solution)/shard_map/ppermute | solution.py:37
  14.0 5.6 %collective-permute-start.5 = (f32[280,128]{1,0:T(8,128)S(1)}, f32[280,128]{1,0:T(8,128)S(1)}, u32[]{:S(2)}, u32[]{:S(2)}) collective-permute-start(f32[280,128]{1,0:T(8,128)S(1)} %get-tuple-element.46), channel_id=1, source_target_pairs={{0,224},{32,0},{64,32},{96,64},{128,96},{160,128},{192,160},{224,1... | collective-permute-start | bytes 430088 | tf_op jit(solution)/shard_map/ppermute | solution.py:32
  20.2 4.2 %collective-permute-done.4.below = f32[216,128]{1,0:T(8,128)S(1)} collective-permute-done((f32[216,128]{1,0:T(8,128)S(1)}, f32[216,128]{1,0:T(8,128)S(1)}, u32[]{:S(2)}, u32[]{:S(2)}) %collective-permute-start.4) | collective-permute-done | bytes 110624 | tf_op jit(solution)/shard_map/ppermute | solution.py:32
  24.5 0.6 setup.1
  25.1 3.3 %collective-permute-start.6 = (f32[24,128]{1,0:T(8,128)S(1)}, f32[24,128]{1,0:T(8,128)S(1)}, u32[]{:S(2)}, u32[]{:S(2)}) collective-permute-start(f32[24,128]{1,0:T(8,128)S(1)} %get-tuple-element.53.own.vector.first), channel_id=1, source_target_pairs={{0,28},{4,8},{8,4},{12,16},{16,12},{20,24},{24,20},{28,0},{1,29},{... | collective-permute-start | bytes 36872 | tf_op jit(solution)/shard_map/ppermute | solution.py:37
  28.5 0.6 own_spread.3.begun
  29.1 1.1 %side_tables.1 = (f32[32,2304]{1,0:T(8,128)S(1)}, bf16[256,2304]{1,0:T(8,128)(2,1)S(1)}, bf16[256,2304]{1,0:T(8,128)(2,1)S(1)}, f32[32,2304]{1,0:T(8,128)S(1)}, ...) custom-call(f32[216,128]{1,0:T(8,128)S(1)} %collective-permute-done.4.below, ...), custom_call_target="tpu_custom_call" | custom-call | tf_op jit(solution)/shard_map/side_tables/pallas_call | solution.py:631
  30.4 2.7 %collective-permute-start.9 = (f32[72,128]{1,0:T(8,128)S(1)}, f32[72,128]{1,0:T(8,128)S(1)}, u32[]{:S(2)}, u32[]{:S(2)}) collective-permute-start(f32[72,128]{1,0:T(8,128)S(1)} %pad_maximum_fusion), channel_id=1, source_target_pairs={{0,224},{32,0},{64,32},{96,64},{128,96},{160,128},{192,160},{224,1... | collective-permute-start | bytes 110600 | tf_op jit(solution)/shard_map/ppermute | solution.py:32
  33.0 2.2 %own_image.3.begun = f32[24,128]{1,0:T(8,128)S(1)} custom-call(f32[528,256]{1,0:T(8,128)S(1)} %own_spread.3.begun, f32[24,128]{1,0:T(8,128)S(1)} %collective-permute-done.6.apart, f32[24,128]{1,0:T(8,128)S(1)} %collective-permute-done.7.near, f32[32,2304]{1,0:T(8,128)S(1)} %get-tuple-element.48.plane_weights.w, ...), custom_call_target="tpu_custom_call" | custom-call | tf_op jit(solution)/shard_map/own_image/pallas_call | solution.py:631
  35.2 1.3 %below.3.begun = f32[24,128]{1,0:T(8,128)S(1)} custom-call(f32[24,128]{1,0:T(8,128)S(1)} %own_image.3.begun, f32[72,128]{1,0:T(8,128)S(1)} %collective-permute-done.8.three, f32[32,2304]{1,0:T(8,128)S(1)} %get-tuple-element.48.plane_weights.w, bf16[256,2304]{1,0:T(8,128)(2,1)S(1)} %get-tuple-element.49.z_high.h, ...), custom_call_target="tpu_custom_call" | custom-call | tf_op jit(solution)/shard_map/below/pallas_call | solution.py:631
  36.5 1.3 %above.3.own.vector.second = f32[24,128]{1,0:T(8,128)S(1)} custom-call(f32[24,128]{1,0:T(8,128)S(1)} %below.3.begun, f32[72,128]{1,0:T(8,128)S(1)} %collective-permute-done.9.three, f32[32,2304]{1,0:T(8,128)S(1)} %get-tuple-element.48.plane_weights.w, bf16[256,2304]{1,0:T(8,128)(2,1)S(1)} %get-tuple-element.49.z_high.h, ...), custom_call_target="tpu_custom_call" | custom-call | tf_op jit(solution)/shard_map/above/pallas_call | solution.py:631
  37.8 2.2 %collective-permute-start.10 = (f32[24,128]{1,0:T(8,128)S(1)}, f32[24,128]{1,0:T(8,128)S(1)}, u32[]{:S(2)}, u32[]{:S(2)}) collective-permute-start(f32[24,128]{1,0:T(8,128)S(1)} %above.3.own.vector.second), channel_id=1, source_target_pairs={{0,28},{4,8},{8,4},{12,16},{16,12},{20,24},{24,20},{28,0},{1,29},{... | collective-permute-start | bytes 36872 | tf_op jit(solution)/shard_map/ppermute | solution.py:37
  40.0 1.0 %collective-permute-start.11 = (f32[24,128]{1,0:T(8,128)S(1)}, f32[24,128]{1,0:T(8,128)S(1)}, u32[]{:S(2)}, u32[]{:S(2)}) collective-permute-start(f32[24,128]{1,0:T(8,128)S(1)} %above.3.own.vector.second), channel_id=1, source_target_pairs={{0,4},{4,0},{8,12},{12,8},{16,20},{20,16},{24,28},{28,24},{1,5},{5... | collective-permute-start | bytes 36872 | tf_op jit(solution)/shard_map/ppermute | solution.py:38
  41.0 0.6 own_spread.4.begun
  41.9 2.7 %collective-permute-start.13 = (f32[72,128]{1,0:T(8,128)S(1)}, f32[72,128]{1,0:T(8,128)S(1)}, u32[]{:S(2)}, u32[]{:S(2)}) collective-permute-start(f32[72,128]{1,0:T(8,128)S(1)} %pad_maximum_fusion.1), channel_id=1, source_target_pairs={{0,224},{32,0},{64,32},{96,64},{128,96},{160,128},{192,160},{224,1... | collective-permute-start | bytes 110600 | tf_op jit(solution)/shard_map/ppermute | solution.py:32
  44.5 2.0 %own_image.4.begun = f32[24,128]{1,0:T(8,128)S(1)} custom-call(f32[528,256]{1,0:T(8,128)S(1)} %own_spread.4.begun, f32[24,128]{1,0:T(8,128)S(1)} %collective-permute-done.10.apart, f32[24,128]{1,0:T(8,128)S(1)} %collective-permute-done.11.near, f32[32,2304]{1,0:T(8,128)S(1)} %get-tuple-element.48.plane_weights.w, ...), custom_call_target="tpu_custom_call" | custom-call | tf_op jit(solution)/shard_map/own_image/pallas_call | solution.py:631
  46.6 1.3 %below.4.begun = f32[24,128]{1,0:T(8,128)S(1)} custom-call(f32[24,128]{1,0:T(8,128)S(1)} %own_image.4.begun, f32[72,128]{1,0:T(8,128)S(1)} %collective-permute-done.12.three, f32[32,2304]{1,0:T(8,128)S(1)} %get-tuple-element.48.plane_weights.w, bf16[256,2304]{1,0:T(8,128)(2,1)S(1)} %get-tuple-element.49.z_high.h, ...), custom_call_target="tpu_custom_call" | custom-call | tf_op jit(solution)/shard_map/below/pallas_call | solution.py:631
  47.9 1.5 %above.4.own.third = f32[24,128]{1,0:T(8,128)S(1)} custom-call(f32[24,128]{1,0:T(8,128)S(1)} %below.4.begun, f32[72,128]{1,0:T(8,128)S(1)} %collective-permute-done.13.three, f32[32,2304]{1,0:T(8,128)S(1)} %get-tuple-element.48.plane_weights.w, bf16[256,2304]{1,0:T(8,128)(2,1)S(1)} %get-tuple-element.49.z_high.h, ...), custom_call_target="tpu_custom_call" | custom-call | tf_op jit(solution)/shard_map/above/pallas_call | solution.py:631
  49.4 2.0 %collective-permute-start.14 = (f32[24,128]{1,0:T(8,128)S(1)}, f32[24,128]{1,0:T(8,128)S(1)}, u32[]{:S(2)}, u32[]{:S(2)}) collective-permute-start(f32[24,128]{1,0:T(8,128)S(1)} %above.4.own.third), channel_id=1, source_target_pairs={{0,28},{4,8},{8,4},{12,16},{16,12},{20,24},{24,20},{28,0},{1,29},{... | collective-permute-start | bytes 36872 | tf_op jit(solution)/shard_map/ppermute | solution.py:37
  51.4 2.2 %collective-permute-start.15 = (f32[24,128]{1,0:T(8,128)S(1)}, f32[24,128]{1,0:T(8,128)S(1)}, u32[]{:S(2)}, u32[]{:S(2)}) collective-permute-start(f32[24,128]{1,0:T(8,128)S(1)} %above.4.own.third), channel_id=1, source_target_pairs={{0,4},{4,0},{8,12},{12,8},{16,20},{20,16},{24,28},{28,24},{1,5},{5... | collective-permute-start | bytes 36872 | tf_op jit(solution)/shard_map/ppermute | solution.py:38
  53.6 1.2 %own_spread.5 = (f32[528,256]{1,0:T(8,128)S(1)}, f32[8,128]{1,0:T(8,128)S(1)}) custom-call(f32[24,128]{1,0:T(8,128)S(1)} %above.4.own.third, f32[32,2304]{1,0:T(8,128)S(1)} %get-tuple-element.48.plane_weights.w, bf16[256,2304]{1,0:T(8,128)(2,1)S(1)} %get-tuple-element.49.z_high.h, bf16[256,2304]{1,0:T(8,128)(2,1)S(1)} %get-tuple-element.50.z_low.l, ...), custom_call_target="tpu_custom_call" | custom-call | tf_op jit(solution)/shard_map/own_spread/pallas_call | solution.py:631
  54.9 2.7 %collective-permute-start.17 = (f32[72,128]{1,0:T(8,128)S(1)}, f32[72,128]{1,0:T(8,128)S(1)}, u32[]{:S(2)}, u32[]{:S(2)}) collective-permute-start(f32[72,128]{1,0:T(8,128)S(1)} %pad_maximum_fusion.2), channel_id=1, source_target_pairs={{0,224},{32,0},{64,32},{96,64},{128,96},{160,128},{192,160},{224,1... | collective-permute-start | bytes 110600 | tf_op jit(solution)/shard_map/ppermute | solution.py:32
  57.6 1.7 %own_image.5.begun = f32[24,128]{1,0:T(8,128)S(1)} custom-call(f32[528,256]{1,0:T(8,128)S(1)} %get-tuple-element.64.begun, f32[24,128]{1,0:T(8,128)S(1)} %collective-permute-done.14.apart, f32[24,128]{1,0:T(8,128)S(1)} %collective-permute-done.15.near, f32[32,2304]{1,0:T(8,128)S(1)} %get-tuple-element.48.plane_weights.w, ...), custom_call_target="tpu_custom_call" | custom-call | tf_op jit(solution)/shard_map/own_image/pallas_call | solution.py:631
  59.4 1.2 %below.5.begun = f32[24,128]{1,0:T(8,128)S(1)} custom-call(f32[24,128]{1,0:T(8,128)S(1)} %own_image.5.begun, f32[72,128]{1,0:T(8,128)S(1)} %collective-permute-done.16.three, f32[32,2304]{1,0:T(8,128)S(1)} %get-tuple-element.48.plane_weights.w, bf16[256,2304]{1,0:T(8,128)(2,1)S(1)} %get-tuple-element.49.z_high.h, ...), custom_call_target="tpu_custom_call" | custom-call | tf_op jit(solution)/shard_map/below/pallas_call | solution.py:631
  60.6 1.7 %above.5 = f32[256,128]{1,0:T(8,128)S(1)} custom-call(f32[24,128]{1,0:T(8,128)S(1)} %below.5.begun, f32[72,128]{1,0:T(8,128)S(1)} %collective-permute-done.17.three, f32[32,2304]{1,0:T(8,128)S(1)} %get-tuple-element.48.plane_weights.w, bf16[256,2304]{1,0:T(8,128)(2,1)S(1)} %get-tuple-element.49.z_high.h, bf16[256,2304]{1,0:T(8,128)(2,1)S(1)} %get-tuple-element.50.z_low.l, ...), custom_call_target="tpu_custom_call" | custom-call | tf_op jit(solution)/shard_map/above/pallas_call | solution.py:631
  62.3 21.4 %all_to_all.11 = f32[256,1,128]{2,1,0:T(1,128)S(1)} all-to-all(f32[256,1,128]{2,1,0:T(1,128)S(1)} %bitcast.5), channel_id=1, replica_groups=mesh['gx'=8,'gy_0'=4,'gy_1'=2,'gz'=4] {'gx','gy_0','gy_1','gz'}, dimensions={0} | all-to-all | bytes 262144 | tf_op jit(solution)/shard_map/all_to_all | solution.py:712
  83.7 1.3 %finish.1 = f32[3,256]{1,0:T(4,128)} custom-call(f32[256,128]{1,0:T(8,128)S(1)} %bitcast.6, f32[24,128]{1,0:T(8,128)S(1)} %get-tuple-element.53.own.vector.first, f32[24,128]{1,0:T(8,128)S(1)} %above.3.own.vector.second, f32[24,128]{1,0:T(8,128)S(1)} %above.4.own.third), custom_call_target="tpu_custom_call" | custom-call | tf_op jit(solution)/shard_map/finish/pallas_call | solution.py:631
  (27 shorter events, 1.4 us)
Async XLA Ops:
  2.0 4.8 %collective-permute-start = (f32[80,128]{1,0:T(8,128)S(1)}, f32[80,128]{1,0:T(8,128)S(1)}, u32[]{:S(2)}, u32[]{:S(2)}) collective-permute-start(f32[80,128]{1,0:T(8,128)S(1)} %get-tuple-element.38), channel_id=1, source_target_pairs={{0,3},{1,2},{2,1},{3,0},{4,7},{5,6},{6,5},{7,4},{8,11},{9,10},{10,... | collective-permute-start | bytes 122888 | tf_op jit(solution)/shard_map/ppermute | solution.py:43
  5.4 2.9 %collective-permute-start.1 = (f32[80,128]{1,0:T(8,128)S(1)}, f32[80,128]{1,0:T(8,128)S(1)}, u32[]{:S(2)}, u32[]{:S(2)}) collective-permute-start(f32[80,128]{1,0:T(8,128)S(1)} %get-tuple-element.39), channel_id=1, source_target_pairs={{0,1},{1,0},{2,3},{3,2},{4,5},{5,4},{6,7},{7,6},{8,9},{9,8},{10,11... | collective-permute-start | bytes 122888 | tf_op jit(solution)/shard_map/ppermute | solution.py:44
  8.5 5.4 %collective-permute-start.2 = (f32[136,128]{1,0:T(8,128)S(1)}, f32[136,128]{1,0:T(8,128)S(1)}, u32[]{:S(2)}, u32[]{:S(2)}) collective-permute-start(f32[136,128]{1,0:T(8,128)S(1)} %get-tuple-element.42), channel_id=1, source_target_pairs={{0,28},{4,8},{8,4},{12,16},{16,12},{20,24},{24,20},{28,0},{1,29},{... | collective-permute-start | bytes 208904 | tf_op jit(solution)/shard_map/ppermute | solution.py:37
  11.9 2.0 %collective-permute-start.3 = (f32[136,128]{1,0:T(8,128)S(1)}, f32[136,128]{1,0:T(8,128)S(1)}, u32[]{:S(2)}, u32[]{:S(2)}) collective-permute-start(f32[136,128]{1,0:T(8,128)S(1)} %get-tuple-element.43), channel_id=1, source_target_pairs={{0,4},{4,0},{8,12},{12,8},{16,20},{20,16},{24,28},{28,24},{1,5},{5... | collective-permute-start | bytes 208904 | tf_op jit(solution)/shard_map/ppermute | solution.py:38
  14.0 10.5 %collective-permute-start.5 = (f32[280,128]{1,0:T(8,128)S(1)}, f32[280,128]{1,0:T(8,128)S(1)}, u32[]{:S(2)}, u32[]{:S(2)}) collective-permute-start(f32[280,128]{1,0:T(8,128)S(1)} %get-tuple-element.46), channel_id=1, source_target_pairs={{0,224},{32,0},{64,32},{96,64},{128,96},{160,128},{192,160},{224,1... | collective-permute-start | bytes 430088 | tf_op jit(solution)/shard_map/ppermute | solution.py:32
  19.6 4.8 %collective-permute-start.4 = (f32[216,128]{1,0:T(8,128)S(1)}, f32[216,128]{1,0:T(8,128)S(1)}, u32[]{:S(2)}, u32[]{:S(2)}) collective-permute-start(f32[216,128]{1,0:T(8,128)S(1)} %get-tuple-element.45), channel_id=1, source_target_pairs={{0,32},{32,64},{64,96},{96,128},{128,160},{160,192},{192,224},{224... | collective-permute-start | bytes 331784 | tf_op jit(solution)/shard_map/ppermute | solution.py:32
  25.1 5.2 %collective-permute-start.6 = (f32[24,128]{1,0:T(8,128)S(1)}, f32[24,128]{1,0:T(8,128)S(1)}, u32[]{:S(2)}, u32[]{:S(2)}) collective-permute-start(f32[24,128]{1,0:T(8,128)S(1)} %get-tuple-element.53.own.vector.first), channel_id=1, source_target_pairs={{0,28},{4,8},{8,4},{12,16},{16,12},{20,24},{24,20},{28,0},{1,29},{... | collective-permute-start | bytes 36872 | tf_op jit(solution)/shard_map/ppermute | solution.py:37
  28.4 1.9 %collective-permute-start.7 = (f32[24,128]{1,0:T(8,128)S(1)}, f32[24,128]{1,0:T(8,128)S(1)}, u32[]{:S(2)}, u32[]{:S(2)}) collective-permute-start(f32[24,128]{1,0:T(8,128)S(1)} %get-tuple-element.53.own.vector.first), channel_id=1, source_target_pairs={{0,4},{4,0},{8,12},{12,8},{16,20},{20,16},{24,28},{28,24},{1,5},{5... | collective-permute-start | bytes 36872 | tf_op jit(solution)/shard_map/ppermute | solution.py:38
  30.3 4.9 %collective-permute-start.8 = (f32[72,128]{1,0:T(8,128)S(1)}, f32[72,128]{1,0:T(8,128)S(1)}, u32[]{:S(2)}, u32[]{:S(2)}) collective-permute-start(f32[72,128]{1,0:T(8,128)S(1)} %pad_maximum_fusion), channel_id=1, source_target_pairs={{0,32},{32,64},{64,96},{96,128},{128,160},{160,192},{192,224},{224... | collective-permute-start | bytes 110600 | tf_op jit(solution)/shard_map/ppermute | solution.py:32
  30.4 6.2 %collective-permute-start.9 = (f32[72,128]{1,0:T(8,128)S(1)}, f32[72,128]{1,0:T(8,128)S(1)}, u32[]{:S(2)}, u32[]{:S(2)}) collective-permute-start(f32[72,128]{1,0:T(8,128)S(1)} %pad_maximum_fusion), channel_id=1, source_target_pairs={{0,224},{32,0},{64,32},{96,64},{128,96},{160,128},{192,160},{224,1... | collective-permute-start | bytes 110600 | tf_op jit(solution)/shard_map/ppermute | solution.py:32
  37.8 3.8 %collective-permute-start.10 = (f32[24,128]{1,0:T(8,128)S(1)}, f32[24,128]{1,0:T(8,128)S(1)}, u32[]{:S(2)}, u32[]{:S(2)}) collective-permute-start(f32[24,128]{1,0:T(8,128)S(1)} %above.3.own.vector.second), channel_id=1, source_target_pairs={{0,28},{4,8},{8,4},{12,16},{16,12},{20,24},{24,20},{28,0},{1,29},{... | collective-permute-start | bytes 36872 | tf_op jit(solution)/shard_map/ppermute | solution.py:37
  40.0 1.8 %collective-permute-start.11 = (f32[24,128]{1,0:T(8,128)S(1)}, f32[24,128]{1,0:T(8,128)S(1)}, u32[]{:S(2)}, u32[]{:S(2)}) collective-permute-start(f32[24,128]{1,0:T(8,128)S(1)} %above.3.own.vector.second), channel_id=1, source_target_pairs={{0,4},{4,0},{8,12},{12,8},{16,20},{20,16},{24,28},{28,24},{1,5},{5... | collective-permute-start | bytes 36872 | tf_op jit(solution)/shard_map/ppermute | solution.py:38
  41.9 4.7 %collective-permute-start.12 = (f32[72,128]{1,0:T(8,128)S(1)}, f32[72,128]{1,0:T(8,128)S(1)}, u32[]{:S(2)}, u32[]{:S(2)}) collective-permute-start(f32[72,128]{1,0:T(8,128)S(1)} %pad_maximum_fusion.1), channel_id=1, source_target_pairs={{0,32},{32,64},{64,96},{96,128},{128,160},{160,192},{192,224},{224... | collective-permute-start | bytes 110600 | tf_op jit(solution)/shard_map/ppermute | solution.py:32
  41.9 6.0 %collective-permute-start.13 = (f32[72,128]{1,0:T(8,128)S(1)}, f32[72,128]{1,0:T(8,128)S(1)}, u32[]{:S(2)}, u32[]{:S(2)}) collective-permute-start(f32[72,128]{1,0:T(8,128)S(1)} %pad_maximum_fusion.1), channel_id=1, source_target_pairs={{0,224},{32,0},{64,32},{96,64},{128,96},{160,128},{192,160},{224,1... | collective-permute-start | bytes 110600 | tf_op jit(solution)/shard_map/ppermute | solution.py:32
  49.4 5.5 %collective-permute-start.14 = (f32[24,128]{1,0:T(8,128)S(1)}, f32[24,128]{1,0:T(8,128)S(1)}, u32[]{:S(2)}, u32[]{:S(2)}) collective-permute-start(f32[24,128]{1,0:T(8,128)S(1)} %above.4.own.third), channel_id=1, source_target_pairs={{0,28},{4,8},{8,4},{12,16},{16,12},{20,24},{24,20},{28,0},{1,29},{... | collective-permute-start | bytes 36872 | tf_op jit(solution)/shard_map/ppermute | solution.py:37
  51.4 3.4 %collective-permute-start.15 = (f32[24,128]{1,0:T(8,128)S(1)}, f32[24,128]{1,0:T(8,128)S(1)}, u32[]{:S(2)}, u32[]{:S(2)}) collective-permute-start(f32[24,128]{1,0:T(8,128)S(1)} %above.4.own.third), channel_id=1, source_target_pairs={{0,4},{4,0},{8,12},{12,8},{16,20},{20,16},{24,28},{28,24},{1,5},{5... | collective-permute-start | bytes 36872 | tf_op jit(solution)/shard_map/ppermute | solution.py:38
  54.9 4.5 %collective-permute-start.16 = (f32[72,128]{1,0:T(8,128)S(1)}, f32[72,128]{1,0:T(8,128)S(1)}, u32[]{:S(2)}, u32[]{:S(2)}) collective-permute-start(f32[72,128]{1,0:T(8,128)S(1)} %pad_maximum_fusion.2), channel_id=1, source_target_pairs={{0,32},{32,64},{64,96},{96,128},{128,160},{160,192},{192,224},{224... | collective-permute-start | bytes 110600 | tf_op jit(solution)/shard_map/ppermute | solution.py:32
  54.9 5.6 %collective-permute-start.17 = (f32[72,128]{1,0:T(8,128)S(1)}, f32[72,128]{1,0:T(8,128)S(1)}, u32[]{:S(2)}, u32[]{:S(2)}) collective-permute-start(f32[72,128]{1,0:T(8,128)S(1)} %pad_maximum_fusion.2), channel_id=1, source_target_pairs={{0,224},{32,0},{64,32},{96,64},{128,96},{160,128},{192,160},{224,1... | collective-permute-start | bytes 110600 | tf_op jit(solution)/shard_map/ppermute | solution.py:32
